TPU v7x, 512 devices: a whole 4x4x16 slice. The times are simulated.
512 devices in a mesh: prow: 16 (over z_hi, y, core), pcol: 32 (over z_lo, x).
Axes of the slice: x: 4, y: 4, z: 16 (z_hi: 2, z_lo: 8; z = z_hi * 8 + z_lo), core: 2. Of those that a mesh axis runs over, the one named last changes fastest.
Arguments:
- inverse_tiles: float32 [32, 16384, 512], P('prow', 'pcol'), may hold values from -0.36 to 0.36
- tile_rows: int32 [32, 32], P('prow', 'pcol'), may hold values from -1 to 1, as said below
- panel: float32 [16384, 1024], P(('prow', 'pcol')), may hold values from -0.6 to 0.6
- pivot_base: float32 [1024, 512], P('pcol'), may hold values from -6 to 6
Outputs:
- panel_inverse: float32 [16384, 1024], P(('prow', 'pcol'))
- pivot_inverse: float32 [1024, 512], P('pcol')
Inputs may be any that keep to these rules, and one draw needn't show every extreme that they name: `tile_rows`: on each device the entries name distinct row tiles first and -1 after; the device at prow 0 and pcol 0 lists 2.
All inputs are finite; a program needn't handle non-finite values.
Results may differ from a plain program's by a relative error of at most 0.0003.
Values sent between devices are 32-bit elements; how exact they have to be, the bound alone decides.
No kernel may reach another device: no remote copies, remote signals or barrier semaphores. Data moves between devices by JAX's collectives and lax.ppermute only.
A program may use at most 64 MiB of HBM per device.

v0:
```python
import jax
import jax.numpy as jnp
from jax import lax
from jax.sharding import Mesh
from jax.sharding import PartitionSpec as P

PCOL = ("pcol_0", "pcol_1")
PROW_PCOL = ("prow", "pcol_0", "pcol_1")


def reduced_to_own(parts, axes, turns):
    inside = parts.shape[1:]
    parts = parts.reshape(*(lax.axis_size(a) for a in axes), *inside)
    parts = jnp.moveaxis(parts, turns, range(len(axes))).reshape(-1, *inside)
    for k in turns:
        parts = lax.psum_scatter(parts, axes[k], scatter_dimension=0, tiled=True)
    return parts[0]


def cut_along(shard, dim, size):
    shape = shard.shape
    parts = shard.reshape(*shape[:dim], size, shape[dim] // size, *shape[dim + 1 :])
    return jnp.moveaxis(parts, dim, 0)


def scatter_axes(shard, axes, turns, dim):
    size = lax.axis_size(axes)
    return reduced_to_own(cut_along(shard, dim, size), axes, turns)


def gathered_total(shard, axis):
    parts = lax.all_gather(shard, axis)
    return parts.sum(axis=0)


def local(inverse_tiles, tile_rows, panel, pivot_base):
    block = inverse_tiles.shape[1]
    width = panel.shape[1]
    share = panel.shape[0]
    row_tiles = share * lax.axis_size(PCOL) // block
    column = lax.all_gather(panel, "prow", axis=0, tiled=True)
    codes = tile_rows[:, 0]
    count = jnp.sum((codes >= 0).astype(jnp.int32))
    totals = jnp.zeros((row_tiles, block, width - 0), jnp.float32)

    def add_tile(slot, totals):
        tile = lax.dynamic_index_in_dim(inverse_tiles, slot, 0, keepdims=False)
        tile_row = lax.dynamic_index_in_dim(codes, slot, 0, keepdims=False)
        product = jnp.dot(
            tile, column, precision=lax.Precision.HIGHEST, preferred_element_type=jnp.float32
        )
        current = lax.dynamic_index_in_dim(totals, tile_row, 0, keepdims=False)
        return lax.dynamic_update_index_in_dim(totals, current + product, tile_row, 0)

    totals = lax.fori_loop(0, count, add_tile, totals)
    trailing = scatter_axes(totals.reshape(row_tiles * block, width - 0), PCOL, (1, 0), 0)
    panel_inverse = -trailing
    upper = panel.reshape(share, width // block, block)
    lower = trailing.reshape(share, width // block, block)
    partial_update = jnp.einsum("rka,rkb->kab", upper, lower, precision=lax.Precision.HIGHEST)
    flat = partial_update.reshape(1, width, block)
    received = lax.all_to_all(flat, PCOL, split_axis=1, concat_axis=0, tiled=True)
    column_part = jnp.sum(received, axis=0)
    mine = gathered_total(column_part, "prow")
    return (panel_inverse, pivot_base + mine)


def solution(mesh):
    finer = Mesh(mesh.devices.reshape(mesh.shape["prow"], 8, 4), ("prow", "pcol_0", "pcol_1"))
    placed = (P("prow", PCOL, None), P("prow", PCOL), P(PROW_PCOL, None), P(PCOL, None))
    return jax.shard_map(
        local,
        mesh=finer,
        in_specs=placed,
        out_specs=(P(PROW_PCOL, None), P(PCOL, None)),
        check_vma=False,
    )
```

profile of v0, /device:TPU:1, one launch (start us, length us, event | category | flops | bytes accessed | tf_op | source)
XLA Modules:
  0.0 446.6 jit_solution(9347757076955287820)
XLA Ops:
  7.2 0.0 all-gather.4.cloned.1.call-start
  7.2 0.7 all-gather.4.cloned.1.call-update
  7.9 0.0 reduce-scatter.3.cloned.1.call-start
  7.9 1.3 fusion.7
  9.2 99.8 %all-gather.4.cloned.1.call-done = f32[512,1024]{1,0:T(8,128)} async-done(((f32[32,1024]{1,0:T(8,128)}), f32[512,1024]{1,0:T(8,128)}) %all-gather.4.cloned.1.call-update) | async-done | bytes 2097168 | tf_op jit(solution)/shard_map/all_gather | solution.py:41
  109.1 2.5 broadcast_in_dim.7
  111.5 0.0 copy-done.2
  111.5 0.0 copy-done.6
  111.5 0.7 while.10
  112.2 4.8 %copy.13 = f32[8,4,32,1024]{3,2,0,1:T(8,128)} copy(f32[8,4,32,1024]{3,2,1,0:T(8,128)} %bitcast.38) | data formatting | bytes 8388608 | tf_op jit(solution)/shard_map/reshape;reshape;reshape | solution.py:13
  116.9 0.0 reduce-scatter.3.cloned.1.call-update
  117.0 0.0 reduce-scatter.5.cloned.1.call-start
  117.0 70.4 %reduce-scatter.3.cloned.1.call-done = f32[8,32,1024]{2,1,0:T(8,128)} async-done(((f32[32,32,1024]{2,1,0:T(8,128)}), f32[8,32,1024]{2,1,0:T(8,128)}) %reduce-scatter.3.cloned.1.call-update) | async-done | bytes 1048592 | tf_op jit(solution)/shard_map/reduce_scatter | solution.py:16
  187.4 0.0 reduce-scatter.5.cloned.1.call-update
  187.4 0.0 all-gather.6.cloned.1.call-start
  187.5 65.0 %reduce-scatter.5.cloned.1.call-done = f32[1,32,1024]{2,1,0:T(8,128)} async-done(((f32[8,32,1024]{2,1,0:T(8,128)}), f32[1,32,1024]{2,1,0:T(8,128)}) %reduce-scatter.5.cloned.1.call-update) | async-done | bytes 131088 | tf_op jit(solution)/shard_map/reduce_scatter | solution.py:16
  252.5 1.0 reshape_squeeze.3
  253.5 0.0 copy-done.3
  253.5 1.8 fusion.3
  255.4 2.2 copy.16
  257.5 101.8 %all_to_all.12 = f32[1,1024,512]{2,0,1:T(1,128)S(1)} all-to-all(f32[1,1024,512]{2,0,1:T(1,128)S(1)} %copy.16), channel_id=1, replica_groups=mesh['prow'=16,'pcol_0'=8,'pcol_1'=4] {'pcol_0','pcol_1'}, dimensions={1} | all-to-all | bytes 4194304 | tf_op jit(solution)/shard_map/all_to_all | solution.py:62
  359.3 0.2 copy.17
  359.5 0.0 copy-start.4
  359.5 0.0 copy-start.5
  359.5 0.8 reduce_sum.28
  360.3 0.0 all-gather.6.cloned.1.call-update
  360.3 0.1 copy-done.4
  360.4 0.7 negate_bitcast_fusion
  361.0 77.1 %all-gather.6.cloned.1.call-done = f32[512,512]{1,0:T(8,128)} async-done(((f32[32,512]{1,0:T(8,128)}), f32[512,512]{1,0:T(8,128)}) %all-gather.6.cloned.1.call-update) | async-done | bytes 1048592 | tf_op jit(solution)/shard_map/all_gather | solution.py:32
  438.1 1.3 reduce_sum.29
  439.4 0.0 copy-done.5
  439.4 0.6 add.25
  (3 shorter events, 0.0 us)
Async XLA Ops:
  7.2 101.9 %all-gather.4.cloned.1.call-start = ((), (), s32[]{:S(2)}) async-start(), calls=%async_computation.3 | async-start | bytes 2228224 | tf_op jit(solution)/shard_map/all_gather | solution.py:41
  7.9 179.5 %reduce-scatter.3.cloned.1.call-start = ((), (), s32[]{:S(2)}) async-start(), calls=%async_computation.4 | async-start | bytes 5242880 | tf_op jit(solution)/shard_map/reduce_scatter | solution.py:16
  109.0 2.5 copy-start.2
  109.0 2.5 copy-start.6
  116.9 136.6 %copy-start.3 = (f32[32,1024]{1,0:T(8,128)S(1)}, f32[32,1024]{1,0:T(8,128)}, u32[]{:S(2)}) copy-start(f32[32,1024]{1,0:T(8,128)} %param.8) | copy-start | bytes 393220
  117.0 135.5 %reduce-scatter.5.cloned.1.call-start = ((), (), s32[]{:S(2)}) async-start(), calls=%async_computation.5 | async-start | bytes 1179648 | tf_op jit(solution)/shard_map/reduce_scatter | solution.py:16
  187.4 250.6 %all-gather.6.cloned.1.call-start = ((), (), s32[]{:S(2)}) async-start(), calls=%async_computation.6 | async-start | bytes 1114112 | tf_op jit(solution)/shard_map/all_gather | solution.py:32
  359.5 0.9 copy-start.4
  359.5 79.9 %copy-start.5 = (f32[32,512]{1,0:T(8,128)S(1)}, f32[32,512]{1,0:T(8,128)}, u32[]{:S(2)}) copy-start(f32[32,512]{1,0:T(8,128)} %param.9) | copy-start | bytes 196612
Sparse Core Ops, SparseCore 0:
  11.3 97.7 all-gather.3
  117.1 70.2 reduce-scatter.2
  190.2 62.2 reduce-scatter.4
  360.4 77.6 all-gather.5
where the time goes:
time: 447 us
  waiting for transfers between devices  313 us (70%)
  blocking collectives  102 us (23%)
  between operations  13.8 us (3%)
  local copies, waits for them, and re-layouts  10.7 us (2%)
  other arithmetic  4.67 us (1%)
    reduce_scatter x2, waiting for transfers between devices, reduced_to_own(): parts = lax.psum_scatter(parts, axes[k], scatter_dimension=0, tiled=True)  135 us
    all_to_all x1, blocking collectives, local(): lax.all_to_all(flat, PCOL, split_axis=1, concat_axis=0, tiled=True)  102 us
    all_gather x1, waiting for transfers between devices, local(): column = lax.all_gather(panel, 'prow', axis=0, tiled=True)  99.8 us
    all_gather x1, waiting for transfers between devices, gathered_total(): parts = lax.all_gather(shard, axis)  77.1 us
  transfers between devices with their start and end apart: 4, of which 4 were waited for; matrix products, arithmetic and copies ran while one was open for 0% of the time, Pallas kernels for 0%

commit v1 on v0

v1 whole, which is shorter than its diff:
```python
import jax
import jax.numpy as jnp
from jax import lax
from jax.sharding import Mesh
from jax.sharding import PartitionSpec as P

HIGH = lax.Precision.HIGH
PROW = ("zh", "y", "c")
PCOL = ("zl", "x")


def shift(x, axis, by):
    n = lax.axis_size(axis)
    return lax.ppermute(x, axis, [(i, (i + by) % n) for i in range(n)])


def swap(x, axis, bit):
    n = lax.axis_size(axis)
    return lax.ppermute(x, axis, [(i, i ^ bit) for i in range(n)])


def ordered(mine, other, bit, axis):
    low = bit == 0
    return jnp.stack([jnp.where(low, mine, other), jnp.where(low, other, mine)], axis)


def pick(x, index, axis):
    return lax.dynamic_index_in_dim(x, index, axis, keepdims=False)


def dot(a, b, dims=(((1,), (0,)), ((), ()))):
    return lax.dot_general(a, b, dims, precision=HIGH, preferred_element_type=jnp.float32)


def gathered_column(panel):
    c = lax.axis_index("c")
    zh = lax.axis_index("zh")
    far = swap(panel, "zh", 1)
    halves = []
    for rows in (panel, far):
        mine = lax.all_gather(rows, "y", axis=0)
        halves.append(ordered(mine, swap(mine, "c", 1), c, 1))
    return ordered(halves[0], halves[1], zh, 0)


def gathered_over_zl(rows):
    zl = lax.axis_index("zl")
    rows = rows[None]
    for bit in (4, 2, 1):
        other = swap(rows, "zl", bit)
        rows = ordered(rows, other, zl & bit, 1 if bit != 4 else 0)
        rows = rows.reshape(-1, *rows.shape[2:])
    return rows


def products(inverse_tiles, codes, column):
    x = lax.axis_index("x")
    slots, block = inverse_tiles.shape[:2]
    tiles = inverse_tiles.reshape(slots, 4, 4, block // 16, block)
    column = column.reshape(block, -1)
    out = {}
    for d in (2, 1, 3, 0):
        part = pick(tiles, (x + d) % 4, 2)
        for i in range(2):
            left = jnp.where(codes[0] == i, part[0], jnp.where(codes[1] == i, part[1], 0.0))
            out[d, i] = dot(left.reshape(block // 4, block), column)
    return out


def reduced_over_x(t):
    up_a = shift(t[2, 0], "x", 1)
    down_a = shift(t[2, 1], "x", -1)
    up_b = shift(t[1, 1], "x", 1)
    down_b = shift(t[3, 0], "x", -1)
    up_c = shift(t[1, 0] + up_a, "x", 1)
    down_c = shift(t[3, 1] + down_a, "x", -1)
    return jnp.stack([t[0, 0] + down_b + up_c, t[0, 1] + up_b + down_c])


def reduced_over_zl(t):
    zl = lax.axis_index("zl")
    for bit, axis in ((1, 2), (2, 1), (4, 0)):
        mine = (zl // bit) % 2
        t = pick(t, mine, axis) + swap(pick(t, 1 - mine, axis), "zl", bit)
    return t


def local(inverse_tiles, tile_rows, panel, pivot_base):
    share, width = panel.shape
    block = inverse_tiles.shape[1]
    half = block // 2
    c = lax.axis_index("c")
    codes = tile_rows[:, 0]
    column = gathered_column(panel)
    upper = gathered_over_zl(panel)
    t = reduced_over_x(products(inverse_tiles, codes, column))
    trailing = reduced_over_zl(t.reshape(2, 2, 2, share, width))

    u = upper.reshape(8 * share, 2, block)
    v = t.reshape(8 * share, 2, 2, half)
    pair = (((0,), (0,)), ((1,), (1,)))
    away = dot(u, pick(v, 1 - c, 2), pair)
    home = dot(u, pick(v, c, 2), pair)
    w = home + swap(away, "c", 1)
    w = w.reshape(8, 4, 4, 8, half).transpose(2, 1, 0, 3, 4)
    w = w.reshape(16, 8, 8, half)
    w = lax.all_to_all(w, ("y", "x"), 0, 0, tiled=True).sum(axis=0)
    w = lax.all_to_all(w, "zl", 0, 0, tiled=True).sum(axis=0)
    w = lax.all_gather(w, PROW, axis=0).reshape(2, 4, 2, 8, half).sum(axis=0)
    w = w.transpose(0, 2, 1, 3).reshape(share, block)
    return (-trailing, pivot_base + w)


def solution(mesh):
    finer = Mesh(mesh.devices.reshape(2, 4, 2, 8, 4), PROW + PCOL)
    placed = (P(PROW, PCOL, None), P(PROW, PCOL), P(PROW + PCOL, None), P(PCOL, None))
    return jax.shard_map(
        local,
        mesh=finer,
        in_specs=placed,
        out_specs=(P(PROW + PCOL, None), P(PCOL, None)),
        check_vma=False,
    )
```

time: 447 us -> 229 us (0.51)
  waiting for transfers between devices: 313 us -> 46.3 us
  starting transfers between devices: 0.16 us -> 78.8 us
  blocking collectives: 102 us -> 66.4 us
  matrix products: 1.83 us -> 15 us
  between operations: 13.8 us -> 4 us
    all_gather x2 -> x0, waiting for transfers between devices: 177 us -> none  [the longest x1 99.8 us: local(): column = lax.all_gather(panel, 'prow', axis=0, tiled=True)]
    reduce_scatter x2 -> x0, waiting for transfers between devices: 135 us -> none  [reduced_to_own(): parts = lax.psum_scatter(parts, axes[k], scatter_dimension=0, tiled=True)]
    all_to_all x1 -> x0, blocking collectives: 102 us -> none  [local(): lax.all_to_all(flat, PCOL, split_axis=1, concat_axis=0, tiled=True)]
    ppermute x0 -> x16, starting transfers between devices: none -> 70.8 us  [the longest x10 51.9 us: swap(): return lax.ppermute(x, axis, [(i, i ^ bit) for i in range(n)])]
    all_gather x0 -> x3, blocking collectives: none -> 66.4 us  [the longest x1 43.1 us: local(): w = lax.all_gather(w, PROW, axis=0).reshape(2, 4, 2, 8, half).sum(axis=0)]
    ppermute x0 -> x16, waiting for transfers between devices: none -> 44.5 us  [the longest x10 25.5 us: swap(): return lax.ppermute(x, axis, [(i, i ^ bit) for i in range(n)])]
    dot_general x1 -> x10, matrix products: 1.83 us -> 15 us  [dot(): lax.dot_general(a, b, dims, precision=HIGH, preferred_element_type=jnp.fl...]
    all_to_all x0 -> x2, starting transfers between devices: none -> 7.95 us  [the longest x1 4.6 us: local(): w = lax.all_to_all(w, ('y', 'x'), 0, 0, tiled=True).sum(axis=0)]
  transfers between devices with their start and end apart: 4 -> 18, of which waited for: 4 -> 6; matrix products, arithmetic and copies ran while one was open for 0% -> 11% of each run, Pallas kernels for 0% -> 0%
where the time goes in v1:
time: 229 us; the launch traced here: 228 us
  starting transfers between devices  78.8 us (34%)
  blocking collectives  66.4 us (29%)
  waiting for transfers between devices  46.3 us (20%)
  matrix products  15 us (7%)
  local copies, waits for them, and re-layouts  9.95 us (4%)
  other arithmetic  7.92 us (3%)
  between operations  4 us (2%)
    ppermute x10, starting transfers between devices, swap(): return lax.ppermute(x, axis, [(i, i ^ bit) for i in range(n)])  51.9 us
    all_gather x1, blocking collectives, local(): w = lax.all_gather(w, PROW, axis=0).reshape(2, 4, 2, 8, half).sum(axis=0)  43.1 us
    ppermute x10, waiting for transfers between devices, swap(): return lax.ppermute(x, axis, [(i, i ^ bit) for i in range(n)])  25.5 us
    all_gather x2, blocking collectives, gathered_column(): mine = lax.all_gather(rows, 'y', axis=0)  23.4 us
    ppermute x6, starting transfers between devices, shift(): return lax.ppermute(x, axis, [(i, (i + by) % n) for i in range(n)])  19 us
    ppermute x6, waiting for transfers between devices, shift(): return lax.ppermute(x, axis, [(i, (i + by) % n) for i in range(n)])  19 us
    dot_general x10, matrix products, dot(): lax.dot_general(a, b, dims, precision=HIGH, preferred_element_type=jnp.fl...  15 us
    all_to_all x1, starting transfers between devices, local(): w = lax.all_to_all(w, ('y', 'x'), 0, 0, tiled=True).sum(axis=0)  4.6 us
  transfers between devices with their start and end apart: 18, of which 6 were waited for; matrix products, arithmetic and copies ran while one was open for 11% of the time, Pallas kernels for 0%

profile of v1, /device:TPU:1, one launch (start us, length us, event | category | flops | bytes accessed | tf_op | source)
XLA Modules:
  0.0 228.3 jit_solution(7984989947372093958)
XLA Ops:
  0.6 16.3 %collective-permute-start.1 = (f32[32,1024]{1,0:T(8,128)}, f32[32,1024]{1,0:T(8,128)S(1)}, u32[]{:S(2)}, u32[]{:S(2)}) collective-permute-start(f32[32,1024]{1,0:T(8,128)} %param.6), channel_id=1, source_target_pairs={{0,256},{256,0},{1,257},{257,1},{2,258},{258,2},{3,259},{259,3},{4... | collective-permute-start | bytes 393224 | tf_op jit(solution)/shard_map/ppermute | solution.py:19
  16.9 4.0 %collective-permute-start.12 = (f32[1,32,1024]{2,1,0:T(8,128)}, f32[1,32,1024]{2,1,0:T(8,128)S(1)}, u32[]{:S(2)}, u32[]{:S(2)}) collective-permute-start(f32[1,32,1024]{2,1,0:T(8,128)} %bitcast.141), channel_id=1, source_target_pairs={{0,16},{4,20},{8,24},{12,28},{16,0},{20,4},{24,8},{28,12},{1,17},{... | collective-permute-start | bytes 393224 | tf_op jit(solution)/shard_map/ppermute | solution.py:19
  20.9 11.9 %all-gather = f32[128,1024]{1,0:T(8,128)S(1)} all-gather(f32[32,1024]{1,0:T(8,128)} %param.6), channel_id=2, replica_groups=mesh['zh'=2,'y'=4,'c'=2,'zl'=8,'x'=4] {'y'}, dimensions={0}, use_global_device_ids=true | all-gather | bytes 655360 | tf_op jit(solution)/shard_map/all_gather | solution.py:41
  32.8 4.8 %collective-permute-start = (f32[4,32,1024]{2,1,0:T(8,128)S(1)}, f32[4,32,1024]{2,1,0:T(8,128)S(1)}, u32[]{:S(2)}, u32[]{:S(2)}) collective-permute-start(f32[4,32,1024]{2,1,0:T(8,128)S(1)} %bitcast.127), channel_id=1, source_target_pairs={{0,32},{32,0},{1,33},{33,1},{2,34},{34,2},{3,35},{35,3},{4,36},{36... | collective-permute-start | bytes 1572872 | tf_op jit(solution)/shard_map/ppermute | solution.py:19
  42.5 3.1 %collective-permute-start.13 = (f32[2,32,1024]{2,1,0:T(8,128)S(1)}, f32[2,32,1024]{2,1,0:T(8,128)S(1)}, u32[]{:S(2)}, u32[]{:S(2)}) collective-permute-start(f32[2,32,1024]{2,1,0:T(8,128)S(1)} %maximum_bitcast_fusion), channel_id=1, source_target_pairs={{0,8},{4,12},{8,0},{12,4},{16,24},{20,28},{24,16},{28,20},{1,9},{5... | collective-permute-start | bytes 786440 | tf_op jit(solution)/shard_map/ppermute | solution.py:19
  45.6 2.9 %select_select_fusion.3 = (f32[1,4,1,32,512]{4,3,2,1,0:T(8,128)}, f32[1,4,1,32,512]{4,3,2,1,0:T(8,128)}, f32[1,4,1,32,512]{4,3,2,1,0:T(8,128)S(1)}, f32[1,4,1,32...) fusion(f32[2,4,4,32,512]{4,3,2,1,0:T(8,128)} %bitcast.131, ...), kind=kLoop, calls=%fused_computation.43 | loop fusion | flops 1048576 | bytes 4194328 | tf_op jit(solution)/shard_map/jit(_where)/select_n | solution.py:65
  48.5 11.5 %all-gather.1 = f32[128,1024]{1,0:T(8,128)S(1)} all-gather(f32[32,1024]{1,0:T(8,128)S(1)} %collective-permute-done.1), channel_id=3, replica_groups=mesh['zh'=2,'y'=4,'c'=2,'zl'=8,'x'=4] {'y'}, dimensions={0}, use_global_device_ids=true | all-gather | bytes 655360 | tf_op jit(solution)/shard_map/all_gather | solution.py:41
  60.0 3.7 %collective-permute-start.2 = (f32[4,32,1024]{2,1,0:T(8,128)S(1)}, f32[4,32,1024]{2,1,0:T(8,128)S(1)}, u32[]{:S(2)}, u32[]{:S(2)}) collective-permute-start(f32[4,32,1024]{2,1,0:T(8,128)S(1)} %bitcast.129), channel_id=1, source_target_pairs={{0,32},{32,0},{1,33},{33,1},{2,34},{34,2},{3,35},{35,3},{4,36},{36... | collective-permute-start | bytes 1572872 | tf_op jit(solution)/shard_map/ppermute | solution.py:19
  63.9 2.5 %collective-permute-start.14 = (f32[4,32,1024]{2,1,0:T(8,128)S(1)}, f32[4,32,1024]{2,1,0:T(8,128)S(1)}, u32[]{:S(2)}, u32[]{:S(2)}) collective-permute-start(f32[4,32,1024]{2,1,0:T(8,128)S(1)} %bitcast.132), channel_id=1, source_target_pairs={{0,4},{4,0},{8,12},{12,8},{16,20},{20,16},{24,28},{28,24},{1,5},{5... | collective-permute-start | bytes 1572872 | tf_op jit(solution)/shard_map/ppermute | solution.py:19
  68.7 4.5 %collective-permute-start.7 = (f32[128,1024]{1,0:T(8,128)S(1)}, f32[128,1024]{1,0:T(8,128)S(1)}, u32[]{:S(2)}, u32[]{:S(2)}) collective-permute-start(f32[128,1024]{1,0:T(8,128)S(1)} %fusion.19), channel_id=1, source_target_pairs={{0,3},{1,0},{2,1},{3,2},{4,7},{5,4},{6,5},{7,6},{8,11},{9,8},{10,9... | collective-permute-start | bytes 1572872 | tf_op jit(solution)/shard_map/ppermute | solution.py:14
  74.8 2.0 collective-permute-start.6
  77.6 2.2 collective-permute-start.4
  81.3 4.4 %collective-permute-start.3 = (f32[128,1024]{1,0:T(8,128)}, f32[128,1024]{1,0:T(8,128)}, u32[]{:S(2)}, u32[]{:S(2)}) collective-permute-start(f32[128,1024]{1,0:T(8,128)} %fusion.16), channel_id=1, source_target_pairs={{0,3},{1,0},{2,1},{3,2},{4,7},{5,4},{6,5},{7,6},{8,11},{9,8},{10,9... | collective-permute-start | bytes 1572872 | tf_op jit(solution)/shard_map/ppermute | solution.py:14
  87.3 3.7 %collective-permute-start.8 = (f32[128,1024]{1,0:T(8,128)}, f32[128,1024]{1,0:T(8,128)}, u32[]{:S(2)}, u32[]{:S(2)}) collective-permute-start(f32[128,1024]{1,0:T(8,128)} %convolution_add_fusion.1), channel_id=1, source_target_pairs={{0,3},{1,0},{2,1},{3,2},{4,7},{5,4},{6,5},{7,6},{8,11},{9,8},{10,9... | collective-permute-start | bytes 1572872 | tf_op jit(solution)/shard_map/ppermute | solution.py:14
  91.0 11.3 %collective-permute-done.4 = f32[128,1024]{1,0:T(8,128)S(1)} collective-permute-done((f32[128,1024]{1,0:T(8,128)S(1)}, f32[128,1024]{1,0:T(8,128)S(1)}, u32[]{:S(2)}, u32[]{:S(2)}) %collective-permute-start.4) | collective-permute-done | bytes 524320 | tf_op jit(solution)/shard_map/ppermute | solution.py:14
  103.9 2.1 collective-permute-start.5
  106.3 1.9 reshape_reshape.3
  109.7 2.0 fusion
  111.7 7.7 %collective-permute-done.5 = f32[128,1024]{1,0:T(8,128)} collective-permute-done((f32[128,1024]{1,0:T(8,128)}, f32[128,1024]{1,0:T(8,128)}, u32[]{:S(2)}, u32[]{:S(2)}) %collective-permute-start.5) | collective-permute-done | bytes 524320 | tf_op jit(solution)/shard_map/ppermute | solution.py:14
  119.3 1.9 fusion.1
  126.4 4.2 %collective-permute-start.15 = (f32[2,512,256]{2,1,0:T(8,128)}, f32[2,512,256]{2,1,0:T(8,128)}, u32[]{:S(2)}, u32[]{:S(2)}) collective-permute-start(f32[2,512,256]{2,1,0:T(8,128)} %fusion.9), channel_id=1, source_target_pairs={{0,32},{32,0},{1,33},{33,1},{2,34},{34,2},{3,35},{35,3},{4,36},{36... | collective-permute-start | bytes 3145736 | tf_op jit(solution)/shard_map/ppermute | solution.py:19
  131.5 2.7 %collective-permute-start.9 = (f32[2,2,32,1024]{3,2,1,0:T(8,128)}, f32[2,2,32,1024]{3,2,1,0:T(8,128)S(1)}, u32[]{:S(2)}, u32[]{:S(2)}) collective-permute-start(f32[2,2,32,1024]{3,2,1,0:T(8,128)} %fusion.5), channel_id=1, source_target_pairs={{0,4},{4,0},{8,12},{12,8},{16,20},{20,16},{24,28},{28,24},{1,5},{5... | collective-permute-start | bytes 1572872 | tf_op jit(solution)/shard_map/ppermute | solution.py:19
  134.3 1.8 convolution_add_fusion
  137.2 4.6 %all-to-all-start = ((f32[16,8,8,256]{3,2,1,0:T(8,128)}), f32[16,8,8,256]{3,2,1,0:T(8,128)S(1)}, u32[]{:S(2)}, u32[]{:S(2)}) async-start(f32[16,8,8,256]{3,2,1,0:T(8,128)} %bitcast.48), calls=%async_computation | async-start | bytes 2097152 | tf_op jit(solution)/shard_map/all_to_all | solution.py:107
  141.8 5.2 %collective-permute-done.9 = f32[2,2,32,1024]{3,2,1,0:T(8,128)S(1)} collective-permute-done((f32[2,2,32,1024]{3,2,1,0:T(8,128)}, f32[2,2,32,1024]{3,2,1,0:T(8,128)S(1)}, u32[]{:S(2)}, u32[]{:S(2)}) %collective-permute-start.9) | collective-permute-done | bytes 524320 | tf_op jit(solution)/shard_map/ppermute | solution.py:19
  147.1 3.0 %collective-permute-start.10 = (f32[2,32,1024]{2,1,0:T(8,128)S(1)}, f32[2,32,1024]{2,1,0:T(8,128)S(1)}, u32[]{:S(2)}, u32[]{:S(2)}) collective-permute-start(f32[2,32,1024]{2,1,0:T(8,128)S(1)} %dynamic-slice_bitcast_fusion), channel_id=1, source_target_pairs={{0,8},{4,12},{8,0},{12,4},{16,24},{20,28},{24,16},{28,20},{1,9},{5... | collective-permute-start | bytes 786440 | tf_op jit(solution)/shard_map/ppermute | solution.py:19
  150.2 13.0 %collective-permute-done.10 = f32[2,32,1024]{2,1,0:T(8,128)S(1)} collective-permute-done((f32[2,32,1024]{2,1,0:T(8,128)S(1)}, f32[2,32,1024]{2,1,0:T(8,128)S(1)}, u32[]{:S(2)}, u32[]{:S(2)}) %collective-permute-start.10) | collective-permute-done | bytes 262176 | tf_op jit(solution)/shard_map/ppermute | solution.py:19
  163.3 7.5 %collective-permute-start.11 = (f32[32,1024]{1,0:T(8,128)S(1)}, f32[32,1024]{1,0:T(8,128)S(1)}, u32[]{:S(2)}, u32[]{:S(2)}) collective-permute-start(f32[32,1024]{1,0:T(8,128)S(1)} %dynamic-slice_bitcast_fusion.1), channel_id=1, source_target_pairs={{0,16},{4,20},{8,24},{12,28},{16,0},{20,4},{24,8},{28,12},{1,17},{... | collective-permute-start | bytes 393224 | tf_op jit(solution)/shard_map/ppermute | solution.py:19
  171.5 3.4 %all-to-all-start.1 = ((f32[8,8,256]{2,1,0:T(8,128)}), f32[8,8,256]{2,1,0:T(8,128)S(1)}, u32[]{:S(2)}, u32[]{:S(2)}) async-start(f32[8,8,256]{2,1,0:T(8,128)} %reduce_sum.27), calls=%async_computation.1 | async-start | bytes 131072 | tf_op jit(solution)/shard_map/all_to_all | solution.py:108
  174.9 7.3 %collective-permute-done.11 = f32[32,1024]{1,0:T(8,128)S(1)} collective-permute-done((f32[32,1024]{1,0:T(8,128)S(1)}, f32[32,1024]{1,0:T(8,128)S(1)}, u32[]{:S(2)}, u32[]{:S(2)}) %collective-permute-start.11) | collective-permute-done | bytes 131104 | tf_op jit(solution)/shard_map/ppermute | solution.py:19
  182.8 1.8 all-to-all-done.1
  184.6 43.1 %all-gather.2 = f32[128,256]{1,0:T(8,128)S(1)} all-gather(f32[8,256]{1,0:T(8,128)S(1)} %reduce_sum.28), channel_id=4, replica_groups=mesh['zh'=2,'y'=4,'c'=2,'zl'=8,'x'=4] {'zh','y','c'}, dimensions={0}, use_global_device_ids=true | all-gather | bytes 139264 | tf_op jit(solution)/shard_map/all_gather | solution.py:109
  (72 shorter events, 22.4 us)
Async XLA Ops:
  0.6 47.9 %collective-permute-start.1 = (f32[32,1024]{1,0:T(8,128)}, f32[32,1024]{1,0:T(8,128)S(1)}, u32[]{:S(2)}, u32[]{:S(2)}) collective-permute-start(f32[32,1024]{1,0:T(8,128)} %param.6), channel_id=1, source_target_pairs={{0,256},{256,0},{1,257},{257,1},{2,258},{258,2},{3,259},{259,3},{4... | collective-permute-start | bytes 393224 | tf_op jit(solution)/shard_map/ppermute | solution.py:19
  16.9 24.7 %collective-permute-start.12 = (f32[1,32,1024]{2,1,0:T(8,128)}, f32[1,32,1024]{2,1,0:T(8,128)S(1)}, u32[]{:S(2)}, u32[]{:S(2)}) collective-permute-start(f32[1,32,1024]{2,1,0:T(8,128)} %bitcast.141), channel_id=1, source_target_pairs={{0,16},{4,20},{8,24},{12,28},{16,0},{20,4},{24,8},{28,12},{1,17},{... | collective-permute-start | bytes 393224 | tf_op jit(solution)/shard_map/ppermute | solution.py:19
  32.8 33.6 %collective-permute-start = (f32[4,32,1024]{2,1,0:T(8,128)S(1)}, f32[4,32,1024]{2,1,0:T(8,128)S(1)}, u32[]{:S(2)}, u32[]{:S(2)}) collective-permute-start(f32[4,32,1024]{2,1,0:T(8,128)S(1)} %bitcast.127), channel_id=1, source_target_pairs={{0,32},{32,0},{1,33},{33,1},{2,34},{34,2},{3,35},{35,3},{4,36},{36... | collective-permute-start | bytes 1572872 | tf_op jit(solution)/shard_map/ppermute | solution.py:19
  42.5 21.2 %collective-permute-start.13 = (f32[2,32,1024]{2,1,0:T(8,128)S(1)}, f32[2,32,1024]{2,1,0:T(8,128)S(1)}, u32[]{:S(2)}, u32[]{:S(2)}) collective-permute-start(f32[2,32,1024]{2,1,0:T(8,128)S(1)} %maximum_bitcast_fusion), channel_id=1, source_target_pairs={{0,8},{4,12},{8,0},{12,4},{16,24},{20,28},{24,16},{28,20},{1,9},{5... | collective-permute-start | bytes 786440 | tf_op jit(solution)/shard_map/ppermute | solution.py:19
  60.0 6.5 %collective-permute-start.2 = (f32[4,32,1024]{2,1,0:T(8,128)S(1)}, f32[4,32,1024]{2,1,0:T(8,128)S(1)}, u32[]{:S(2)}, u32[]{:S(2)}) collective-permute-start(f32[4,32,1024]{2,1,0:T(8,128)S(1)} %bitcast.129), channel_id=1, source_target_pairs={{0,32},{32,0},{1,33},{33,1},{2,34},{34,2},{3,35},{35,3},{4,36},{36... | collective-permute-start | bytes 1572872 | tf_op jit(solution)/shard_map/ppermute | solution.py:19
  63.9 42.1 %collective-permute-start.14 = (f32[4,32,1024]{2,1,0:T(8,128)S(1)}, f32[4,32,1024]{2,1,0:T(8,128)S(1)}, u32[]{:S(2)}, u32[]{:S(2)}) collective-permute-start(f32[4,32,1024]{2,1,0:T(8,128)S(1)} %bitcast.132), channel_id=1, source_target_pairs={{0,4},{4,0},{8,12},{12,8},{16,20},{20,16},{24,28},{28,24},{1,5},{5... | collective-permute-start | bytes 1572872 | tf_op jit(solution)/shard_map/ppermute | solution.py:19
  67.0 1.0 copy-start.9
  67.2 6.0 %copy-start.8 = (f32[1,4,1,32,512]{4,3,2,1,0:T(8,128)S(1)}, f32[1,4,1,32,512]{4,3,2,1,0:T(8,128)}, u32[]{:S(2)}) copy-start(f32[1,4,1,32,512]{4,3,2,1,0:T(8,128)} %get-tuple-element.8) | copy-start | bytes 786436
  68.7 8.1 %copy-start.7 = (f32[1,4,1,32,512]{4,3,2,1,0:T(8,128)S(1)}, f32[1,4,1,32,512]{4,3,2,1,0:T(8,128)}, u32[]{:S(2)}) copy-start(f32[1,4,1,32,512]{4,3,2,1,0:T(8,128)} %get-tuple-element.3) | copy-start | bytes 786436
  68.7 17.1 %collective-permute-start.7 = (f32[128,1024]{1,0:T(8,128)S(1)}, f32[128,1024]{1,0:T(8,128)S(1)}, u32[]{:S(2)}, u32[]{:S(2)}) collective-permute-start(f32[128,1024]{1,0:T(8,128)S(1)} %fusion.19), channel_id=1, source_target_pairs={{0,3},{1,0},{2,1},{3,2},{4,7},{5,4},{6,5},{7,6},{8,11},{9,8},{10,9... | collective-permute-start | bytes 1572872 | tf_op jit(solution)/shard_map/ppermute | solution.py:14
  74.8 5.0 %copy-start.6 = (f32[1,4,1,32,512]{4,3,2,1,0:T(8,128)S(1)}, f32[1,4,1,32,512]{4,3,2,1,0:T(8,128)}, u32[]{:S(2)}) copy-start(f32[1,4,1,32,512]{4,3,2,1,0:T(8,128)} %get-tuple-element.5) | copy-start | bytes 786436
  74.8 34.9 %collective-permute-start.6 = (f32[128,1024]{1,0:T(8,128)}, f32[128,1024]{1,0:T(8,128)}, u32[]{:S(2)}, u32[]{:S(2)}) collective-permute-start(f32[128,1024]{1,0:T(8,128)} %fusion.18), channel_id=1, source_target_pairs={{0,1},{1,2},{2,3},{3,0},{4,5},{5,6},{6,7},{7,4},{8,9},{9,10},{10,1... | collective-permute-start | bytes 1572872 | tf_op jit(solution)/shard_map/ppermute | solution.py:14
  77.6 8.2 %copy-start.5 = (f32[1,4,1,32,512]{4,3,2,1,0:T(8,128)S(1)}, f32[1,4,1,32,512]{4,3,2,1,0:T(8,128)}, u32[]{:S(2)}) copy-start(f32[1,4,1,32,512]{4,3,2,1,0:T(8,128)} %get-tuple-element.7) | copy-start | bytes 786436
  77.6 24.8 %collective-permute-start.4 = (f32[128,1024]{1,0:T(8,128)S(1)}, f32[128,1024]{1,0:T(8,128)S(1)}, u32[]{:S(2)}, u32[]{:S(2)}) collective-permute-start(f32[128,1024]{1,0:T(8,128)S(1)} %fusion.17), channel_id=1, source_target_pairs={{0,1},{1,2},{2,3},{3,0},{4,5},{5,6},{6,7},{7,4},{8,9},{9,10},{10,1... | collective-permute-start | bytes 1572872 | tf_op jit(solution)/shard_map/ppermute | solution.py:14
  81.3 30.3 %collective-permute-start.3 = (f32[128,1024]{1,0:T(8,128)}, f32[128,1024]{1,0:T(8,128)}, u32[]{:S(2)}, u32[]{:S(2)}) collective-permute-start(f32[128,1024]{1,0:T(8,128)} %fusion.16), channel_id=1, source_target_pairs={{0,3},{1,0},{2,1},{3,2},{4,7},{5,4},{6,5},{7,6},{8,11},{9,8},{10,9... | collective-permute-start | bytes 1572872 | tf_op jit(solution)/shard_map/ppermute | solution.py:14
  87.3 22.4 %collective-permute-start.8 = (f32[128,1024]{1,0:T(8,128)}, f32[128,1024]{1,0:T(8,128)}, u32[]{:S(2)}, u32[]{:S(2)}) collective-permute-start(f32[128,1024]{1,0:T(8,128)} %convolution_add_fusion.1), channel_id=1, source_target_pairs={{0,3},{1,0},{2,1},{3,2},{4,7},{5,4},{6,5},{7,6},{8,11},{9,8},{10,9... | collective-permute-start | bytes 1572872 | tf_op jit(solution)/shard_map/ppermute | solution.py:14
  103.9 15.5 %collective-permute-start.5 = (f32[128,1024]{1,0:T(8,128)}, f32[128,1024]{1,0:T(8,128)}, u32[]{:S(2)}, u32[]{:S(2)}) collective-permute-start(f32[128,1024]{1,0:T(8,128)} %convolution_add_fusion.3), channel_id=1, source_target_pairs={{0,1},{1,2},{2,3},{3,0},{4,5},{5,6},{6,7},{7,4},{8,9},{9,10},{10,1... | collective-permute-start | bytes 1572872 | tf_op jit(solution)/shard_map/ppermute | solution.py:14
  106.3 3.4 %copy-start.11 = (f32[1,4,1,32,512]{4,3,2,1,0:T(8,128)S(1)}, f32[1,4,1,32,512]{4,3,2,1,0:T(8,128)}, u32[]{:S(2)}) copy-start(f32[1,4,1,32,512]{4,3,2,1,0:T(8,128)} %get-tuple-element.2) | copy-start | bytes 786436
  109.7 9.7 %copy-start.10 = (f32[1,4,1,32,512]{4,3,2,1,0:T(8,128)S(1)}, f32[1,4,1,32,512]{4,3,2,1,0:T(8,128)}, u32[]{:S(2)}) copy-start(f32[1,4,1,32,512]{4,3,2,1,0:T(8,128)} %get-tuple-element.6) | copy-start | bytes 786436
  111.7 9.6 %copy-start = (f32[128,1024]{1,0:T(8,128)}, f32[128,1024]{1,0:T(8,128)S(1)}, u32[]{:S(2)}) copy-start(f32[128,1024]{1,0:T(8,128)S(1)} %fusion) | copy-start | bytes 1572868
  121.3 0.8 copy-start.2
  123.1 7.5 %copy-start.1 = (f32[128,1024]{1,0:T(8,128)S(1)}, f32[128,1024]{1,0:T(8,128)}, u32[]{:S(2)}) copy-start(f32[128,1024]{1,0:T(8,128)} %copy-done) | copy-start | bytes 1572868
  123.1 7.5 %copy-start.3 = (f32[128,1024]{1,0:T(8,128)S(1)}, f32[128,1024]{1,0:T(8,128)}, u32[]{:S(2)}) copy-start(f32[128,1024]{1,0:T(8,128)} %copy-done.2) | copy-start | bytes 1572868
  124.8 9.4 %copy-start.4 = (f32[256,2,1,256]{3,2,1,0:T(1,128)S(1)}, f32[256,2,1,256]{3,2,1,0:T(1,128)}, u32[]{:S(2)}) copy-start(f32[256,2,1,256]{3,2,1,0:T(1,128)} %get-tuple-element.12) | copy-start | bytes 1572868
  126.4 7.9 %collective-permute-start.15 = (f32[2,512,256]{2,1,0:T(8,128)}, f32[2,512,256]{2,1,0:T(8,128)}, u32[]{:S(2)}, u32[]{:S(2)}) collective-permute-start(f32[2,512,256]{2,1,0:T(8,128)} %fusion.9), channel_id=1, source_target_pairs={{0,32},{32,0},{1,33},{33,1},{2,34},{34,2},{3,35},{35,3},{4,36},{36... | collective-permute-start | bytes 3145736 | tf_op jit(solution)/shard_map/ppermute | solution.py:19
  131.5 15.6 %collective-permute-start.9 = (f32[2,2,32,1024]{3,2,1,0:T(8,128)}, f32[2,2,32,1024]{3,2,1,0:T(8,128)S(1)}, u32[]{:S(2)}, u32[]{:S(2)}) collective-permute-start(f32[2,2,32,1024]{3,2,1,0:T(8,128)} %fusion.5), channel_id=1, source_target_pairs={{0,4},{4,0},{8,12},{12,8},{16,20},{20,16},{24,28},{28,24},{1,5},{5... | collective-permute-start | bytes 1572872 | tf_op jit(solution)/shard_map/ppermute | solution.py:19
  137.2 33.6 %all-to-all-start = ((f32[16,8,8,256]{3,2,1,0:T(8,128)}), f32[16,8,8,256]{3,2,1,0:T(8,128)S(1)}, u32[]{:S(2)}, u32[]{:S(2)}) async-start(f32[16,8,8,256]{3,2,1,0:T(8,128)} %bitcast.48), calls=%async_computation | async-start | bytes 2097152 | tf_op jit(solution)/shard_map/all_to_all | solution.py:107
  147.1 80.6 %copy-start.12 = (f32[32,512]{1,0:T(8,128)S(1)}, f32[32,512]{1,0:T(8,128)}, u32[]{:S(2)}) copy-start(f32[32,512]{1,0:T(8,128)} %param.7) | copy-start | bytes 196612
  147.1 16.1 %collective-permute-start.10 = (f32[2,32,1024]{2,1,0:T(8,128)S(1)}, f32[2,32,1024]{2,1,0:T(8,128)S(1)}, u32[]{:S(2)}, u32[]{:S(2)}) collective-permute-start(f32[2,32,1024]{2,1,0:T(8,128)S(1)} %dynamic-slice_bitcast_fusion), channel_id=1, source_target_pairs={{0,8},{4,12},{8,0},{12,4},{16,24},{20,28},{24,16},{28,20},{1,9},{5... | collective-permute-start | bytes 786440 | tf_op jit(solution)/shard_map/ppermute | solution.py:19
  163.3 18.9 %collective-permute-start.11 = (f32[32,1024]{1,0:T(8,128)S(1)}, f32[32,1024]{1,0:T(8,128)S(1)}, u32[]{:S(2)}, u32[]{:S(2)}) collective-permute-start(f32[32,1024]{1,0:T(8,128)S(1)} %dynamic-slice_bitcast_fusion.1), channel_id=1, source_target_pairs={{0,16},{4,20},{8,24},{12,28},{16,0},{20,4},{24,8},{28,12},{1,17},{... | collective-permute-start | bytes 393224 | tf_op jit(solution)/shard_map/ppermute | solution.py:19
  171.5 13.1 %all-to-all-start.1 = ((f32[8,8,256]{2,1,0:T(8,128)}), f32[8,8,256]{2,1,0:T(8,128)S(1)}, u32[]{:S(2)}, u32[]{:S(2)}) async-start(f32[8,8,256]{2,1,0:T(8,128)} %reduce_sum.27), calls=%async_computation.1 | async-start | bytes 131072 | tf_op jit(solution)/shard_map/all_to_all | solution.py:108

commit v2 on v1

v2 whole, which is shorter than its diff:
```python
import jax
import jax.numpy as jnp
from jax import lax
from jax.sharding import Mesh
from jax.sharding import PartitionSpec as P

HIGH = lax.Precision.HIGH
PROW = ("zh", "y", "c")
PCOL = ("zl", "x")


def shift(x, axis, by):
    n = lax.axis_size(axis)
    return lax.ppermute(x, axis, [(i, (i + by) % n) for i in range(n)])


def swap(x, axis, bit):
    n = lax.axis_size(axis)
    return lax.ppermute(x, axis, [(i, i ^ bit) for i in range(n)])


def spread(x, axes):
    copies = jnp.broadcast_to(x, (lax.axis_size(axes), *x.shape))
    return lax.all_to_all(copies, axes, 0, 0, tiled=True)


def ordered(mine, other, bit, axis):
    low = bit == 0
    return jnp.stack([jnp.where(low, mine, other), jnp.where(low, other, mine)], axis)


def pick(x, index, axis):
    return lax.dynamic_index_in_dim(x, index, axis, keepdims=False)


def dot(a, b):
    return jnp.dot(a, b, precision=HIGH, preferred_element_type=jnp.float32)


def gathered_column(panel):
    c = lax.axis_index("c")
    zh = lax.axis_index("zh")
    far = swap(panel, "zh", 1)
    near = spread(panel, "y")
    far = spread(far, "y")
    near = ordered(near, swap(near, "c", 1), c, 1)
    far = ordered(far, swap(far, "c", 1), c, 1)
    return ordered(near, far, zh, 0)


def gathered_over_zl(rows):
    zl = lax.axis_index("zl")
    rows = rows[None]
    for bit in (4, 2, 1):
        other = swap(rows, "zl", bit)
        rows = ordered(rows, other, zl & bit, 1 if bit != 4 else 0)
        rows = rows.reshape(-1, *rows.shape[2:])
    return rows


def reduced_products(inverse_tiles, codes, column):
    x = lax.axis_index("x")
    slots, block = inverse_tiles.shape[:2]
    tiles = inverse_tiles.reshape(slots, 4, 4, block // 16, block)
    column = column.reshape(block, -1)

    def product(d, i):
        part = pick(tiles, (x + d) % 4, 2)
        left = jnp.where(codes[0] == i, part[0], jnp.where(codes[1] == i, part[1], 0.0))
        return dot(left.reshape(block // 4, block), column)

    up_a = shift(product(2, 0), "x", 1)
    down_a = shift(product(2, 1), "x", -1)
    up_b = shift(product(1, 1), "x", 1)
    down_b = shift(product(3, 0), "x", -1)
    up_c = shift(product(1, 0) + up_a, "x", 1)
    down_c = shift(product(3, 1) + down_a, "x", -1)
    return product(0, 0) + down_b + up_c, product(0, 1) + up_b + down_c


def reduced_over_zl(t):
    zl = lax.axis_index("zl")
    for bit, axis in ((1, 2), (2, 1), (4, 0)):
        mine = (zl // bit) % 2
        t = pick(t, mine, axis) + swap(pick(t, 1 - mine, axis), "zl", bit)
    return t


def local(inverse_tiles, tile_rows, panel, pivot_base):
    share, width = panel.shape
    block = inverse_tiles.shape[1]
    half = block // 2
    c = lax.axis_index("c")
    codes = tile_rows[:, 0]
    column = gathered_column(panel)
    u = gathered_over_zl(panel).reshape(8 * share, width).T
    t = jnp.concatenate(reduced_products(inverse_tiles, codes, column))
    trailing = reduced_over_zl(t.reshape(2, 2, 2, share, width))

    def pivot(side):
        parts = []
        for j in range(2):
            v = lax.dynamic_slice_in_dim(t[:, j * block : (j + 1) * block], side * half, half, 1)
            parts.append(dot(u[j * block : (j + 1) * block], v))
        return jnp.stack(parts)

    away = swap(pivot(1 - c), "c", 1)
    w = pivot(c) + away
    w = w.reshape(8, 4, 4, 8, half).transpose(2, 1, 0, 3, 4)
    w = w.reshape(16, 8, 8, half)
    w = lax.all_to_all(w, ("y", "x"), 0, 0, tiled=True).sum(axis=0)
    w = jnp.concatenate([w, w])
    w = lax.all_to_all(w, ("zh", "zl"), 0, 0, tiled=True).sum(axis=0)
    w = spread(w, ("y", "c"))
    w = w.reshape(4, 2, 8, half).transpose(0, 2, 1, 3).reshape(share, block)
    return (-trailing, pivot_base + w)


def solution(mesh):
    finer = Mesh(mesh.devices.reshape(2, 4, 2, 8, 4), PROW + PCOL)
    placed = (P(PROW, PCOL, None), P(PROW, PCOL), P(PROW + PCOL, None), P(PCOL, None))

    return jax.shard_map(
        local,
        mesh=finer,
        in_specs=placed,
        out_specs=(P(PROW + PCOL, None), P(PCOL, None)),
        check_vma=False,
    )
```

time: 229 us -> 196 us (0.86)
  blocking collectives: 66.4 us -> 0 us
  starting transfers between devices: 78.8 us -> 118 us
  matrix products: 15 us -> 9.17 us
  local copies, waits for them, and re-layouts: 9.95 us -> 5.84 us
  other arithmetic: 7.92 us -> 10.8 us
    all_gather x3 -> x0, blocking collectives: 66.4 us -> none  [the longest x1 43.1 us: local(): w = lax.all_gather(w, PROW, axis=0).reshape(2, 4, 2, 8, half).sum(axis=0)]
    all_to_all x1 -> x4, starting transfers between devices: 3.35 us -> 25.4 us  [the longest x3 20.6 us: spread(): return lax.all_to_all(copies, axes, 0, 0, tiled=True)]
    ppermute x10, waiting for transfers between devices: 25.5 us -> 5.52 us  [swap(): return lax.ppermute(x, axis, [(i, i ^ bit) for i in range(n)])]
    ppermute x10, starting transfers between devices: 51.9 us -> 66.2 us  [swap(): return lax.ppermute(x, axis, [(i, i ^ bit) for i in range(n)])]
    all_to_all x1, waiting for transfers between devices: 0.01 us -> 10.7 us  [local(): w = lax.all_to_all(w, ('y', 'x'), 0, 0, tiled=True).sum(axis=0)]
    all_to_all x1 -> x4, waiting for transfers between devices: 1.76 us -> 8.9 us  [the longest x1 4.7 us: local(): w = lax.all_to_all(w, ('zh', 'zl'), 0, 0, tiled=True).sum(axis=0)]
    dot_general x10 -> x12, matrix products: 15 us -> 9.17 us  [dot(): return jnp.dot(a, b, precision=HIGH, preferred_element_type=jnp.float32)]
    another operation x2 -> x0, local copies, waits for them, and re-layouts: 3.33 us -> none  [local(): u = upper.reshape(8 * share, 2, block)]
  transfers between devices with their start and end apart: 18 -> 21, of which waited for: 6 -> 9; matrix products, arithmetic and copies ran while one was open for 11% -> 10% of each run, Pallas kernels for 0% -> 0%
where the time goes in v2:
time: 196 us; the launch traced here: 193 us
  starting transfers between devices  118 us (60%)
  waiting for transfers between devices  45.3 us (23%)
  other arithmetic  10.8 us (6%)
  matrix products  9.17 us (5%)
  local copies, waits for them, and re-layouts  5.84 us (3%)
  between operations  4.05 us (2%)
    ppermute x10, starting transfers between devices, swap(): return lax.ppermute(x, axis, [(i, i ^ bit) for i in range(n)])  66.2 us
    all_to_all x3, starting transfers between devices, spread(): return lax.all_to_all(copies, axes, 0, 0, tiled=True)  20.6 us
    ppermute x6, waiting for transfers between devices, shift(): return lax.ppermute(x, axis, [(i, (i + by) % n) for i in range(n)])  20.2 us
    ppermute x6, starting transfers between devices, shift(): return lax.ppermute(x, axis, [(i, (i + by) % n) for i in range(n)])  18.8 us
    all_to_all x1, waiting for transfers between devices, local(): w = lax.all_to_all(w, ('y', 'x'), 0, 0, tiled=True).sum(axis=0)  10.7 us
    dot_general x12, matrix products, dot(): return jnp.dot(a, b, precision=HIGH, preferred_element_type=jnp.float32)  9.17 us
    all_to_all x1, starting transfers between devices, local(): w = lax.all_to_all(w, ('y', 'x'), 0, 0, tiled=True).sum(axis=0)  7.76 us
    ppermute x10, waiting for transfers between devices, swap(): return lax.ppermute(x, axis, [(i, i ^ bit) for i in range(n)])  5.52 us
  transfers between devices with their start and end apart: 21, of which 9 were waited for; matrix products, arithmetic and copies ran while one was open for 10% of the time, Pallas kernels for 0%

profile of v2, /device:TPU:1, one launch (start us, length us, event | category | flops | bytes accessed | tf_op | source)
XLA Modules:
  0.0 193.3 jit_solution(18127031337304562568)
XLA Ops:
  0.6 1.8 broadcast_in_dim.24
  2.4 5.1 %all-to-all-start = ((f32[4,32,1024]{2,1,0:T(8,128)}), f32[4,32,1024]{2,1,0:T(8,128)S(1)}, u32[]{:S(2)}, u32[]{:S(2)}) async-start(f32[4,32,1024]{2,1,0:T(8,128)} %broadcast_in_dim.24), calls=%async_computation | async-start | bytes 1048576 | tf_op jit(solution)/shard_map/all_to_all | solution.py:24
  7.5 8.8 %collective-permute-start.12 = (f32[1,32,1024]{2,1,0:T(8,128)}, f32[1,32,1024]{2,1,0:T(8,128)S(1)}, u32[]{:S(2)}, u32[]{:S(2)}) collective-permute-start(f32[1,32,1024]{2,1,0:T(8,128)} %bitcast.128), channel_id=1, source_target_pairs={{0,16},{4,20},{8,24},{12,28},{16,0},{20,4},{24,8},{28,12},{1,17},{... | collective-permute-start | bytes 393224 | tf_op jit(solution)/shard_map/ppermute | solution.py:19
  16.3 10.6 %collective-permute-start.1 = (f32[32,1024]{1,0:T(8,128)}, f32[32,1024]{1,0:T(8,128)S(1)}, u32[]{:S(2)}, u32[]{:S(2)}) collective-permute-start(f32[32,1024]{1,0:T(8,128)} %param.6), channel_id=1, source_target_pairs={{0,256},{256,0},{1,257},{257,1},{2,258},{258,2},{3,259},{259,3},{4... | collective-permute-start | bytes 393224 | tf_op jit(solution)/shard_map/ppermute | solution.py:19
  28.0 3.9 %collective-permute-done.1 = f32[32,1024]{1,0:T(8,128)S(1)} collective-permute-done((f32[32,1024]{1,0:T(8,128)}, f32[32,1024]{1,0:T(8,128)S(1)}, u32[]{:S(2)}, u32[]{:S(2)}) %collective-permute-start.1) | collective-permute-done | bytes 131104 | tf_op jit(solution)/shard_map/ppermute | solution.py:19
  32.8 3.7 %all-to-all-start.1 = ((f32[4,32,1024]{2,1,0:T(8,128)}), f32[4,32,1024]{2,1,0:T(8,128)S(1)}, u32[]{:S(2)}, u32[]{:S(2)}) async-start(f32[4,32,1024]{2,1,0:T(8,128)} %broadcast_in_dim.25), calls=%async_computation.1 | async-start | bytes 1048576 | tf_op jit(solution)/shard_map/all_to_all | solution.py:24
  37.2 16.3 %collective-permute-start.13 = (f32[2,32,1024]{2,1,0:T(8,128)}, f32[2,32,1024]{2,1,0:T(8,128)}, u32[]{:S(2)}, u32[]{:S(2)}) collective-permute-start(f32[2,32,1024]{2,1,0:T(8,128)} %maximum_bitcast_fusion), channel_id=1, source_target_pairs={{0,8},{4,12},{8,0},{12,4},{16,24},{20,28},{24,16},{28,20},{1,9},{5... | collective-permute-start | bytes 786440 | tf_op jit(solution)/shard_map/ppermute | solution.py:19
  56.7 3.5 %collective-permute-start = (f32[4,32,1024]{2,1,0:T(8,128)S(1)}, f32[4,32,1024]{2,1,0:T(8,128)}, u32[]{:S(2)}, u32[]{:S(2)}) collective-permute-start(f32[4,32,1024]{2,1,0:T(8,128)S(1)} %all-to-all-done), channel_id=1, source_target_pairs={{0,32},{32,0},{1,33},{33,1},{2,34},{34,2},{3,35},{35,3},{4,36},{36... | collective-permute-start | bytes 1572872 | tf_op jit(solution)/shard_map/ppermute | solution.py:19
  60.2 1.4 select_select_fusion.7
  61.6 1.9 collective-permute-start.2
  64.6 6.9 %collective-permute-start.14 = (f32[4,32,1024]{2,1,0:T(8,128)S(1)}, f32[4,32,1024]{2,1,0:T(8,128)S(1)}, u32[]{:S(2)}, u32[]{:S(2)}) collective-permute-start(f32[4,32,1024]{2,1,0:T(8,128)S(1)} %bitcast.119), channel_id=1, source_target_pairs={{0,4},{4,0},{8,12},{12,8},{16,20},{20,16},{24,28},{28,24},{1,5},{5... | collective-permute-start | bytes 1572872 | tf_op jit(solution)/shard_map/ppermute | solution.py:19
  74.8 3.3 %collective-permute-start.4 = (f32[128,1024]{1,0:T(8,128)S(1)}, f32[128,1024]{1,0:T(8,128)S(1)}, u32[]{:S(2)}, u32[]{:S(2)}) collective-permute-start(f32[128,1024]{1,0:T(8,128)S(1)} %fusion.19), channel_id=1, source_target_pairs={{0,1},{1,2},{2,3},{3,0},{4,5},{5,6},{6,7},{7,4},{8,9},{9,10},{10,1... | collective-permute-start | bytes 1572872 | tf_op jit(solution)/shard_map/ppermute | solution.py:14
  78.9 3.5 %collective-permute-start.3 = (f32[128,1024]{1,0:T(8,128)S(1)}, f32[128,1024]{1,0:T(8,128)S(1)}, u32[]{:S(2)}, u32[]{:S(2)}) collective-permute-start(f32[128,1024]{1,0:T(8,128)S(1)} %fusion.18), channel_id=1, source_target_pairs={{0,3},{1,0},{2,1},{3,2},{4,7},{5,4},{6,5},{7,6},{8,11},{9,8},{10,9... | collective-permute-start | bytes 1572872 | tf_op jit(solution)/shard_map/ppermute | solution.py:14
  83.3 3.3 %collective-permute-start.7 = (f32[128,1024]{1,0:T(8,128)S(1)}, f32[128,1024]{1,0:T(8,128)S(1)}, u32[]{:S(2)}, u32[]{:S(2)}) collective-permute-start(f32[128,1024]{1,0:T(8,128)S(1)} %fusion.21), channel_id=1, source_target_pairs={{0,3},{1,0},{2,1},{3,2},{4,7},{5,4},{6,5},{7,6},{8,11},{9,8},{10,9... | collective-permute-start | bytes 1572872 | tf_op jit(solution)/shard_map/ppermute | solution.py:14
  87.4 2.2 %collective-permute-start.6 = (f32[128,1024]{1,0:T(8,128)S(1)}, f32[128,1024]{1,0:T(8,128)S(1)}, u32[]{:S(2)}, u32[]{:S(2)}) collective-permute-start(f32[128,1024]{1,0:T(8,128)S(1)} %fusion.20), channel_id=1, source_target_pairs={{0,1},{1,2},{2,3},{3,0},{4,5},{5,6},{6,7},{7,4},{8,9},{9,10},{10,1... | collective-permute-start | bytes 1572872 | tf_op jit(solution)/shard_map/ppermute | solution.py:14
  91.5 1.9 collective-permute-start.5
  93.5 11.1 %collective-permute-done.7 = f32[128,1024]{1,0:T(8,128)S(1)} collective-permute-done((f32[128,1024]{1,0:T(8,128)S(1)}, f32[128,1024]{1,0:T(8,128)S(1)}, u32[]{:S(2)}, u32[]{:S(2)}) %collective-permute-start.7) | collective-permute-done | bytes 524320 | tf_op jit(solution)/shard_map/ppermute | solution.py:14
  105.4 4.6 %collective-permute-start.8 = (f32[128,1024]{1,0:T(8,128)S(1)}, f32[128,1024]{1,0:T(8,128)S(1)}, u32[]{:S(2)}, u32[]{:S(2)}) collective-permute-start(f32[128,1024]{1,0:T(8,128)S(1)} %convolution_add_fusion), channel_id=1, source_target_pairs={{0,3},{1,0},{2,1},{3,2},{4,7},{5,4},{6,5},{7,6},{8,11},{9,8},{10,9... | collective-permute-start | bytes 1572872 | tf_op jit(solution)/shard_map/ppermute | solution.py:14
  110.4 3.4 %collective-permute-done.5 = f32[128,1024]{1,0:T(8,128)S(1)} collective-permute-done((f32[128,1024]{1,0:T(8,128)S(1)}, f32[128,1024]{1,0:T(8,128)S(1)}, u32[]{:S(2)}, u32[]{:S(2)}) %collective-permute-start.5) | collective-permute-done | bytes 524320 | tf_op jit(solution)/shard_map/ppermute | solution.py:14
  114.6 4.7 %collective-permute-done.8 = f32[128,1024]{1,0:T(8,128)S(1)} collective-permute-done((f32[128,1024]{1,0:T(8,128)S(1)}, f32[128,1024]{1,0:T(8,128)S(1)}, u32[]{:S(2)}, u32[]{:S(2)}) %collective-permute-start.8) | collective-permute-done | bytes 524320 | tf_op jit(solution)/shard_map/ppermute | solution.py:14
  122.6 4.7 %collective-permute-start.15 = (f32[2,512,256]{2,1,0:T(8,128)}, f32[2,512,256]{2,1,0:T(8,128)}, u32[]{:S(2)}, u32[]{:S(2)}) collective-permute-start(f32[2,512,256]{2,1,0:T(8,128)} %pad_maximum_fusion.5), channel_id=1, source_target_pairs={{0,32},{32,0},{1,33},{33,1},{2,34},{34,2},{3,35},{35,3},{4,36},{36... | collective-permute-start | bytes 3145736 | tf_op jit(solution)/shard_map/ppermute | solution.py:19
  127.5 2.3 %collective-permute-start.9 = (f32[2,2,32,1024]{3,2,1,0:T(8,128)S(1)}, f32[2,2,32,1024]{3,2,1,0:T(8,128)S(1)}, u32[]{:S(2)}, u32[]{:S(2)}) collective-permute-start(f32[2,2,32,1024]{3,2,1,0:T(8,128)S(1)} %dynamic-slice_bitcast_fusion), channel_id=1, source_target_pairs={{0,4},{4,0},{8,12},{12,8},{16,20},{20,16},{24,28},{28,24},{1,5},{5... | collective-permute-start | bytes 1572872 | tf_op jit(solution)/shard_map/ppermute | solution.py:19
  131.2 1.4 maximum_add_fusion
  133.6 7.8 %all-to-all-start.2 = ((f32[16,8,8,256]{3,2,1,0:T(8,128)}), f32[16,8,8,256]{3,2,1,0:T(8,128)S(1)}, u32[]{:S(2)}, u32[]{:S(2)}) async-start(f32[16,8,8,256]{3,2,1,0:T(8,128)} %bitcast.46), calls=%async_computation.2 | async-start | bytes 2097152 | tf_op jit(solution)/shard_map/all_to_all | solution.py:111
  141.4 1.6 collective-permute-done.9
  143.1 4.0 %collective-permute-start.10 = (f32[2,32,1024]{2,1,0:T(8,128)S(1)}, f32[2,32,1024]{2,1,0:T(8,128)S(1)}, u32[]{:S(2)}, u32[]{:S(2)}) collective-permute-start(f32[2,32,1024]{2,1,0:T(8,128)S(1)} %dynamic-slice_bitcast_fusion.1), channel_id=1, source_target_pairs={{0,8},{4,12},{8,0},{12,4},{16,24},{20,28},{24,16},{28,20},{1,9},{5... | collective-permute-start | bytes 786440 | tf_op jit(solution)/shard_map/ppermute | solution.py:19
  147.2 10.7 %all-to-all-done.2 = f32[16,8,8,256]{3,2,1,0:T(8,128)S(1)} async-done(((f32[16,8,8,256]{3,2,1,0:T(8,128)}), f32[16,8,8,256]{3,2,1,0:T(8,128)S(1)}, u32[]{:S(2)}, u32[]{:S(2)}) %all-to-all-start.2) | async-done | bytes 1048608 | tf_op jit(solution)/shard_map/all_to_all | solution.py:111
  158.6 4.8 %all-to-all-start.3 = ((f32[16,8,256]{2,1,0:T(8,128)}), f32[16,8,256]{2,1,0:T(8,128)S(1)}, u32[]{:S(2)}, u32[]{:S(2)}) async-start(f32[16,8,256]{2,1,0:T(8,128)} %pad_maximum_fusion.7), calls=%async_computation.3 | async-start | bytes 262144 | tf_op jit(solution)/shard_map/all_to_all | solution.py:113
  163.5 7.1 %collective-permute-start.11 = (f32[32,1024]{1,0:T(8,128)S(1)}, f32[32,1024]{1,0:T(8,128)S(1)}, u32[]{:S(2)}, u32[]{:S(2)}) collective-permute-start(f32[32,1024]{1,0:T(8,128)S(1)} %dynamic-slice_bitcast_fusion.2), channel_id=1, source_target_pairs={{0,16},{4,20},{8,24},{12,28},{16,0},{20,4},{24,8},{28,12},{1,17},{... | collective-permute-start | bytes 393224 | tf_op jit(solution)/shard_map/ppermute | solution.py:19
  170.6 4.7 %all-to-all-done.3 = f32[16,8,256]{2,1,0:T(8,128)S(1)} async-done(((f32[16,8,256]{2,1,0:T(8,128)}), f32[16,8,256]{2,1,0:T(8,128)S(1)}, u32[]{:S(2)}, u32[]{:S(2)}) %all-to-all-start.3) | async-done | bytes 131104 | tf_op jit(solution)/shard_map/all_to_all | solution.py:113
  176.0 11.8 %all-to-all-start.4 = ((f32[8,8,256]{2,1,0:T(8,128)}), f32[8,8,256]{2,1,0:T(8,128)S(1)}, u32[]{:S(2)}, u32[]{:S(2)}) async-start(f32[8,8,256]{2,1,0:T(8,128)} %broadcast_in_dim.27), calls=%async_computation.4 | async-start | bytes 131072 | tf_op jit(solution)/shard_map/all_to_all | solution.py:24
  188.5 4.2 %all-to-all-done.4 = f32[8,8,256]{2,1,0:T(8,128)S(1)} async-done(((f32[8,8,256]{2,1,0:T(8,128)}), f32[8,8,256]{2,1,0:T(8,128)S(1)}, u32[]{:S(2)}, u32[]{:S(2)}) %all-to-all-start.4) | async-done | bytes 65568 | tf_op jit(solution)/shard_map/all_to_all | solution.py:24
  (83 shorter events, 22.3 us)
Async XLA Ops:
  2.4 51.1 %copy-start.14 = (s32[2,1]{0,1:T(1,128)S(1)}, s32[2,1]{0,1:T(1,128)}, u32[]{:S(2)}) copy-start(s32[2,1]{0,1:T(1,128)} %param.5) | copy-start | bytes 28
  2.4 57.8 %copy-start = (f32[2,512,512]{2,1,0:T(8,128)S(1)}, f32[2,512,512]{2,1,0:T(8,128)}, u32[]{:S(2)}) copy-start(f32[2,512,512]{2,1,0:T(8,128)} %param.4) | copy-start | bytes 6291460
  2.4 29.5 %all-to-all-start = ((f32[4,32,1024]{2,1,0:T(8,128)}), f32[4,32,1024]{2,1,0:T(8,128)S(1)}, u32[]{:S(2)}, u32[]{:S(2)}) async-start(f32[4,32,1024]{2,1,0:T(8,128)} %broadcast_in_dim.24), calls=%async_computation | async-start | bytes 1048576 | tf_op jit(solution)/shard_map/all_to_all | solution.py:24
  7.5 19.5 %collective-permute-start.12 = (f32[1,32,1024]{2,1,0:T(8,128)}, f32[1,32,1024]{2,1,0:T(8,128)S(1)}, u32[]{:S(2)}, u32[]{:S(2)}) collective-permute-start(f32[1,32,1024]{2,1,0:T(8,128)} %bitcast.128), channel_id=1, source_target_pairs={{0,16},{4,20},{8,24},{12,28},{16,0},{20,4},{24,8},{28,12},{1,17},{... | collective-permute-start | bytes 393224 | tf_op jit(solution)/shard_map/ppermute | solution.py:19
  16.3 15.6 %collective-permute-start.1 = (f32[32,1024]{1,0:T(8,128)}, f32[32,1024]{1,0:T(8,128)S(1)}, u32[]{:S(2)}, u32[]{:S(2)}) collective-permute-start(f32[32,1024]{1,0:T(8,128)} %param.6), channel_id=1, source_target_pairs={{0,256},{256,0},{1,257},{257,1},{2,258},{258,2},{3,259},{259,3},{4... | collective-permute-start | bytes 393224 | tf_op jit(solution)/shard_map/ppermute | solution.py:19
  32.8 28.8 %all-to-all-start.1 = ((f32[4,32,1024]{2,1,0:T(8,128)}), f32[4,32,1024]{2,1,0:T(8,128)S(1)}, u32[]{:S(2)}, u32[]{:S(2)}) async-start(f32[4,32,1024]{2,1,0:T(8,128)} %broadcast_in_dim.25), calls=%async_computation.1 | async-start | bytes 1048576 | tf_op jit(solution)/shard_map/all_to_all | solution.py:24
  37.2 26.3 %collective-permute-start.13 = (f32[2,32,1024]{2,1,0:T(8,128)}, f32[2,32,1024]{2,1,0:T(8,128)}, u32[]{:S(2)}, u32[]{:S(2)}) collective-permute-start(f32[2,32,1024]{2,1,0:T(8,128)} %maximum_bitcast_fusion), channel_id=1, source_target_pairs={{0,8},{4,12},{8,0},{12,4},{16,24},{20,28},{24,16},{28,20},{1,9},{5... | collective-permute-start | bytes 786440 | tf_op jit(solution)/shard_map/ppermute | solution.py:19
  56.7 14.7 %collective-permute-start = (f32[4,32,1024]{2,1,0:T(8,128)S(1)}, f32[4,32,1024]{2,1,0:T(8,128)}, u32[]{:S(2)}, u32[]{:S(2)}) collective-permute-start(f32[4,32,1024]{2,1,0:T(8,128)S(1)} %all-to-all-done), channel_id=1, source_target_pairs={{0,32},{32,0},{1,33},{33,1},{2,34},{34,2},{3,35},{35,3},{4,36},{36... | collective-permute-start | bytes 1572872 | tf_op jit(solution)/shard_map/ppermute | solution.py:19
  61.6 11.0 %collective-permute-start.2 = (f32[4,32,1024]{2,1,0:T(8,128)S(1)}, f32[4,32,1024]{2,1,0:T(8,128)S(1)}, u32[]{:S(2)}, u32[]{:S(2)}) collective-permute-start(f32[4,32,1024]{2,1,0:T(8,128)S(1)} %all-to-all-done.1), channel_id=1, source_target_pairs={{0,32},{32,0},{1,33},{33,1},{2,34},{34,2},{3,35},{35,3},{4,36},{36... | collective-permute-start | bytes 1572872 | tf_op jit(solution)/shard_map/ppermute | solution.py:19
  64.6 45.4 %collective-permute-start.14 = (f32[4,32,1024]{2,1,0:T(8,128)S(1)}, f32[4,32,1024]{2,1,0:T(8,128)S(1)}, u32[]{:S(2)}, u32[]{:S(2)}) collective-permute-start(f32[4,32,1024]{2,1,0:T(8,128)S(1)} %bitcast.119), channel_id=1, source_target_pairs={{0,4},{4,0},{8,12},{12,8},{16,20},{20,16},{24,28},{28,24},{1,5},{5... | collective-permute-start | bytes 1572872 | tf_op jit(solution)/shard_map/ppermute | solution.py:19
  73.2 4.8 %copy-start.9 = (f32[1,4,1,32,512]{4,3,2,1,0:T(8,128)S(1)}, f32[1,4,1,32,512]{4,3,2,1,0:T(8,128)}, u32[]{:S(2)}) copy-start(f32[1,4,1,32,512]{4,3,2,1,0:T(8,128)} %get-tuple-element.5) | copy-start | bytes 786436
  74.8 7.6 %copy-start.8 = (f32[1,4,1,32,512]{4,3,2,1,0:T(8,128)S(1)}, f32[1,4,1,32,512]{4,3,2,1,0:T(8,128)}, u32[]{:S(2)}) copy-start(f32[1,4,1,32,512]{4,3,2,1,0:T(8,128)} %get-tuple-element.9) | copy-start | bytes 786436
  74.8 15.9 %collective-permute-start.4 = (f32[128,1024]{1,0:T(8,128)S(1)}, f32[128,1024]{1,0:T(8,128)S(1)}, u32[]{:S(2)}, u32[]{:S(2)}) collective-permute-start(f32[128,1024]{1,0:T(8,128)S(1)} %fusion.19), channel_id=1, source_target_pairs={{0,1},{1,2},{2,3},{3,0},{4,5},{5,6},{6,7},{7,4},{8,9},{9,10},{10,1... | collective-permute-start | bytes 1572872 | tf_op jit(solution)/shard_map/ppermute | solution.py:14
  78.9 7.7 %copy-start.7 = (f32[1,4,1,32,512]{4,3,2,1,0:T(8,128)S(1)}, f32[1,4,1,32,512]{4,3,2,1,0:T(8,128)}, u32[]{:S(2)}) copy-start(f32[1,4,1,32,512]{4,3,2,1,0:T(8,128)} %get-tuple-element.8) | copy-start | bytes 786436
  78.9 31.5 %collective-permute-start.3 = (f32[128,1024]{1,0:T(8,128)S(1)}, f32[128,1024]{1,0:T(8,128)S(1)}, u32[]{:S(2)}, u32[]{:S(2)}) collective-permute-start(f32[128,1024]{1,0:T(8,128)S(1)} %fusion.18), channel_id=1, source_target_pairs={{0,3},{1,0},{2,1},{3,2},{4,7},{5,4},{6,5},{7,6},{8,11},{9,8},{10,9... | collective-permute-start | bytes 1572872 | tf_op jit(solution)/shard_map/ppermute | solution.py:14
  83.2 7.5 %copy-start.6 = (f32[1,4,1,32,512]{4,3,2,1,0:T(8,128)S(1)}, f32[1,4,1,32,512]{4,3,2,1,0:T(8,128)}, u32[]{:S(2)}) copy-start(f32[1,4,1,32,512]{4,3,2,1,0:T(8,128)} %get-tuple-element.4) | copy-start | bytes 786436
  83.3 21.3 %collective-permute-start.7 = (f32[128,1024]{1,0:T(8,128)S(1)}, f32[128,1024]{1,0:T(8,128)S(1)}, u32[]{:S(2)}, u32[]{:S(2)}) collective-permute-start(f32[128,1024]{1,0:T(8,128)S(1)} %fusion.21), channel_id=1, source_target_pairs={{0,3},{1,0},{2,1},{3,2},{4,7},{5,4},{6,5},{7,6},{8,11},{9,8},{10,9... | collective-permute-start | bytes 1572872 | tf_op jit(solution)/shard_map/ppermute | solution.py:14
  87.4 17.1 %copy-start.5 = (f32[1,4,1,32,512]{4,3,2,1,0:T(8,128)S(1)}, f32[1,4,1,32,512]{4,3,2,1,0:T(8,128)}, u32[]{:S(2)}) copy-start(f32[1,4,1,32,512]{4,3,2,1,0:T(8,128)} %get-tuple-element.7) | copy-start | bytes 786436
  87.4 27.2 %collective-permute-start.6 = (f32[128,1024]{1,0:T(8,128)S(1)}, f32[128,1024]{1,0:T(8,128)S(1)}, u32[]{:S(2)}, u32[]{:S(2)}) collective-permute-start(f32[128,1024]{1,0:T(8,128)S(1)} %fusion.20), channel_id=1, source_target_pairs={{0,1},{1,2},{2,3},{3,0},{4,5},{5,6},{6,7},{7,4},{8,9},{9,10},{10,1... | collective-permute-start | bytes 1572872 | tf_op jit(solution)/shard_map/ppermute | solution.py:14
  91.5 22.2 %collective-permute-start.5 = (f32[128,1024]{1,0:T(8,128)S(1)}, f32[128,1024]{1,0:T(8,128)S(1)}, u32[]{:S(2)}, u32[]{:S(2)}) collective-permute-start(f32[128,1024]{1,0:T(8,128)S(1)} %convolution_add_fusion.2), channel_id=1, source_target_pairs={{0,1},{1,2},{2,3},{3,0},{4,5},{5,6},{6,7},{7,4},{8,9},{9,10},{10,1... | collective-permute-start | bytes 1572872 | tf_op jit(solution)/shard_map/ppermute | solution.py:14
  105.4 13.9 %collective-permute-start.8 = (f32[128,1024]{1,0:T(8,128)S(1)}, f32[128,1024]{1,0:T(8,128)S(1)}, u32[]{:S(2)}, u32[]{:S(2)}) collective-permute-start(f32[128,1024]{1,0:T(8,128)S(1)} %convolution_add_fusion), channel_id=1, source_target_pairs={{0,3},{1,0},{2,1},{3,2},{4,7},{5,4},{6,5},{7,6},{8,11},{9,8},{10,9... | collective-permute-start | bytes 1572872 | tf_op jit(solution)/shard_map/ppermute | solution.py:14
  110.1 3.6 %copy-start.12 = (f32[1,4,1,32,512]{4,3,2,1,0:T(8,128)S(1)}, f32[1,4,1,32,512]{4,3,2,1,0:T(8,128)}, u32[]{:S(2)}) copy-start(f32[1,4,1,32,512]{4,3,2,1,0:T(8,128)} %get-tuple-element.2) | copy-start | bytes 786436
  110.3 9.0 %copy-start.11 = (f32[1,4,1,32,512]{4,3,2,1,0:T(8,128)S(1)}, f32[1,4,1,32,512]{4,3,2,1,0:T(8,128)}, u32[]{:S(2)}) copy-start(f32[1,4,1,32,512]{4,3,2,1,0:T(8,128)} %get-tuple-element.6) | copy-start | bytes 786436
  122.6 8.5 %collective-permute-start.15 = (f32[2,512,256]{2,1,0:T(8,128)}, f32[2,512,256]{2,1,0:T(8,128)}, u32[]{:S(2)}, u32[]{:S(2)}) collective-permute-start(f32[2,512,256]{2,1,0:T(8,128)} %pad_maximum_fusion.5), channel_id=1, source_target_pairs={{0,32},{32,0},{1,33},{33,1},{2,34},{34,2},{3,35},{35,3},{4,36},{36... | collective-permute-start | bytes 3145736 | tf_op jit(solution)/shard_map/ppermute | solution.py:19
  127.3 3.2 %copy-start.2 = (f32[256,512]{1,0:T(8,128)S(1)}, f32[256,512]{1,0:T(8,128)}, u32[]{:S(2)}) copy-start(f32[256,512]{1,0:T(8,128)} %copy-done.1) | copy-start | bytes 1572868
  127.5 15.5 %collective-permute-start.9 = (f32[2,2,32,1024]{3,2,1,0:T(8,128)S(1)}, f32[2,2,32,1024]{3,2,1,0:T(8,128)S(1)}, u32[]{:S(2)}, u32[]{:S(2)}) collective-permute-start(f32[2,2,32,1024]{3,2,1,0:T(8,128)S(1)} %dynamic-slice_bitcast_fusion), channel_id=1, source_target_pairs={{0,4},{4,0},{8,12},{12,8},{16,20},{20,16},{24,28},{28,24},{1,5},{5... | collective-permute-start | bytes 1572872 | tf_op jit(solution)/shard_map/ppermute | solution.py:19
  133.6 24.2 %all-to-all-start.2 = ((f32[16,8,8,256]{3,2,1,0:T(8,128)}), f32[16,8,8,256]{3,2,1,0:T(8,128)S(1)}, u32[]{:S(2)}, u32[]{:S(2)}) async-start(f32[16,8,8,256]{3,2,1,0:T(8,128)} %bitcast.46), calls=%async_computation.2 | async-start | bytes 2097152 | tf_op jit(solution)/shard_map/all_to_all | solution.py:111
  143.1 49.6 %copy-start.13 = (f32[32,512]{1,0:T(8,128)S(1)}, f32[32,512]{1,0:T(8,128)}, u32[]{:S(2)}) copy-start(f32[32,512]{1,0:T(8,128)} %param.7) | copy-start | bytes 196612
  143.1 20.3 %collective-permute-start.10 = (f32[2,32,1024]{2,1,0:T(8,128)S(1)}, f32[2,32,1024]{2,1,0:T(8,128)S(1)}, u32[]{:S(2)}, u32[]{:S(2)}) collective-permute-start(f32[2,32,1024]{2,1,0:T(8,128)S(1)} %dynamic-slice_bitcast_fusion.1), channel_id=1, source_target_pairs={{0,8},{4,12},{8,0},{12,4},{16,24},{20,28},{24,16},{28,20},{1,9},{5... | collective-permute-start | bytes 786440 | tf_op jit(solution)/shard_map/ppermute | solution.py:19
  158.6 16.7 %all-to-all-start.3 = ((f32[16,8,256]{2,1,0:T(8,128)}), f32[16,8,256]{2,1,0:T(8,128)S(1)}, u32[]{:S(2)}, u32[]{:S(2)}) async-start(f32[16,8,256]{2,1,0:T(8,128)} %pad_maximum_fusion.7), calls=%async_computation.3 | async-start | bytes 262144 | tf_op jit(solution)/shard_map/all_to_all | solution.py:113
  163.5 24.3 %collective-permute-start.11 = (f32[32,1024]{1,0:T(8,128)S(1)}, f32[32,1024]{1,0:T(8,128)S(1)}, u32[]{:S(2)}, u32[]{:S(2)}) collective-permute-start(f32[32,1024]{1,0:T(8,128)S(1)} %dynamic-slice_bitcast_fusion.2), channel_id=1, source_target_pairs={{0,16},{4,20},{8,24},{12,28},{16,0},{20,4},{24,8},{28,12},{1,17},{... | collective-permute-start | bytes 393224 | tf_op jit(solution)/shard_map/ppermute | solution.py:19
  176.0 16.7 %all-to-all-start.4 = ((f32[8,8,256]{2,1,0:T(8,128)}), f32[8,8,256]{2,1,0:T(8,128)S(1)}, u32[]{:S(2)}, u32[]{:S(2)}) async-start(f32[8,8,256]{2,1,0:T(8,128)} %broadcast_in_dim.27), calls=%async_computation.4 | async-start | bytes 131072 | tf_op jit(solution)/shard_map/all_to_all | solution.py:24
  (4 other events, 8.1 us)

commit v3 on v2

--- a/solution.py
+++ b/solution.py
@@ -40,8 +40,16 @@
 def gathered_column(panel):
     c = lax.axis_index("c")
     zh = lax.axis_index("zh")
+    y = lax.axis_index("y")
     far = swap(panel, "zh", 1)
-    near = spread(panel, "y")
+    got = [panel]
+    for k in (1, 2, 3):
+        got.append(shift(panel, "y", -k))
+    near = []
+    for i in range(4):
+        away = (i - y) % 4
+        near.append(jnp.where(away < 2, jnp.where(away < 1, got[0], got[1]), jnp.where(away < 3, got[2], got[3])))
+    near = jnp.stack(near)
     far = spread(far, "y")
     near = ordered(near, swap(near, "c", 1), c, 1)
     far = ordered(far, swap(far, "c", 1), c, 1)
@@ -56,6 +64,14 @@
         rows = ordered(rows, other, zl & bit, 1 if bit != 4 else 0)
         rows = rows.reshape(-1, *rows.shape[2:])
     return rows
+
+
+def reduced_over_zl(t):
+    zl = lax.axis_index("zl")
+    for bit, axis in ((1, 2), (2, 1), (4, 0)):
+        mine = (zl // bit) % 2
+        t = pick(t, mine, axis) + swap(pick(t, 1 - mine, axis), "zl", bit)
+    return t
 
 
 def reduced_products(inverse_tiles, codes, column):
@@ -73,17 +89,11 @@
     down_a = shift(product(2, 1), "x", -1)
     up_b = shift(product(1, 1), "x", 1)
     down_b = shift(product(3, 0), "x", -1)
-    up_c = shift(product(1, 0) + up_a, "x", 1)
-    down_c = shift(product(3, 1) + down_a, "x", -1)
-    return product(0, 0) + down_b + up_c, product(0, 1) + up_b + down_c
-
-
-def reduced_over_zl(t):
-    zl = lax.axis_index("zl")
-    for bit, axis in ((1, 2), (2, 1), (4, 0)):
-        mine = (zl // bit) % 2
-        t = pick(t, mine, axis) + swap(pick(t, 1 - mine, axis), "zl", bit)
-    return t
+    rest = [product(*di) for di in ((1, 0), (3, 1), (0, 0), (0, 1))]
+    rest = lax.optimization_barrier(rest)
+    up_c = shift(rest[0] + up_a, "x", 1)
+    down_c = shift(rest[1] + down_a, "x", -1)
+    return rest[2] + down_b + up_c, rest[3] + up_b + down_c
 
 
 def local(inverse_tiles, tile_rows, panel, pivot_base):
@@ -94,20 +104,22 @@
     codes = tile_rows[:, 0]
     column = gathered_column(panel)
     u = gathered_over_zl(panel).reshape(8 * share, width).T
+    u = u.reshape(2, 4, 4, 4, 8, 8 * share).transpose(0, 3, 2, 1, 4, 5)
+    u = lax.optimization_barrier(u.reshape(2, block, 8 * share))
+    other_u = swap(u, "c", 1)
     t = jnp.concatenate(reduced_products(inverse_tiles, codes, column))
     trailing = reduced_over_zl(t.reshape(2, 2, 2, share, width))
 
-    def pivot(side):
-        parts = []
-        for j in range(2):
-            v = lax.dynamic_slice_in_dim(t[:, j * block : (j + 1) * block], side * half, half, 1)
-            parts.append(dot(u[j * block : (j + 1) * block], v))
-        return jnp.stack(parts)
+    def side(which):
+        first = which * half
+        cut = [lax.dynamic_slice_in_dim(t, first + j * block, half, 1) for j in range(2)]
+        return jnp.stack(cut)
 
-    away = swap(pivot(1 - c), "c", 1)
-    w = pivot(c) + away
-    w = w.reshape(8, 4, 4, 8, half).transpose(2, 1, 0, 3, 4)
-    w = w.reshape(16, 8, 8, half)
+    other_t = swap(side(1 - c), "c", 1)
+    mine = side(c)
+    own = lax.optimization_barrier([dot(u[j], mine[j]) for j in range(2)])
+    w = [own[j] + dot(other_u[j], other_t[j]) for j in range(2)]
+    w = jnp.concatenate([x.reshape(16, 4, 8, half) for x in w], axis=1)
     w = lax.all_to_all(w, ("y", "x"), 0, 0, tiled=True).sum(axis=0)
     w = jnp.concatenate([w, w])
     w = lax.all_to_all(w, ("zh", "zl"), 0, 0, tiled=True).sum(axis=0)

time: 196 us -> 186 us (0.949)
  starting transfers between devices: 118 us -> 110 us
  waiting for transfers between devices: 45.3 us -> 37.7 us
  other arithmetic: 10.8 us -> 14.8 us
    ppermute x10 -> x11, starting transfers between devices: 66.2 us -> 51.7 us  [swap(): return lax.ppermute(x, axis, [(i, i ^ bit) for i in range(n)])]
    ppermute x6 -> x9, waiting for transfers between devices: 20.2 us -> 10.4 us  [shift(): return lax.ppermute(x, axis, [(i, (i + by) % n) for i in range(n)])]
    ppermute x6 -> x9, starting transfers between devices: 18.8 us -> 27.7 us  [shift(): return lax.ppermute(x, axis, [(i, (i + by) % n) for i in range(n)])]
    all_to_all x3 -> x2, starting transfers between devices: 20.6 us -> 15.4 us  [spread(): return lax.all_to_all(copies, axes, 0, 0, tiled=True)]
    all_to_all x1, starting transfers between devices: 4.77 us -> 8.68 us  [local(): w = lax.all_to_all(w, ('zh', 'zl'), 0, 0, tiled=True).sum(axis=0)]
    ppermute x10 -> x11, waiting for transfers between devices: 5.52 us -> 9.17 us  [swap(): return lax.ppermute(x, axis, [(i, i ^ bit) for i in range(n)])]
    add x1 -> x4, other arithmetic: 1.36 us -> 4.27 us  [the longest x2 2.58 us: reduced_products(): return (rest[2] + down_b + up_c, rest[3] + up_b + down_c)]
    all_to_all x3 -> x2, waiting for transfers between devices: 4.2 us -> 4.2 us  [spread(): return lax.all_to_all(copies, axes, 0, 0, tiled=True)]
  transfers between devices with their start and end apart: 21 -> 24, of which waited for: 9 -> 10; matrix products, arithmetic and copies ran while one was open for 10% -> 15% of each run, Pallas kernels for 0% -> 0%
where the time goes in v3:
time: 186 us; the launch traced here: 183 us
  starting transfers between devices  110 us (59%)
  waiting for transfers between devices  37.7 us (20%)
  other arithmetic  14.8 us (8%)
  matrix products  9.78 us (5%)
  local copies, waits for them, and re-layouts  6.4 us (3%)
  between operations  4.16 us (2%)
    ppermute x11, starting transfers between devices, swap(): return lax.ppermute(x, axis, [(i, i ^ bit) for i in range(n)])  51.7 us
    ppermute x9, starting transfers between devices, shift(): return lax.ppermute(x, axis, [(i, (i + by) % n) for i in range(n)])  27.7 us
    all_to_all x2, starting transfers between devices, spread(): return lax.all_to_all(copies, axes, 0, 0, tiled=True)  15.4 us
    ppermute x9, waiting for transfers between devices, shift(): return lax.ppermute(x, axis, [(i, (i + by) % n) for i in range(n)])  10.4 us
    dot_general x12, matrix products, dot(): return jnp.dot(a, b, precision=HIGH, preferred_element_type=jnp.float32)  9.78 us
    all_to_all x1, waiting for transfers between devices, local(): w = lax.all_to_all(w, ('y', 'x'), 0, 0, tiled=True).sum(axis=0)  9.23 us
    ppermute x11, waiting for transfers between devices, swap(): return lax.ppermute(x, axis, [(i, i ^ bit) for i in range(n)])  9.17 us
    all_to_all x1, starting transfers between devices, local(): w = lax.all_to_all(w, ('zh', 'zl'), 0, 0, tiled=True).sum(axis=0)  8.68 us
  transfers between devices with their start and end apart: 24, of which 10 were waited for; matrix products, arithmetic and copies ran while one was open for 15% of the time, Pallas kernels for 0%

profile of v3, /device:TPU:1, one launch (start us, length us, event | category | flops | bytes accessed | tf_op | source)
XLA Modules:
  0.0 182.9 jit_solution(12484641819774161046)
XLA Ops:
  0.6 16.4 %collective-permute-start.4 = (f32[32,1024]{1,0:T(8,128)}, f32[32,1024]{1,0:T(8,128)S(1)}, u32[]{:S(2)}, u32[]{:S(2)}) collective-permute-start(f32[32,1024]{1,0:T(8,128)} %param.6), channel_id=1, source_target_pairs={{0,256},{256,0},{1,257},{257,1},{2,258},{258,2},{3,259},{259,3},{4... | collective-permute-start | bytes 393224 | tf_op jit(solution)/shard_map/ppermute | solution.py:19
  17.0 4.0 %collective-permute-start.15 = (f32[1,32,1024]{2,1,0:T(8,128)}, f32[1,32,1024]{2,1,0:T(8,128)S(1)}, u32[]{:S(2)}, u32[]{:S(2)}) collective-permute-start(f32[1,32,1024]{2,1,0:T(8,128)} %bitcast.158), channel_id=1, source_target_pairs={{0,16},{4,20},{8,24},{12,28},{16,0},{20,4},{24,8},{28,12},{1,17},{... | collective-permute-start | bytes 393224 | tf_op jit(solution)/shard_map/ppermute | solution.py:19
  21.1 4.6 %collective-permute-start = (f32[32,1024]{1,0:T(8,128)}, f32[32,1024]{1,0:T(8,128)S(1)}, u32[]{:S(2)}, u32[]{:S(2)}) collective-permute-start(f32[32,1024]{1,0:T(8,128)} %param.6), channel_id=1, source_target_pairs={{0,192},{64,0},{128,64},{192,128},{1,193},{65,1},{129,65},{193,129... | collective-permute-start | bytes 393224 | tf_op jit(solution)/shard_map/ppermute | solution.py:14
  25.7 2.3 %collective-permute-start.1 = (f32[32,1024]{1,0:T(8,128)}, f32[32,1024]{1,0:T(8,128)S(1)}, u32[]{:S(2)}, u32[]{:S(2)}) collective-permute-start(f32[32,1024]{1,0:T(8,128)} %param.6), channel_id=1, source_target_pairs={{0,128},{64,192},{128,0},{192,64},{1,129},{65,193},{129,1},{193,65... | collective-permute-start | bytes 393224 | tf_op jit(solution)/shard_map/ppermute | solution.py:14
  28.0 2.6 %collective-permute-start.2 = (f32[32,1024]{1,0:T(8,128)}, f32[32,1024]{1,0:T(8,128)}, u32[]{:S(2)}, u32[]{:S(2)}) collective-permute-start(f32[32,1024]{1,0:T(8,128)} %param.6), channel_id=1, source_target_pairs={{0,64},{64,128},{128,192},{192,0},{1,65},{65,129},{129,193},{193,1... | collective-permute-start | bytes 393224 | tf_op jit(solution)/shard_map/ppermute | solution.py:14
  35.5 3.6 %all-to-all-start = ((f32[4,32,1024]{2,1,0:T(8,128)}), f32[4,32,1024]{2,1,0:T(8,128)S(1)}, u32[]{:S(2)}, u32[]{:S(2)}) async-start(f32[4,32,1024]{2,1,0:T(8,128)} %broadcast_in_dim.21), calls=%async_computation | async-start | bytes 1048576 | tf_op jit(solution)/shard_map/all_to_all | solution.py:24
  39.2 2.2 %collective-permute-done.15 = f32[1,32,1024]{2,1,0:T(8,128)S(1)} collective-permute-done((f32[1,32,1024]{2,1,0:T(8,128)}, f32[1,32,1024]{2,1,0:T(8,128)S(1)}, u32[]{:S(2)}, u32[]{:S(2)}) %collective-permute-start.15) | collective-permute-done | bytes 131104 | tf_op jit(solution)/shard_map/ppermute | solution.py:19
  42.1 1.9 %collective-permute-start.16 = (f32[2,32,1024]{2,1,0:T(8,128)}, f32[2,32,1024]{2,1,0:T(8,128)}, u32[]{:S(2)}, u32[]{:S(2)}) collective-permute-start(f32[2,32,1024]{2,1,0:T(8,128)} %maximum_bitcast_fusion), channel_id=1, source_target_pairs={{0,8},{4,12},{8,0},{12,4},{16,24},{20,28},{24,16},{28,20},{1,9},{5... | collective-permute-start | bytes 786440 | tf_op jit(solution)/shard_map/ppermute | solution.py:19
  47.3 3.3 %collective-permute-start.3 = (f32[4,32,1024]{2,1,0:T(8,128)}, f32[4,32,1024]{2,1,0:T(8,128)}, u32[]{:S(2)}, u32[]{:S(2)}) collective-permute-start(f32[4,32,1024]{2,1,0:T(8,128)} %pad_maximum_fusion.6), channel_id=1, source_target_pairs={{0,32},{32,0},{1,33},{33,1},{2,34},{34,2},{3,35},{35,3},{4,36},{36... | collective-permute-start | bytes 1572872 | tf_op jit(solution)/shard_map/ppermute | solution.py:19
  52.0 1.9 %collective-permute-start.5 = (f32[4,32,1024]{2,1,0:T(8,128)S(1)}, f32[4,32,1024]{2,1,0:T(8,128)S(1)}, u32[]{:S(2)}, u32[]{:S(2)}) collective-permute-start(f32[4,32,1024]{2,1,0:T(8,128)S(1)} %all-to-all-done), channel_id=1, source_target_pairs={{0,32},{32,0},{1,33},{33,1},{2,34},{34,2},{3,35},{35,3},{4,36},{36... | collective-permute-start | bytes 1572872 | tf_op jit(solution)/shard_map/ppermute | solution.py:19
  54.0 3.4 %collective-permute-done.16 = f32[2,32,1024]{2,1,0:T(8,128)} collective-permute-done((f32[2,32,1024]{2,1,0:T(8,128)}, f32[2,32,1024]{2,1,0:T(8,128)}, u32[]{:S(2)}, u32[]{:S(2)}) %collective-permute-start.16) | collective-permute-done | bytes 262176 | tf_op jit(solution)/shard_map/ppermute | solution.py:19
  58.4 1.9 %collective-permute-start.17 = (f32[4,32,1024]{2,1,0:T(8,128)S(1)}, f32[4,32,1024]{2,1,0:T(8,128)S(1)}, u32[]{:S(2)}, u32[]{:S(2)}) collective-permute-start(f32[4,32,1024]{2,1,0:T(8,128)S(1)} %bitcast.147), channel_id=1, source_target_pairs={{0,4},{4,0},{8,12},{12,8},{16,20},{20,16},{24,28},{28,24},{1,5},{5... | collective-permute-start | bytes 1572872 | tf_op jit(solution)/shard_map/ppermute | solution.py:19
  63.6 3.3 %collective-permute-start.7 = (f32[128,1024]{1,0:T(8,128)S(1)}, f32[128,1024]{1,0:T(8,128)S(1)}, u32[]{:S(2)}, u32[]{:S(2)}) collective-permute-start(f32[128,1024]{1,0:T(8,128)S(1)} %fusion.23), channel_id=1, source_target_pairs={{0,1},{1,2},{2,3},{3,0},{4,5},{5,6},{6,7},{7,4},{8,9},{9,10},{10,1... | collective-permute-start | bytes 1572872 | tf_op jit(solution)/shard_map/ppermute | solution.py:14
  71.3 3.4 %collective-permute-start.10 = (f32[128,1024]{1,0:T(8,128)S(1)}, f32[128,1024]{1,0:T(8,128)S(1)}, u32[]{:S(2)}, u32[]{:S(2)}) collective-permute-start(f32[128,1024]{1,0:T(8,128)S(1)} %fusion.25), channel_id=1, source_target_pairs={{0,3},{1,0},{2,1},{3,2},{4,7},{5,4},{6,5},{7,6},{8,11},{9,8},{10,9... | collective-permute-start | bytes 1572872 | tf_op jit(solution)/shard_map/ppermute | solution.py:14
  76.4 3.2 %collective-permute-start.6 = (f32[128,1024]{1,0:T(8,128)}, f32[128,1024]{1,0:T(8,128)}, u32[]{:S(2)}, u32[]{:S(2)}) collective-permute-start(f32[128,1024]{1,0:T(8,128)} %fusion.22), channel_id=1, source_target_pairs={{0,3},{1,0},{2,1},{3,2},{4,7},{5,4},{6,5},{7,6},{8,11},{9,8},{10,9... | collective-permute-start | bytes 1572872 | tf_op jit(solution)/shard_map/ppermute | solution.py:14
  80.7 1.9 %collective-permute-start.8 = (f32[128,1024]{1,0:T(8,128)}, f32[128,1024]{1,0:T(8,128)}, u32[]{:S(2)}, u32[]{:S(2)}) collective-permute-start(f32[128,1024]{1,0:T(8,128)} %add.168), channel_id=1, source_target_pairs={{0,1},{1,2},{2,3},{3,0},{4,5},{5,6},{6,7},{7,4},{8,9},{9,10},{10,1... | collective-permute-start | bytes 1572872 | tf_op jit(solution)/shard_map/ppermute | solution.py:14
  82.6 1.6 fusion.24
  84.3 3.1 %collective-permute-start.9 = (f32[128,1024]{1,0:T(8,128)}, f32[128,1024]{1,0:T(8,128)}, u32[]{:S(2)}, u32[]{:S(2)}) collective-permute-start(f32[128,1024]{1,0:T(8,128)} %fusion.24), channel_id=1, source_target_pairs={{0,1},{1,2},{2,3},{3,0},{4,5},{5,6},{6,7},{7,4},{8,9},{9,10},{10,1... | collective-permute-start | bytes 1572872 | tf_op jit(solution)/shard_map/ppermute | solution.py:14
  88.2 3.4 %collective-permute-start.11 = (f32[128,1024]{1,0:T(8,128)}, f32[128,1024]{1,0:T(8,128)}, u32[]{:S(2)}, u32[]{:S(2)}) collective-permute-start(f32[128,1024]{1,0:T(8,128)} %add.171), channel_id=1, source_target_pairs={{0,3},{1,0},{2,1},{3,2},{4,7},{5,4},{6,5},{7,6},{8,11},{9,8},{10,9... | collective-permute-start | bytes 1572872 | tf_op jit(solution)/shard_map/ppermute | solution.py:14
  92.4 4.8 %collective-permute-start.18 = (f32[2,512,256]{2,1,0:T(8,128)S(1)}, f32[2,512,256]{2,1,0:T(8,128)S(1)}, u32[]{:S(2)}, u32[]{:S(2)}) collective-permute-start(f32[2,512,256]{2,1,0:T(8,128)S(1)} %bitcast.139), channel_id=1, source_target_pairs={{0,32},{32,0},{1,33},{33,1},{2,34},{34,2},{3,35},{35,3},{4,36},{36... | collective-permute-start | bytes 3145736 | tf_op jit(solution)/shard_map/ppermute | solution.py:19
  98.6 8.9 %collective-permute-done.9 = f32[128,1024]{1,0:T(8,128)} collective-permute-done((f32[128,1024]{1,0:T(8,128)}, f32[128,1024]{1,0:T(8,128)}, u32[]{:S(2)}, u32[]{:S(2)}) %collective-permute-start.9) | collective-permute-done | bytes 524320 | tf_op jit(solution)/shard_map/ppermute | solution.py:14
  109.9 3.5 %collective-permute-start.19 = (f32[2,256,256]{2,1,0:T(8,128)S(1)}, f32[2,256,256]{2,1,0:T(8,128)S(1)}, u32[]{:S(2)}, u32[]{:S(2)}) collective-permute-start(f32[2,256,256]{2,1,0:T(8,128)S(1)} %pad_maximum_fusion.8), channel_id=1, source_target_pairs={{0,32},{32,0},{1,33},{33,1},{2,34},{34,2},{3,35},{35,3},{4,36},{36... | collective-permute-start | bytes 1572872 | tf_op jit(solution)/shard_map/ppermute | solution.py:19
  115.2 3.3 %collective-permute-start.12 = (f32[2,2,32,1024]{3,2,1,0:T(8,128)}, f32[2,2,32,1024]{3,2,1,0:T(8,128)S(1)}, u32[]{:S(2)}, u32[]{:S(2)}) collective-permute-start(f32[2,2,32,1024]{3,2,1,0:T(8,128)} %dynamic-slice_bitcast_fusion), channel_id=1, source_target_pairs={{0,4},{4,0},{8,12},{12,8},{16,20},{20,16},{24,28},{28,24},{1,5},{5... | collective-permute-start | bytes 1572872 | tf_op jit(solution)/shard_map/ppermute | solution.py:19
  120.4 6.7 %all-to-all-start.1 = ((f32[16,8,8,256]{3,2,1,0:T(8,128)}), f32[16,8,8,256]{3,2,1,0:T(8,128)S(1)}, u32[]{:S(2)}, u32[]{:S(2)}) async-start(f32[16,8,8,256]{3,2,1,0:T(8,128)} %pad_maximum_fusion.5), calls=%async_computation.1 | async-start | bytes 2097152 | tf_op jit(solution)/shard_map/all_to_all | solution.py:123
  127.2 3.6 %collective-permute-done.12 = f32[2,2,32,1024]{3,2,1,0:T(8,128)S(1)} collective-permute-done((f32[2,2,32,1024]{3,2,1,0:T(8,128)}, f32[2,2,32,1024]{3,2,1,0:T(8,128)S(1)}, u32[]{:S(2)}, u32[]{:S(2)}) %collective-permute-start.12) | collective-permute-done | bytes 524320 | tf_op jit(solution)/shard_map/ppermute | solution.py:19
  130.9 3.4 %collective-permute-start.13 = (f32[2,32,1024]{2,1,0:T(8,128)S(1)}, f32[2,32,1024]{2,1,0:T(8,128)S(1)}, u32[]{:S(2)}, u32[]{:S(2)}) collective-permute-start(f32[2,32,1024]{2,1,0:T(8,128)S(1)} %dynamic-slice_bitcast_fusion.1), channel_id=1, source_target_pairs={{0,8},{4,12},{8,0},{12,4},{16,24},{20,28},{24,16},{28,20},{1,9},{5... | collective-permute-start | bytes 786440 | tf_op jit(solution)/shard_map/ppermute | solution.py:19
  134.3 9.2 %all-to-all-done.1 = f32[16,8,8,256]{3,2,1,0:T(8,128)S(1)} async-done(((f32[16,8,8,256]{3,2,1,0:T(8,128)}), f32[16,8,8,256]{3,2,1,0:T(8,128)S(1)}, u32[]{:S(2)}, u32[]{:S(2)}) %all-to-all-start.1) | async-done | bytes 1048608 | tf_op jit(solution)/shard_map/all_to_all | solution.py:123
  144.3 8.7 %all-to-all-start.2 = ((f32[16,8,256]{2,1,0:T(8,128)}), f32[16,8,256]{2,1,0:T(8,128)S(1)}, u32[]{:S(2)}, u32[]{:S(2)}) async-start(f32[16,8,256]{2,1,0:T(8,128)} %pad_maximum_fusion.9), calls=%async_computation.2 | async-start | bytes 262144 | tf_op jit(solution)/shard_map/all_to_all | solution.py:125
  153.1 7.1 %collective-permute-start.14 = (f32[32,1024]{1,0:T(8,128)S(1)}, f32[32,1024]{1,0:T(8,128)S(1)}, u32[]{:S(2)}, u32[]{:S(2)}) collective-permute-start(f32[32,1024]{1,0:T(8,128)S(1)} %dynamic-slice_bitcast_fusion.2), channel_id=1, source_target_pairs={{0,16},{4,20},{8,24},{12,28},{16,0},{20,4},{24,8},{28,12},{1,17},{... | collective-permute-start | bytes 393224 | tf_op jit(solution)/shard_map/ppermute | solution.py:19
  160.3 4.7 %all-to-all-done.2 = f32[16,8,256]{2,1,0:T(8,128)S(1)} async-done(((f32[16,8,256]{2,1,0:T(8,128)}), f32[16,8,256]{2,1,0:T(8,128)S(1)}, u32[]{:S(2)}, u32[]{:S(2)}) %all-to-all-start.2) | async-done | bytes 131104 | tf_op jit(solution)/shard_map/all_to_all | solution.py:125
  165.6 11.8 %all-to-all-start.3 = ((f32[8,8,256]{2,1,0:T(8,128)}), f32[8,8,256]{2,1,0:T(8,128)S(1)}, u32[]{:S(2)}, u32[]{:S(2)}) async-start(f32[8,8,256]{2,1,0:T(8,128)} %broadcast_in_dim.23), calls=%async_computation.3 | async-start | bytes 131072 | tf_op jit(solution)/shard_map/all_to_all | solution.py:24
  178.1 4.2 %all-to-all-done.3 = f32[8,8,256]{2,1,0:T(8,128)S(1)} async-done(((f32[8,8,256]{2,1,0:T(8,128)}), f32[8,8,256]{2,1,0:T(8,128)S(1)}, u32[]{:S(2)}, u32[]{:S(2)}) %all-to-all-start.3) | async-done | bytes 65568 | tf_op jit(solution)/shard_map/all_to_all | solution.py:24
  (91 shorter events, 30.8 us)
Async XLA Ops:
  0.6 40.7 %copy-start.9 = (f32[32,1024]{1,0:T(8,128)S(1)}, f32[32,1024]{1,0:T(8,128)}, u32[]{:S(2)}) copy-start(f32[32,1024]{1,0:T(8,128)} %param.6) | copy-start | bytes 393220
  0.6 34.0 %collective-permute-start.4 = (f32[32,1024]{1,0:T(8,128)}, f32[32,1024]{1,0:T(8,128)S(1)}, u32[]{:S(2)}, u32[]{:S(2)}) collective-permute-start(f32[32,1024]{1,0:T(8,128)} %param.6), channel_id=1, source_target_pairs={{0,256},{256,0},{1,257},{257,1},{2,258},{258,2},{3,259},{259,3},{4... | collective-permute-start | bytes 393224 | tf_op jit(solution)/shard_map/ppermute | solution.py:19
  17.0 24.3 %collective-permute-start.15 = (f32[1,32,1024]{2,1,0:T(8,128)}, f32[1,32,1024]{2,1,0:T(8,128)S(1)}, u32[]{:S(2)}, u32[]{:S(2)}) collective-permute-start(f32[1,32,1024]{2,1,0:T(8,128)} %bitcast.158), channel_id=1, source_target_pairs={{0,16},{4,20},{8,24},{12,28},{16,0},{20,4},{24,8},{28,12},{1,17},{... | collective-permute-start | bytes 393224 | tf_op jit(solution)/shard_map/ppermute | solution.py:19
  21.1 23.0 %collective-permute-start = (f32[32,1024]{1,0:T(8,128)}, f32[32,1024]{1,0:T(8,128)S(1)}, u32[]{:S(2)}, u32[]{:S(2)}) collective-permute-start(f32[32,1024]{1,0:T(8,128)} %param.6), channel_id=1, source_target_pairs={{0,192},{64,0},{128,64},{192,128},{1,193},{65,1},{129,65},{193,129... | collective-permute-start | bytes 393224 | tf_op jit(solution)/shard_map/ppermute | solution.py:14
  25.7 18.3 %collective-permute-start.1 = (f32[32,1024]{1,0:T(8,128)}, f32[32,1024]{1,0:T(8,128)S(1)}, u32[]{:S(2)}, u32[]{:S(2)}) collective-permute-start(f32[32,1024]{1,0:T(8,128)} %param.6), channel_id=1, source_target_pairs={{0,128},{64,192},{128,0},{192,64},{1,129},{65,193},{129,1},{193,65... | collective-permute-start | bytes 393224 | tf_op jit(solution)/shard_map/ppermute | solution.py:14
  28.0 17.4 %collective-permute-start.2 = (f32[32,1024]{1,0:T(8,128)}, f32[32,1024]{1,0:T(8,128)}, u32[]{:S(2)}, u32[]{:S(2)}) collective-permute-start(f32[32,1024]{1,0:T(8,128)} %param.6), channel_id=1, source_target_pairs={{0,64},{64,128},{128,192},{192,0},{1,65},{65,129},{129,193},{193,1... | collective-permute-start | bytes 393224 | tf_op jit(solution)/shard_map/ppermute | solution.py:14
  35.5 15.1 %copy-start = (f32[2,512,512]{2,1,0:T(8,128)S(1)}, f32[2,512,512]{2,1,0:T(8,128)}, u32[]{:S(2)}) copy-start(f32[2,512,512]{2,1,0:T(8,128)} %param.4) | copy-start | bytes 6291460
  35.5 16.5 %all-to-all-start = ((f32[4,32,1024]{2,1,0:T(8,128)}), f32[4,32,1024]{2,1,0:T(8,128)S(1)}, u32[]{:S(2)}, u32[]{:S(2)}) async-start(f32[4,32,1024]{2,1,0:T(8,128)} %broadcast_in_dim.21), calls=%async_computation | async-start | bytes 1048576 | tf_op jit(solution)/shard_map/all_to_all | solution.py:24
  42.1 15.2 %collective-permute-start.16 = (f32[2,32,1024]{2,1,0:T(8,128)}, f32[2,32,1024]{2,1,0:T(8,128)}, u32[]{:S(2)}, u32[]{:S(2)}) collective-permute-start(f32[2,32,1024]{2,1,0:T(8,128)} %maximum_bitcast_fusion), channel_id=1, source_target_pairs={{0,8},{4,12},{8,0},{12,4},{16,24},{20,28},{24,16},{28,20},{1,9},{5... | collective-permute-start | bytes 786440 | tf_op jit(solution)/shard_map/ppermute | solution.py:19
  47.3 13.0 %collective-permute-start.3 = (f32[4,32,1024]{2,1,0:T(8,128)}, f32[4,32,1024]{2,1,0:T(8,128)}, u32[]{:S(2)}, u32[]{:S(2)}) collective-permute-start(f32[4,32,1024]{2,1,0:T(8,128)} %pad_maximum_fusion.6), channel_id=1, source_target_pairs={{0,32},{32,0},{1,33},{33,1},{2,34},{34,2},{3,35},{35,3},{4,36},{36... | collective-permute-start | bytes 1572872 | tf_op jit(solution)/shard_map/ppermute | solution.py:19
  52.0 9.4 %collective-permute-start.5 = (f32[4,32,1024]{2,1,0:T(8,128)S(1)}, f32[4,32,1024]{2,1,0:T(8,128)S(1)}, u32[]{:S(2)}, u32[]{:S(2)}) collective-permute-start(f32[4,32,1024]{2,1,0:T(8,128)S(1)} %all-to-all-done), channel_id=1, source_target_pairs={{0,32},{32,0},{1,33},{33,1},{2,34},{34,2},{3,35},{35,3},{4,36},{36... | collective-permute-start | bytes 1572872 | tf_op jit(solution)/shard_map/ppermute | solution.py:19
  58.4 33.3 %collective-permute-start.17 = (f32[4,32,1024]{2,1,0:T(8,128)S(1)}, f32[4,32,1024]{2,1,0:T(8,128)S(1)}, u32[]{:S(2)}, u32[]{:S(2)}) collective-permute-start(f32[4,32,1024]{2,1,0:T(8,128)S(1)} %bitcast.147), channel_id=1, source_target_pairs={{0,4},{4,0},{8,12},{12,8},{16,20},{20,16},{24,28},{28,24},{1,5},{5... | collective-permute-start | bytes 1572872 | tf_op jit(solution)/shard_map/ppermute | solution.py:19
  62.1 4.8 %copy-start.7 = (f32[1,4,1,32,512]{4,3,2,1,0:T(8,128)S(1)}, f32[1,4,1,32,512]{4,3,2,1,0:T(8,128)}, u32[]{:S(2)}) copy-start(f32[1,4,1,32,512]{4,3,2,1,0:T(8,128)} %get-tuple-element.20) | copy-start | bytes 786436
  63.6 4.1 %copy-start.6 = (f32[1,4,1,32,512]{4,3,2,1,0:T(8,128)S(1)}, f32[1,4,1,32,512]{4,3,2,1,0:T(8,128)}, u32[]{:S(2)}) copy-start(f32[1,4,1,32,512]{4,3,2,1,0:T(8,128)} %get-tuple-element.16) | copy-start | bytes 786436
  63.6 16.2 %collective-permute-start.7 = (f32[128,1024]{1,0:T(8,128)S(1)}, f32[128,1024]{1,0:T(8,128)S(1)}, u32[]{:S(2)}, u32[]{:S(2)}) collective-permute-start(f32[128,1024]{1,0:T(8,128)S(1)} %fusion.23), channel_id=1, source_target_pairs={{0,1},{1,2},{2,3},{3,0},{4,5},{5,6},{6,7},{7,4},{8,9},{9,10},{10,1... | collective-permute-start | bytes 1572872 | tf_op jit(solution)/shard_map/ppermute | solution.py:14
  68.6 1.0 copy-start.4
  70.4 4.3 %copy-start.2 = (f32[1,4,1,32,512]{4,3,2,1,0:T(8,128)S(1)}, f32[1,4,1,32,512]{4,3,2,1,0:T(8,128)}, u32[]{:S(2)}) copy-start(f32[1,4,1,32,512]{4,3,2,1,0:T(8,128)} %get-tuple-element.14) | copy-start | bytes 786436
  71.3 16.1 %collective-permute-start.10 = (f32[128,1024]{1,0:T(8,128)S(1)}, f32[128,1024]{1,0:T(8,128)S(1)}, u32[]{:S(2)}, u32[]{:S(2)}) collective-permute-start(f32[128,1024]{1,0:T(8,128)S(1)} %fusion.25), channel_id=1, source_target_pairs={{0,3},{1,0},{2,1},{3,2},{4,7},{5,4},{6,5},{7,6},{8,11},{9,8},{10,9... | collective-permute-start | bytes 1572872 | tf_op jit(solution)/shard_map/ppermute | solution.py:14
  74.7 7.9 %copy-start.1 = (f32[1,4,1,32,512]{4,3,2,1,0:T(8,128)S(1)}, f32[1,4,1,32,512]{4,3,2,1,0:T(8,128)}, u32[]{:S(2)}) copy-start(f32[1,4,1,32,512]{4,3,2,1,0:T(8,128)} %get-tuple-element.19) | copy-start | bytes 786436
  76.4 20.9 %collective-permute-start.6 = (f32[128,1024]{1,0:T(8,128)}, f32[128,1024]{1,0:T(8,128)}, u32[]{:S(2)}, u32[]{:S(2)}) collective-permute-start(f32[128,1024]{1,0:T(8,128)} %fusion.22), channel_id=1, source_target_pairs={{0,3},{1,0},{2,1},{3,2},{4,7},{5,4},{6,5},{7,6},{8,11},{9,8},{10,9... | collective-permute-start | bytes 1572872 | tf_op jit(solution)/shard_map/ppermute | solution.py:14
  80.7 16.6 %collective-permute-start.8 = (f32[128,1024]{1,0:T(8,128)}, f32[128,1024]{1,0:T(8,128)}, u32[]{:S(2)}, u32[]{:S(2)}) collective-permute-start(f32[128,1024]{1,0:T(8,128)} %add.168), channel_id=1, source_target_pairs={{0,1},{1,2},{2,3},{3,0},{4,5},{5,6},{6,7},{7,4},{8,9},{9,10},{10,1... | collective-permute-start | bytes 1572872 | tf_op jit(solution)/shard_map/ppermute | solution.py:14
  84.3 23.2 %collective-permute-start.9 = (f32[128,1024]{1,0:T(8,128)}, f32[128,1024]{1,0:T(8,128)}, u32[]{:S(2)}, u32[]{:S(2)}) collective-permute-start(f32[128,1024]{1,0:T(8,128)} %fusion.24), channel_id=1, source_target_pairs={{0,1},{1,2},{2,3},{3,0},{4,5},{5,6},{6,7},{7,4},{8,9},{9,10},{10,1... | collective-permute-start | bytes 1572872 | tf_op jit(solution)/shard_map/ppermute | solution.py:14
  88.2 20.3 %collective-permute-start.11 = (f32[128,1024]{1,0:T(8,128)}, f32[128,1024]{1,0:T(8,128)}, u32[]{:S(2)}, u32[]{:S(2)}) collective-permute-start(f32[128,1024]{1,0:T(8,128)} %add.171), channel_id=1, source_target_pairs={{0,3},{1,0},{2,1},{3,2},{4,7},{5,4},{6,5},{7,6},{8,11},{9,8},{10,9... | collective-permute-start | bytes 1572872 | tf_op jit(solution)/shard_map/ppermute | solution.py:14
  92.4 26.1 %collective-permute-start.18 = (f32[2,512,256]{2,1,0:T(8,128)S(1)}, f32[2,512,256]{2,1,0:T(8,128)S(1)}, u32[]{:S(2)}, u32[]{:S(2)}) collective-permute-start(f32[2,512,256]{2,1,0:T(8,128)S(1)} %bitcast.139), channel_id=1, source_target_pairs={{0,32},{32,0},{1,33},{33,1},{2,34},{34,2},{3,35},{35,3},{4,36},{36... | collective-permute-start | bytes 3145736 | tf_op jit(solution)/shard_map/ppermute | solution.py:19
  109.9 8.7 %collective-permute-start.19 = (f32[2,256,256]{2,1,0:T(8,128)S(1)}, f32[2,256,256]{2,1,0:T(8,128)S(1)}, u32[]{:S(2)}, u32[]{:S(2)}) collective-permute-start(f32[2,256,256]{2,1,0:T(8,128)S(1)} %pad_maximum_fusion.8), channel_id=1, source_target_pairs={{0,32},{32,0},{1,33},{33,1},{2,34},{34,2},{3,35},{35,3},{4,36},{36... | collective-permute-start | bytes 1572872 | tf_op jit(solution)/shard_map/ppermute | solution.py:19
  115.2 15.6 %collective-permute-start.12 = (f32[2,2,32,1024]{3,2,1,0:T(8,128)}, f32[2,2,32,1024]{3,2,1,0:T(8,128)S(1)}, u32[]{:S(2)}, u32[]{:S(2)}) collective-permute-start(f32[2,2,32,1024]{3,2,1,0:T(8,128)} %dynamic-slice_bitcast_fusion), channel_id=1, source_target_pairs={{0,4},{4,0},{8,12},{12,8},{16,20},{20,16},{24,28},{28,24},{1,5},{5... | collective-permute-start | bytes 1572872 | tf_op jit(solution)/shard_map/ppermute | solution.py:19
  120.4 23.1 %all-to-all-start.1 = ((f32[16,8,8,256]{3,2,1,0:T(8,128)}), f32[16,8,8,256]{3,2,1,0:T(8,128)S(1)}, u32[]{:S(2)}, u32[]{:S(2)}) async-start(f32[16,8,8,256]{3,2,1,0:T(8,128)} %pad_maximum_fusion.5), calls=%async_computation.1 | async-start | bytes 2097152 | tf_op jit(solution)/shard_map/all_to_all | solution.py:123
  130.8 51.5 %copy-start.12 = (f32[32,512]{1,0:T(8,128)S(1)}, f32[32,512]{1,0:T(8,128)}, u32[]{:S(2)}) copy-start(f32[32,512]{1,0:T(8,128)} %param.7) | copy-start | bytes 196612
  130.9 22.1 %collective-permute-start.13 = (f32[2,32,1024]{2,1,0:T(8,128)S(1)}, f32[2,32,1024]{2,1,0:T(8,128)S(1)}, u32[]{:S(2)}, u32[]{:S(2)}) collective-permute-start(f32[2,32,1024]{2,1,0:T(8,128)S(1)} %dynamic-slice_bitcast_fusion.1), channel_id=1, source_target_pairs={{0,8},{4,12},{8,0},{12,4},{16,24},{20,28},{24,16},{28,20},{1,9},{5... | collective-permute-start | bytes 786440 | tf_op jit(solution)/shard_map/ppermute | solution.py:19
  144.3 20.7 %all-to-all-start.2 = ((f32[16,8,256]{2,1,0:T(8,128)}), f32[16,8,256]{2,1,0:T(8,128)S(1)}, u32[]{:S(2)}, u32[]{:S(2)}) async-start(f32[16,8,256]{2,1,0:T(8,128)} %pad_maximum_fusion.9), calls=%async_computation.2 | async-start | bytes 262144 | tf_op jit(solution)/shard_map/all_to_all | solution.py:125
  153.1 24.3 %collective-permute-start.14 = (f32[32,1024]{1,0:T(8,128)S(1)}, f32[32,1024]{1,0:T(8,128)S(1)}, u32[]{:S(2)}, u32[]{:S(2)}) collective-permute-start(f32[32,1024]{1,0:T(8,128)S(1)} %dynamic-slice_bitcast_fusion.2), channel_id=1, source_target_pairs={{0,16},{4,20},{8,24},{12,28},{16,0},{20,4},{24,8},{28,12},{1,17},{... | collective-permute-start | bytes 393224 | tf_op jit(solution)/shard_map/ppermute | solution.py:19
  165.6 16.7 %all-to-all-start.3 = ((f32[8,8,256]{2,1,0:T(8,128)}), f32[8,8,256]{2,1,0:T(8,128)S(1)}, u32[]{:S(2)}, u32[]{:S(2)}) async-start(f32[8,8,256]{2,1,0:T(8,128)} %broadcast_in_dim.23), calls=%async_computation.3 | async-start | bytes 131072 | tf_op jit(solution)/shard_map/all_to_all | solution.py:24
  (5 other events, 4.2 us)

commit v4 on v3

--- a/solution.py
+++ b/solution.py
@@ -66,12 +66,20 @@
     return rows
 
 
-def reduced_over_zl(t):
+def reduced_over_zl(halves):
     zl = lax.axis_index("zl")
-    for bit, axis in ((1, 2), (2, 1), (4, 0)):
-        mine = (zl // bit) % 2
-        t = pick(t, mine, axis) + swap(pick(t, 1 - mine, axis), "zl", bit)
-    return t
+    low, mid, high = zl % 2, (zl // 2) % 2, zl // 4
+    rows = []
+    for t in halves:
+        t = t.reshape(2, 2, -1, t.shape[-1])
+        rows.append(pick(t, low, 1) + swap(pick(t, 1 - low, 1), "zl", 1))
+    kept = [pick(t, mid, 0) for t in rows]
+    sent = jnp.stack([pick(t, 1 - mid, 0) for t in rows])
+    sent = swap(sent, "zl", 2)
+    rows = [kept[i] + sent[i] for i in range(2)]
+    first = high == 0
+    sent = swap(jnp.where(first, rows[1], rows[0]), "zl", 4)
+    return jnp.where(first, rows[0], rows[1]) + sent
 
 
 def reduced_products(inverse_tiles, codes, column):
@@ -93,7 +101,8 @@
     rest = lax.optimization_barrier(rest)
     up_c = shift(rest[0] + up_a, "x", 1)
     down_c = shift(rest[1] + down_a, "x", -1)
-    return rest[2] + down_b + up_c, rest[3] + up_b + down_c
+    first = rest[2] + down_b + up_c
+    return first, rest[3] + up_b + down_c
 
 
 def local(inverse_tiles, tile_rows, panel, pivot_base):
@@ -107,18 +116,25 @@
     u = u.reshape(2, 4, 4, 4, 8, 8 * share).transpose(0, 3, 2, 1, 4, 5)
     u = lax.optimization_barrier(u.reshape(2, block, 8 * share))
     other_u = swap(u, "c", 1)
-    t = jnp.concatenate(reduced_products(inverse_tiles, codes, column))
-    trailing = reduced_over_zl(t.reshape(2, 2, 2, share, width))
+    halves = reduced_products(inverse_tiles, codes, column)
+    trailing = reduced_over_zl(halves)
 
-    def side(which):
+    def side(t, which):
         first = which * half
         cut = [lax.dynamic_slice_in_dim(t, first + j * block, half, 1) for j in range(2)]
         return jnp.stack(cut)
 
-    other_t = swap(side(1 - c), "c", 1)
-    mine = side(c)
-    own = lax.optimization_barrier([dot(u[j], mine[j]) for j in range(2)])
-    w = [own[j] + dot(other_u[j], other_t[j]) for j in range(2)]
+    mine, other = [], []
+    for t in halves:
+        other.append(swap(side(t, 1 - c), "c", 1))
+        mine.append(side(t, c))
+    k = 4 * share
+    own = [dot(u[j, :, :k], mine[0][j]) for j in range(2)]
+    own = lax.optimization_barrier(own)
+    own = [own[j] + dot(u[j, :, k:], mine[1][j]) for j in range(2)]
+    own = lax.optimization_barrier(own)
+    other = [jnp.concatenate([other[0][j], other[1][j]]) for j in range(2)]
+    w = [own[j] + dot(other_u[j], other[j]) for j in range(2)]
     w = jnp.concatenate([x.reshape(16, 4, 8, half) for x in w], axis=1)
     w = lax.all_to_all(w, ("y", "x"), 0, 0, tiled=True).sum(axis=0)
     w = jnp.concatenate([w, w])

time: 186 us -> 191 us (1.027)
  waiting for transfers between devices: 37.7 us -> 42.2 us
  starting transfers between devices: 110 us -> 112 us
  local copies, waits for them, and re-layouts: 6.4 us -> 4.44 us
    ppermute x11 -> x13, waiting for transfers between devices: 9.17 us -> 15.1 us  [swap(): return lax.ppermute(x, axis, [(i, i ^ bit) for i in range(n)])]
    all_to_all x1, waiting for transfers between devices: 9.23 us -> 5.14 us  [local(): w = lax.all_to_all(w, ('y', 'x'), 0, 0, tiled=True).sum(axis=0)]
    ppermute x9, waiting for transfers between devices: 10.4 us -> 13 us  [shift(): return lax.ppermute(x, axis, [(i, (i + by) % n) for i in range(n)])]
    ppermute x11 -> x13, starting transfers between devices: 51.7 us -> 52.6 us  [swap(): return lax.ppermute(x, axis, [(i, i ^ bit) for i in range(n)])]
    dot_general x12 -> x14, matrix products: 9.78 us -> 10.4 us  [dot(): return jnp.dot(a, b, precision=HIGH, preferred_element_type=jnp.float32)]
  transfers between devices with their start and end apart: 24 -> 26, of which waited for: 10 -> 10; matrix products, arithmetic and copies ran while one was open for 15% -> 15% of each run, Pallas kernels for 0% -> 0%
where the time goes in v4:
time: 191 us; the launch traced here: 188 us
  starting transfers between devices  112 us (59%)
  waiting for transfers between devices  42.2 us (22%)
  other arithmetic  14.8 us (8%)
  matrix products  10.4 us (5%)
  local copies, waits for them, and re-layouts  4.44 us (2%)
  between operations  4.23 us (2%)
    ppermute x13, starting transfers between devices, swap(): return lax.ppermute(x, axis, [(i, i ^ bit) for i in range(n)])  52.6 us
    ppermute x9, starting transfers between devices, shift(): return lax.ppermute(x, axis, [(i, (i + by) % n) for i in range(n)])  29 us
    all_to_all x2, starting transfers between devices, spread(): return lax.all_to_all(copies, axes, 0, 0, tiled=True)  15.4 us
    ppermute x13, waiting for transfers between devices, swap(): return lax.ppermute(x, axis, [(i, i ^ bit) for i in range(n)])  15.1 us
    ppermute x9, waiting for transfers between devices, shift(): return lax.ppermute(x, axis, [(i, (i + by) % n) for i in range(n)])  13 us
    dot_general x14, matrix products, dot(): return jnp.dot(a, b, precision=HIGH, preferred_element_type=jnp.float32)  10.4 us
    all_to_all x1, starting transfers between devices, local(): w = lax.all_to_all(w, ('y', 'x'), 0, 0, tiled=True).sum(axis=0)  7.41 us
    all_to_all x1, starting transfers between devices, local(): w = lax.all_to_all(w, ('zh', 'zl'), 0, 0, tiled=True).sum(axis=0)  7.41 us
  transfers between devices with their start and end apart: 26, of which 10 were waited for; matrix products, arithmetic and copies ran while one was open for 15% of the time, Pallas kernels for 0%

profile of v4, /device:TPU:1, one launch (start us, length us, event | category | flops | bytes accessed | tf_op | source)
XLA Modules:
  0.0 188.0 jit_solution(9244917407575427618)
XLA Ops:
  0.6 16.4 %collective-permute-start.4 = (f32[32,1024]{1,0:T(8,128)}, f32[32,1024]{1,0:T(8,128)S(1)}, u32[]{:S(2)}, u32[]{:S(2)}) collective-permute-start(f32[32,1024]{1,0:T(8,128)} %param.6), channel_id=1, source_target_pairs={{0,256},{256,0},{1,257},{257,1},{2,258},{258,2},{3,259},{259,3},{4... | collective-permute-start | bytes 393224 | tf_op jit(solution)/shard_map/ppermute | solution.py:19
  17.0 4.0 %collective-permute-start.16 = (f32[1,32,1024]{2,1,0:T(8,128)}, f32[1,32,1024]{2,1,0:T(8,128)S(1)}, u32[]{:S(2)}, u32[]{:S(2)}) collective-permute-start(f32[1,32,1024]{2,1,0:T(8,128)} %bitcast.175), channel_id=1, source_target_pairs={{0,16},{4,20},{8,24},{12,28},{16,0},{20,4},{24,8},{28,12},{1,17},{... | collective-permute-start | bytes 393224 | tf_op jit(solution)/shard_map/ppermute | solution.py:19
  21.1 4.6 %collective-permute-start = (f32[32,1024]{1,0:T(8,128)}, f32[32,1024]{1,0:T(8,128)}, u32[]{:S(2)}, u32[]{:S(2)}) collective-permute-start(f32[32,1024]{1,0:T(8,128)} %param.6), channel_id=1, source_target_pairs={{0,192},{64,0},{128,64},{192,128},{1,193},{65,1},{129,65},{193,129... | collective-permute-start | bytes 393224 | tf_op jit(solution)/shard_map/ppermute | solution.py:14
  25.7 2.3 %collective-permute-start.1 = (f32[32,1024]{1,0:T(8,128)}, f32[32,1024]{1,0:T(8,128)}, u32[]{:S(2)}, u32[]{:S(2)}) collective-permute-start(f32[32,1024]{1,0:T(8,128)} %param.6), channel_id=1, source_target_pairs={{0,128},{64,192},{128,0},{192,64},{1,129},{65,193},{129,1},{193,65... | collective-permute-start | bytes 393224 | tf_op jit(solution)/shard_map/ppermute | solution.py:14
  28.0 2.6 %collective-permute-start.2 = (f32[32,1024]{1,0:T(8,128)}, f32[32,1024]{1,0:T(8,128)}, u32[]{:S(2)}, u32[]{:S(2)}) collective-permute-start(f32[32,1024]{1,0:T(8,128)} %param.6), channel_id=1, source_target_pairs={{0,64},{64,128},{128,192},{192,0},{1,65},{65,129},{129,193},{193,1... | collective-permute-start | bytes 393224 | tf_op jit(solution)/shard_map/ppermute | solution.py:14
  35.6 3.6 %all-to-all-start = ((f32[4,32,1024]{2,1,0:T(8,128)}), f32[4,32,1024]{2,1,0:T(8,128)S(1)}, u32[]{:S(2)}, u32[]{:S(2)}) async-start(f32[4,32,1024]{2,1,0:T(8,128)} %broadcast_in_dim.21), calls=%async_computation | async-start | bytes 1048576 | tf_op jit(solution)/shard_map/all_to_all | solution.py:24
  39.2 2.2 %collective-permute-done.16 = f32[1,32,1024]{2,1,0:T(8,128)S(1)} collective-permute-done((f32[1,32,1024]{2,1,0:T(8,128)}, f32[1,32,1024]{2,1,0:T(8,128)S(1)}, u32[]{:S(2)}, u32[]{:S(2)}) %collective-permute-start.16) | collective-permute-done | bytes 131104 | tf_op jit(solution)/shard_map/ppermute | solution.py:19
  46.0 3.3 %collective-permute-start.3 = (f32[4,32,1024]{2,1,0:T(8,128)}, f32[4,32,1024]{2,1,0:T(8,128)}, u32[]{:S(2)}, u32[]{:S(2)}) collective-permute-start(f32[4,32,1024]{2,1,0:T(8,128)} %pad_maximum_fusion.5), channel_id=1, source_target_pairs={{0,32},{32,0},{1,33},{33,1},{2,34},{34,2},{3,35},{35,3},{4,36},{36... | collective-permute-start | bytes 1572872 | tf_op jit(solution)/shard_map/ppermute | solution.py:19
  52.7 4.7 %collective-permute-done.17 = f32[2,32,1024]{2,1,0:T(8,128)} collective-permute-done((f32[2,32,1024]{2,1,0:T(8,128)}, f32[2,32,1024]{2,1,0:T(8,128)}, u32[]{:S(2)}, u32[]{:S(2)}) %collective-permute-start.17) | collective-permute-done | bytes 262176 | tf_op jit(solution)/shard_map/ppermute | solution.py:19
  58.4 1.9 %collective-permute-start.18 = (f32[4,32,1024]{2,1,0:T(8,128)S(1)}, f32[4,32,1024]{2,1,0:T(8,128)S(1)}, u32[]{:S(2)}, u32[]{:S(2)}) collective-permute-start(f32[4,32,1024]{2,1,0:T(8,128)S(1)} %bitcast.164), channel_id=1, source_target_pairs={{0,4},{4,0},{8,12},{12,8},{16,20},{20,16},{24,28},{28,24},{1,5},{5... | collective-permute-start | bytes 1572872 | tf_op jit(solution)/shard_map/ppermute | solution.py:19
  63.7 3.2 %collective-permute-start.7 = (f32[128,1024]{1,0:T(8,128)S(1)}, f32[128,1024]{1,0:T(8,128)S(1)}, u32[]{:S(2)}, u32[]{:S(2)}) collective-permute-start(f32[128,1024]{1,0:T(8,128)S(1)} %fusion.27), channel_id=1, source_target_pairs={{0,1},{1,2},{2,3},{3,0},{4,5},{5,6},{6,7},{7,4},{8,9},{9,10},{10,1... | collective-permute-start | bytes 1572872 | tf_op jit(solution)/shard_map/ppermute | solution.py:14
  72.2 3.4 %collective-permute-start.6 = (f32[128,1024]{1,0:T(8,128)}, f32[128,1024]{1,0:T(8,128)}, u32[]{:S(2)}, u32[]{:S(2)}) collective-permute-start(f32[128,1024]{1,0:T(8,128)} %fusion.26), channel_id=1, source_target_pairs={{0,3},{1,0},{2,1},{3,2},{4,7},{5,4},{6,5},{7,6},{8,11},{9,8},{10,9... | collective-permute-start | bytes 1572872 | tf_op jit(solution)/shard_map/ppermute | solution.py:14
  76.4 3.3 %collective-permute-start.11 = (f32[128,1024]{1,0:T(8,128)S(1)}, f32[128,1024]{1,0:T(8,128)S(1)}, u32[]{:S(2)}, u32[]{:S(2)}) collective-permute-start(f32[128,1024]{1,0:T(8,128)S(1)} %fusion.29), channel_id=1, source_target_pairs={{0,3},{1,0},{2,1},{3,2},{4,7},{5,4},{6,5},{7,6},{8,11},{9,8},{10,9... | collective-permute-start | bytes 1572872 | tf_op jit(solution)/shard_map/ppermute | solution.py:14
  80.8 2.0 %collective-permute-start.8 = (f32[128,1024]{1,0:T(8,128)}, f32[128,1024]{1,0:T(8,128)}, u32[]{:S(2)}, u32[]{:S(2)}) collective-permute-start(f32[128,1024]{1,0:T(8,128)} %add.180), channel_id=1, source_target_pairs={{0,1},{1,2},{2,3},{3,0},{4,5},{5,6},{6,7},{7,4},{8,9},{9,10},{10,1... | collective-permute-start | bytes 1572872 | tf_op jit(solution)/shard_map/ppermute | solution.py:14
  84.6 3.1 %collective-permute-start.10 = (f32[128,1024]{1,0:T(8,128)}, f32[128,1024]{1,0:T(8,128)}, u32[]{:S(2)}, u32[]{:S(2)}) collective-permute-start(f32[128,1024]{1,0:T(8,128)} %fusion.28), channel_id=1, source_target_pairs={{0,1},{1,2},{2,3},{3,0},{4,5},{5,6},{6,7},{7,4},{8,9},{9,10},{10,1... | collective-permute-start | bytes 1572872 | tf_op jit(solution)/shard_map/ppermute | solution.py:14
  87.7 10.6 %collective-permute-done.11 = f32[128,1024]{1,0:T(8,128)S(1)} collective-permute-done((f32[128,1024]{1,0:T(8,128)S(1)}, f32[128,1024]{1,0:T(8,128)S(1)}, u32[]{:S(2)}, u32[]{:S(2)}) %collective-permute-start.11) | collective-permute-done | bytes 524320 | tf_op jit(solution)/shard_map/ppermute | solution.py:14
  99.2 4.5 %collective-permute-start.12 = (f32[128,1024]{1,0:T(8,128)}, f32[128,1024]{1,0:T(8,128)}, u32[]{:S(2)}, u32[]{:S(2)}) collective-permute-start(f32[128,1024]{1,0:T(8,128)} %add.190), channel_id=1, source_target_pairs={{0,3},{1,0},{2,1},{3,2},{4,7},{5,4},{6,5},{7,6},{8,11},{9,8},{10,9... | collective-permute-start | bytes 1572872 | tf_op jit(solution)/shard_map/ppermute | solution.py:14
  104.3 3.8 %collective-permute-start.19 = (f32[2,512,256]{2,1,0:T(8,128)S(1)}, f32[2,512,256]{2,1,0:T(8,128)S(1)}, u32[]{:S(2)}, u32[]{:S(2)}) collective-permute-start(f32[2,512,256]{2,1,0:T(8,128)S(1)} %bitcast.156), channel_id=1, source_target_pairs={{0,32},{32,0},{1,33},{33,1},{2,34},{34,2},{3,35},{35,3},{4,36},{36... | collective-permute-start | bytes 3145736 | tf_op jit(solution)/shard_map/ppermute | solution.py:19
  109.5 1.9 %collective-permute-start.20 = (f32[2,128,256]{2,1,0:T(8,128)S(1)}, f32[2,128,256]{2,1,0:T(8,128)S(1)}, u32[]{:S(2)}, u32[]{:S(2)}) collective-permute-start(f32[2,128,256]{2,1,0:T(8,128)S(1)} %pad_maximum_fusion.8), channel_id=1, source_target_pairs={{0,32},{32,0},{1,33},{33,1},{2,34},{34,2},{3,35},{35,3},{4,36},{36... | collective-permute-start | bytes 786440 | tf_op jit(solution)/shard_map/ppermute | solution.py:19
  111.5 2.2 %collective-permute-done.12 = f32[128,1024]{1,0:T(8,128)} collective-permute-done((f32[128,1024]{1,0:T(8,128)}, f32[128,1024]{1,0:T(8,128)}, u32[]{:S(2)}, u32[]{:S(2)}) %collective-permute-start.12) | collective-permute-done | bytes 524320 | tf_op jit(solution)/shard_map/ppermute | solution.py:14
  115.0 4.4 %collective-permute-start.21 = (f32[2,128,256]{2,1,0:T(8,128)S(1)}, f32[2,128,256]{2,1,0:T(8,128)S(1)}, u32[]{:S(2)}, u32[]{:S(2)}) collective-permute-start(f32[2,128,256]{2,1,0:T(8,128)S(1)} %pad_maximum_fusion.9), channel_id=1, source_target_pairs={{0,32},{32,0},{1,33},{33,1},{2,34},{34,2},{3,35},{35,3},{4,36},{36... | collective-permute-start | bytes 786440 | tf_op jit(solution)/shard_map/ppermute | solution.py:19
  120.9 3.1 %collective-permute-start.9 = (f32[2,32,1024]{2,1,0:T(8,128)S(1)}, f32[2,32,1024]{2,1,0:T(8,128)S(1)}, u32[]{:S(2)}, u32[]{:S(2)}) collective-permute-start(f32[2,32,1024]{2,1,0:T(8,128)S(1)} %dynamic-slice_bitcast_fusion.1), channel_id=1, source_target_pairs={{0,4},{4,0},{8,12},{12,8},{16,20},{20,16},{24,28},{28,24},{1,5},{5... | collective-permute-start | bytes 786440 | tf_op jit(solution)/shard_map/ppermute | solution.py:19
  126.0 7.4 %all-to-all-start.1 = ((f32[16,8,8,256]{3,2,1,0:T(8,128)}), f32[16,8,8,256]{3,2,1,0:T(8,128)S(1)}, u32[]{:S(2)}, u32[]{:S(2)}) async-start(f32[16,8,8,256]{3,2,1,0:T(8,128)} %pad_maximum_fusion.4), calls=%async_computation.1 | async-start | bytes 2097152 | tf_op jit(solution)/shard_map/all_to_all | solution.py:139
  133.5 2.2 %collective-permute-start.13 = (f32[2,32,1024]{2,1,0:T(8,128)S(1)}, f32[2,32,1024]{2,1,0:T(8,128)S(1)}, u32[]{:S(2)}, u32[]{:S(2)}) collective-permute-start(f32[2,32,1024]{2,1,0:T(8,128)S(1)} %dynamic-slice_bitcast_fusion), channel_id=1, source_target_pairs={{0,4},{4,0},{8,12},{12,8},{16,20},{20,16},{24,28},{28,24},{1,5},{5... | collective-permute-start | bytes 786440 | tf_op jit(solution)/shard_map/ppermute | solution.py:19
  135.8 6.9 %collective-permute-done.13 = f32[2,32,1024]{2,1,0:T(8,128)S(1)} collective-permute-done((f32[2,32,1024]{2,1,0:T(8,128)S(1)}, f32[2,32,1024]{2,1,0:T(8,128)S(1)}, u32[]{:S(2)}, u32[]{:S(2)}) %collective-permute-start.13) | collective-permute-done | bytes 262176 | tf_op jit(solution)/shard_map/ppermute | solution.py:19
  142.8 1.9 %collective-permute-start.14 = (f32[2,32,1024]{2,1,0:T(8,128)S(1)}, f32[2,32,1024]{2,1,0:T(8,128)S(1)}, u32[]{:S(2)}, u32[]{:S(2)}) collective-permute-start(f32[2,32,1024]{2,1,0:T(8,128)S(1)} %pad_maximum_fusion.7), channel_id=1, source_target_pairs={{0,8},{4,12},{8,0},{12,4},{16,24},{20,28},{24,16},{28,20},{1,9},{5... | collective-permute-start | bytes 786440 | tf_op jit(solution)/shard_map/ppermute | solution.py:19
  144.7 5.1 %all-to-all-done.1 = f32[16,8,8,256]{3,2,1,0:T(8,128)S(1)} async-done(((f32[16,8,8,256]{3,2,1,0:T(8,128)}), f32[16,8,8,256]{3,2,1,0:T(8,128)S(1)}, u32[]{:S(2)}, u32[]{:S(2)}) %all-to-all-start.1) | async-done | bytes 1048608 | tf_op jit(solution)/shard_map/all_to_all | solution.py:139
  150.6 7.4 %all-to-all-start.2 = ((f32[16,8,256]{2,1,0:T(8,128)}), f32[16,8,256]{2,1,0:T(8,128)S(1)}, u32[]{:S(2)}, u32[]{:S(2)}) async-start(f32[16,8,256]{2,1,0:T(8,128)} %pad_maximum_fusion.10), calls=%async_computation.2 | async-start | bytes 262144 | tf_op jit(solution)/shard_map/all_to_all | solution.py:141
  159.4 5.8 %collective-permute-start.15 = (f32[32,1024]{1,0:T(8,128)S(1)}, f32[32,1024]{1,0:T(8,128)S(1)}, u32[]{:S(2)}, u32[]{:S(2)}) collective-permute-start(f32[32,1024]{1,0:T(8,128)S(1)} %select_bitcast_fusion.10), channel_id=1, source_target_pairs={{0,16},{4,20},{8,24},{12,28},{16,0},{20,4},{24,8},{28,12},{1,17},{... | collective-permute-start | bytes 393224 | tf_op jit(solution)/shard_map/ppermute | solution.py:19
  165.2 4.7 %all-to-all-done.2 = f32[16,8,256]{2,1,0:T(8,128)S(1)} async-done(((f32[16,8,256]{2,1,0:T(8,128)}), f32[16,8,256]{2,1,0:T(8,128)S(1)}, u32[]{:S(2)}, u32[]{:S(2)}) %all-to-all-start.2) | async-done | bytes 131104 | tf_op jit(solution)/shard_map/all_to_all | solution.py:141
  170.6 11.8 %all-to-all-start.3 = ((f32[8,8,256]{2,1,0:T(8,128)}), f32[8,8,256]{2,1,0:T(8,128)S(1)}, u32[]{:S(2)}, u32[]{:S(2)}) async-start(f32[8,8,256]{2,1,0:T(8,128)} %broadcast_in_dim.23), calls=%async_computation.3 | async-start | bytes 131072 | tf_op jit(solution)/shard_map/all_to_all | solution.py:24
  183.1 4.2 %all-to-all-done.3 = f32[8,8,256]{2,1,0:T(8,128)S(1)} async-done(((f32[8,8,256]{2,1,0:T(8,128)}), f32[8,8,256]{2,1,0:T(8,128)S(1)}, u32[]{:S(2)}, u32[]{:S(2)}) %all-to-all-start.3) | async-done | bytes 65568 | tf_op jit(solution)/shard_map/all_to_all | solution.py:24
  (99 shorter events, 35.1 us)
Async XLA Ops:
  0.6 40.7 %copy-start.9 = (f32[32,1024]{1,0:T(8,128)S(1)}, f32[32,1024]{1,0:T(8,128)}, u32[]{:S(2)}) copy-start(f32[32,1024]{1,0:T(8,128)} %param.6) | copy-start | bytes 393220
  0.6 34.1 %collective-permute-start.4 = (f32[32,1024]{1,0:T(8,128)}, f32[32,1024]{1,0:T(8,128)S(1)}, u32[]{:S(2)}, u32[]{:S(2)}) collective-permute-start(f32[32,1024]{1,0:T(8,128)} %param.6), channel_id=1, source_target_pairs={{0,256},{256,0},{1,257},{257,1},{2,258},{258,2},{3,259},{259,3},{4... | collective-permute-start | bytes 393224 | tf_op jit(solution)/shard_map/ppermute | solution.py:19
  17.0 24.3 %collective-permute-start.16 = (f32[1,32,1024]{2,1,0:T(8,128)}, f32[1,32,1024]{2,1,0:T(8,128)S(1)}, u32[]{:S(2)}, u32[]{:S(2)}) collective-permute-start(f32[1,32,1024]{2,1,0:T(8,128)} %bitcast.175), channel_id=1, source_target_pairs={{0,16},{4,20},{8,24},{12,28},{16,0},{20,4},{24,8},{28,12},{1,17},{... | collective-permute-start | bytes 393224 | tf_op jit(solution)/shard_map/ppermute | solution.py:19
  21.1 23.0 %collective-permute-start = (f32[32,1024]{1,0:T(8,128)}, f32[32,1024]{1,0:T(8,128)}, u32[]{:S(2)}, u32[]{:S(2)}) collective-permute-start(f32[32,1024]{1,0:T(8,128)} %param.6), channel_id=1, source_target_pairs={{0,192},{64,0},{128,64},{192,128},{1,193},{65,1},{129,65},{193,129... | collective-permute-start | bytes 393224 | tf_op jit(solution)/shard_map/ppermute | solution.py:14
  25.7 18.3 %collective-permute-start.1 = (f32[32,1024]{1,0:T(8,128)}, f32[32,1024]{1,0:T(8,128)}, u32[]{:S(2)}, u32[]{:S(2)}) collective-permute-start(f32[32,1024]{1,0:T(8,128)} %param.6), channel_id=1, source_target_pairs={{0,128},{64,192},{128,0},{192,64},{1,129},{65,193},{129,1},{193,65... | collective-permute-start | bytes 393224 | tf_op jit(solution)/shard_map/ppermute | solution.py:14
  28.0 16.1 %collective-permute-start.2 = (f32[32,1024]{1,0:T(8,128)}, f32[32,1024]{1,0:T(8,128)}, u32[]{:S(2)}, u32[]{:S(2)}) collective-permute-start(f32[32,1024]{1,0:T(8,128)} %param.6), channel_id=1, source_target_pairs={{0,64},{64,128},{128,192},{192,0},{1,65},{65,129},{129,193},{193,1... | collective-permute-start | bytes 393224 | tf_op jit(solution)/shard_map/ppermute | solution.py:14
  35.6 13.8 %copy-start = (f32[2,512,512]{2,1,0:T(8,128)S(1)}, f32[2,512,512]{2,1,0:T(8,128)}, u32[]{:S(2)}) copy-start(f32[2,512,512]{2,1,0:T(8,128)} %param.4) | copy-start | bytes 6291460
  35.6 15.2 %all-to-all-start = ((f32[4,32,1024]{2,1,0:T(8,128)}), f32[4,32,1024]{2,1,0:T(8,128)S(1)}, u32[]{:S(2)}, u32[]{:S(2)}) async-start(f32[4,32,1024]{2,1,0:T(8,128)} %broadcast_in_dim.21), calls=%async_computation | async-start | bytes 1048576 | tf_op jit(solution)/shard_map/all_to_all | solution.py:24
  42.1 15.2 %collective-permute-start.17 = (f32[2,32,1024]{2,1,0:T(8,128)}, f32[2,32,1024]{2,1,0:T(8,128)}, u32[]{:S(2)}, u32[]{:S(2)}) collective-permute-start(f32[2,32,1024]{2,1,0:T(8,128)} %maximum_bitcast_fusion), channel_id=1, source_target_pairs={{0,8},{4,12},{8,0},{12,4},{16,24},{20,28},{24,16},{28,20},{1,9},{5... | collective-permute-start | bytes 786440 | tf_op jit(solution)/shard_map/ppermute | solution.py:19
  46.0 14.3 %collective-permute-start.3 = (f32[4,32,1024]{2,1,0:T(8,128)}, f32[4,32,1024]{2,1,0:T(8,128)}, u32[]{:S(2)}, u32[]{:S(2)}) collective-permute-start(f32[4,32,1024]{2,1,0:T(8,128)} %pad_maximum_fusion.5), channel_id=1, source_target_pairs={{0,32},{32,0},{1,33},{33,1},{2,34},{34,2},{3,35},{35,3},{4,36},{36... | collective-permute-start | bytes 1572872 | tf_op jit(solution)/shard_map/ppermute | solution.py:19
  50.8 10.7 %collective-permute-start.5 = (f32[4,32,1024]{2,1,0:T(8,128)S(1)}, f32[4,32,1024]{2,1,0:T(8,128)S(1)}, u32[]{:S(2)}, u32[]{:S(2)}) collective-permute-start(f32[4,32,1024]{2,1,0:T(8,128)S(1)} %all-to-all-done), channel_id=1, source_target_pairs={{0,32},{32,0},{1,33},{33,1},{2,34},{34,2},{3,35},{35,3},{4,36},{36... | collective-permute-start | bytes 1572872 | tf_op jit(solution)/shard_map/ppermute | solution.py:19
  58.4 24.4 %collective-permute-start.18 = (f32[4,32,1024]{2,1,0:T(8,128)S(1)}, f32[4,32,1024]{2,1,0:T(8,128)S(1)}, u32[]{:S(2)}, u32[]{:S(2)}) collective-permute-start(f32[4,32,1024]{2,1,0:T(8,128)S(1)} %bitcast.164), channel_id=1, source_target_pairs={{0,4},{4,0},{8,12},{12,8},{16,20},{20,16},{24,28},{28,24},{1,5},{5... | collective-permute-start | bytes 1572872 | tf_op jit(solution)/shard_map/ppermute | solution.py:19
  62.2 4.8 %copy-start.7 = (f32[1,4,1,32,512]{4,3,2,1,0:T(8,128)S(1)}, f32[1,4,1,32,512]{4,3,2,1,0:T(8,128)}, u32[]{:S(2)}) copy-start(f32[1,4,1,32,512]{4,3,2,1,0:T(8,128)} %get-tuple-element.24) | copy-start | bytes 786436
  63.7 16.2 %collective-permute-start.7 = (f32[128,1024]{1,0:T(8,128)S(1)}, f32[128,1024]{1,0:T(8,128)S(1)}, u32[]{:S(2)}, u32[]{:S(2)}) collective-permute-start(f32[128,1024]{1,0:T(8,128)S(1)} %fusion.27), channel_id=1, source_target_pairs={{0,1},{1,2},{2,3},{3,0},{4,5},{5,6},{6,7},{7,4},{8,9},{9,10},{10,1... | collective-permute-start | bytes 1572872 | tf_op jit(solution)/shard_map/ppermute | solution.py:14
  70.5 5.1 %copy-start.2 = (f32[1,4,1,32,512]{4,3,2,1,0:T(8,128)S(1)}, f32[1,4,1,32,512]{4,3,2,1,0:T(8,128)}, u32[]{:S(2)}) copy-start(f32[1,4,1,32,512]{4,3,2,1,0:T(8,128)} %get-tuple-element.25) | copy-start | bytes 786436
  72.2 36.0 %collective-permute-start.6 = (f32[128,1024]{1,0:T(8,128)}, f32[128,1024]{1,0:T(8,128)}, u32[]{:S(2)}, u32[]{:S(2)}) collective-permute-start(f32[128,1024]{1,0:T(8,128)} %fusion.26), channel_id=1, source_target_pairs={{0,3},{1,0},{2,1},{3,2},{4,7},{5,4},{6,5},{7,6},{8,11},{9,8},{10,9... | collective-permute-start | bytes 1572872 | tf_op jit(solution)/shard_map/ppermute | solution.py:14
  76.4 6.6 %copy-start.1 = (f32[1,4,1,32,512]{4,3,2,1,0:T(8,128)S(1)}, f32[1,4,1,32,512]{4,3,2,1,0:T(8,128)}, u32[]{:S(2)}) copy-start(f32[1,4,1,32,512]{4,3,2,1,0:T(8,128)} %get-tuple-element.23) | copy-start | bytes 786436
  76.4 21.9 %collective-permute-start.11 = (f32[128,1024]{1,0:T(8,128)S(1)}, f32[128,1024]{1,0:T(8,128)S(1)}, u32[]{:S(2)}, u32[]{:S(2)}) collective-permute-start(f32[128,1024]{1,0:T(8,128)S(1)} %fusion.29), channel_id=1, source_target_pairs={{0,3},{1,0},{2,1},{3,2},{4,7},{5,4},{6,5},{7,6},{8,11},{9,8},{10,9... | collective-permute-start | bytes 1572872 | tf_op jit(solution)/shard_map/ppermute | solution.py:14
  80.8 27.3 %collective-permute-start.8 = (f32[128,1024]{1,0:T(8,128)}, f32[128,1024]{1,0:T(8,128)}, u32[]{:S(2)}, u32[]{:S(2)}) collective-permute-start(f32[128,1024]{1,0:T(8,128)} %add.180), channel_id=1, source_target_pairs={{0,1},{1,2},{2,3},{3,0},{4,5},{5,6},{6,7},{7,4},{8,9},{9,10},{10,1... | collective-permute-start | bytes 1572872 | tf_op jit(solution)/shard_map/ppermute | solution.py:14
  84.6 26.8 %collective-permute-start.10 = (f32[128,1024]{1,0:T(8,128)}, f32[128,1024]{1,0:T(8,128)}, u32[]{:S(2)}, u32[]{:S(2)}) collective-permute-start(f32[128,1024]{1,0:T(8,128)} %fusion.28), channel_id=1, source_target_pairs={{0,1},{1,2},{2,3},{3,0},{4,5},{5,6},{6,7},{7,4},{8,9},{9,10},{10,1... | collective-permute-start | bytes 1572872 | tf_op jit(solution)/shard_map/ppermute | solution.py:14
  99.2 14.4 %collective-permute-start.12 = (f32[128,1024]{1,0:T(8,128)}, f32[128,1024]{1,0:T(8,128)}, u32[]{:S(2)}, u32[]{:S(2)}) collective-permute-start(f32[128,1024]{1,0:T(8,128)} %add.190), channel_id=1, source_target_pairs={{0,3},{1,0},{2,1},{3,2},{4,7},{5,4},{6,5},{7,6},{8,11},{9,8},{10,9... | collective-permute-start | bytes 1572872 | tf_op jit(solution)/shard_map/ppermute | solution.py:14
  104.3 19.8 %collective-permute-start.19 = (f32[2,512,256]{2,1,0:T(8,128)S(1)}, f32[2,512,256]{2,1,0:T(8,128)S(1)}, u32[]{:S(2)}, u32[]{:S(2)}) collective-permute-start(f32[2,512,256]{2,1,0:T(8,128)S(1)} %bitcast.156), channel_id=1, source_target_pairs={{0,32},{32,0},{1,33},{33,1},{2,34},{34,2},{3,35},{35,3},{4,36},{36... | collective-permute-start | bytes 3145736 | tf_op jit(solution)/shard_map/ppermute | solution.py:19
  109.5 14.5 %collective-permute-start.20 = (f32[2,128,256]{2,1,0:T(8,128)S(1)}, f32[2,128,256]{2,1,0:T(8,128)S(1)}, u32[]{:S(2)}, u32[]{:S(2)}) collective-permute-start(f32[2,128,256]{2,1,0:T(8,128)S(1)} %pad_maximum_fusion.8), channel_id=1, source_target_pairs={{0,32},{32,0},{1,33},{33,1},{2,34},{34,2},{3,35},{35,3},{4,36},{36... | collective-permute-start | bytes 786440 | tf_op jit(solution)/shard_map/ppermute | solution.py:19
  115.0 9.1 %collective-permute-start.21 = (f32[2,128,256]{2,1,0:T(8,128)S(1)}, f32[2,128,256]{2,1,0:T(8,128)S(1)}, u32[]{:S(2)}, u32[]{:S(2)}) collective-permute-start(f32[2,128,256]{2,1,0:T(8,128)S(1)} %pad_maximum_fusion.9), channel_id=1, source_target_pairs={{0,32},{32,0},{1,33},{33,1},{2,34},{34,2},{3,35},{35,3},{4,36},{36... | collective-permute-start | bytes 786440 | tf_op jit(solution)/shard_map/ppermute | solution.py:19
  120.9 14.8 %collective-permute-start.9 = (f32[2,32,1024]{2,1,0:T(8,128)S(1)}, f32[2,32,1024]{2,1,0:T(8,128)S(1)}, u32[]{:S(2)}, u32[]{:S(2)}) collective-permute-start(f32[2,32,1024]{2,1,0:T(8,128)S(1)} %dynamic-slice_bitcast_fusion.1), channel_id=1, source_target_pairs={{0,4},{4,0},{8,12},{12,8},{16,20},{20,16},{24,28},{28,24},{1,5},{5... | collective-permute-start | bytes 786440 | tf_op jit(solution)/shard_map/ppermute | solution.py:19
  126.0 23.9 %all-to-all-start.1 = ((f32[16,8,8,256]{3,2,1,0:T(8,128)}), f32[16,8,8,256]{3,2,1,0:T(8,128)S(1)}, u32[]{:S(2)}, u32[]{:S(2)}) async-start(f32[16,8,8,256]{3,2,1,0:T(8,128)} %pad_maximum_fusion.4), calls=%async_computation.1 | async-start | bytes 2097152 | tf_op jit(solution)/shard_map/all_to_all | solution.py:139
  133.5 9.2 %collective-permute-start.13 = (f32[2,32,1024]{2,1,0:T(8,128)S(1)}, f32[2,32,1024]{2,1,0:T(8,128)S(1)}, u32[]{:S(2)}, u32[]{:S(2)}) collective-permute-start(f32[2,32,1024]{2,1,0:T(8,128)S(1)} %dynamic-slice_bitcast_fusion), channel_id=1, source_target_pairs={{0,4},{4,0},{8,12},{12,8},{16,20},{20,16},{24,28},{28,24},{1,5},{5... | collective-permute-start | bytes 786440 | tf_op jit(solution)/shard_map/ppermute | solution.py:19
  142.7 44.6 %copy-start.10 = (f32[32,512]{1,0:T(8,128)S(1)}, f32[32,512]{1,0:T(8,128)}, u32[]{:S(2)}) copy-start(f32[32,512]{1,0:T(8,128)} %param.7) | copy-start | bytes 196612
  142.8 16.6 %collective-permute-start.14 = (f32[2,32,1024]{2,1,0:T(8,128)S(1)}, f32[2,32,1024]{2,1,0:T(8,128)S(1)}, u32[]{:S(2)}, u32[]{:S(2)}) collective-permute-start(f32[2,32,1024]{2,1,0:T(8,128)S(1)} %pad_maximum_fusion.7), channel_id=1, source_target_pairs={{0,8},{4,12},{8,0},{12,4},{16,24},{20,28},{24,16},{28,20},{1,9},{5... | collective-permute-start | bytes 786440 | tf_op jit(solution)/shard_map/ppermute | solution.py:19
  150.6 19.4 %all-to-all-start.2 = ((f32[16,8,256]{2,1,0:T(8,128)}), f32[16,8,256]{2,1,0:T(8,128)S(1)}, u32[]{:S(2)}, u32[]{:S(2)}) async-start(f32[16,8,256]{2,1,0:T(8,128)} %pad_maximum_fusion.10), calls=%async_computation.2 | async-start | bytes 262144 | tf_op jit(solution)/shard_map/all_to_all | solution.py:141
  159.4 23.0 %collective-permute-start.15 = (f32[32,1024]{1,0:T(8,128)S(1)}, f32[32,1024]{1,0:T(8,128)S(1)}, u32[]{:S(2)}, u32[]{:S(2)}) collective-permute-start(f32[32,1024]{1,0:T(8,128)S(1)} %select_bitcast_fusion.10), channel_id=1, source_target_pairs={{0,16},{4,20},{8,24},{12,28},{16,0},{20,4},{24,8},{28,12},{1,17},{... | collective-permute-start | bytes 393224 | tf_op jit(solution)/shard_map/ppermute | solution.py:19
  170.6 16.7 %all-to-all-start.3 = ((f32[8,8,256]{2,1,0:T(8,128)}), f32[8,8,256]{2,1,0:T(8,128)S(1)}, u32[]{:S(2)}, u32[]{:S(2)}) async-start(f32[8,8,256]{2,1,0:T(8,128)} %broadcast_in_dim.23), calls=%async_computation.3 | async-start | bytes 131072 | tf_op jit(solution)/shard_map/all_to_all | solution.py:24
  (5 other events, 8.0 us)

commit v5 on v4

--- a/solution.py
+++ b/solution.py
@@ -37,6 +37,11 @@
     return jnp.dot(a, b, precision=HIGH, preferred_element_type=jnp.float32)
 
 
+def pair(a, b):
+    dims = (((2,), (1,)), ((0,), (0,)))
+    return lax.dot_general(a, b, dims, precision=HIGH, preferred_element_type=jnp.float32)
+
+
 def gathered_column(panel):
     c = lax.axis_index("c")
     zh = lax.axis_index("zh")
@@ -73,10 +78,8 @@
     for t in halves:
         t = t.reshape(2, 2, -1, t.shape[-1])
         rows.append(pick(t, low, 1) + swap(pick(t, 1 - low, 1), "zl", 1))
-    kept = [pick(t, mid, 0) for t in rows]
-    sent = jnp.stack([pick(t, 1 - mid, 0) for t in rows])
-    sent = swap(sent, "zl", 2)
-    rows = [kept[i] + sent[i] for i in range(2)]
+    for i, t in enumerate(rows):
+        rows[i] = pick(t, mid, 0) + swap(pick(t, 1 - mid, 0), "zl", 2)
     first = high == 0
     sent = swap(jnp.where(first, rows[1], rows[0]), "zl", 4)
     return jnp.where(first, rows[0], rows[1]) + sent
@@ -97,12 +100,11 @@
     down_a = shift(product(2, 1), "x", -1)
     up_b = shift(product(1, 1), "x", 1)
     down_b = shift(product(3, 0), "x", -1)
-    rest = [product(*di) for di in ((1, 0), (3, 1), (0, 0), (0, 1))]
-    rest = lax.optimization_barrier(rest)
+    rest = lax.optimization_barrier([product(1, 0), product(3, 1)])
     up_c = shift(rest[0] + up_a, "x", 1)
     down_c = shift(rest[1] + down_a, "x", -1)
-    first = rest[2] + down_b + up_c
-    return first, rest[3] + up_b + down_c
+    first = product(0, 0) + down_b + up_c
+    return first, product(0, 1) + up_b + down_c
 
 
 def local(inverse_tiles, tile_rows, panel, pivot_base):
@@ -129,13 +131,14 @@
         other.append(swap(side(t, 1 - c), "c", 1))
         mine.append(side(t, c))
     k = 4 * share
-    own = [dot(u[j, :, :k], mine[0][j]) for j in range(2)]
+    cuts = (slice(0, k), slice(k, 2 * k))
+    own = pair(u[:, :, cuts[0]], mine[0])
     own = lax.optimization_barrier(own)
-    own = [own[j] + dot(u[j, :, k:], mine[1][j]) for j in range(2)]
+    own = own + pair(u[:, :, cuts[1]], mine[1])
     own = lax.optimization_barrier(own)
-    other = [jnp.concatenate([other[0][j], other[1][j]]) for j in range(2)]
-    w = [own[j] + dot(other_u[j], other[j]) for j in range(2)]
-    w = jnp.concatenate([x.reshape(16, 4, 8, half) for x in w], axis=1)
+    for i in range(2):
+        own = own + pair(other_u[:, :, cuts[i]], other[i])
+    w = own.reshape(2, 16, 4, 8, half).transpose(1, 0, 2, 3, 4).reshape(16, 8, 8, half)
     w = lax.all_to_all(w, ("y", "x"), 0, 0, tiled=True).sum(axis=0)
     w = jnp.concatenate([w, w])
     w = lax.all_to_all(w, ("zh", "zl"), 0, 0, tiled=True).sum(axis=0)

time: 191 us -> 188 us (0.984)
  the two profiles are of different devices: /device:TPU:1 before, /device:TPU:64 now
where the time goes in v5:
time: 188 us; the launch traced here: 187 us
  starting transfers between devices  109 us (58%)
  waiting for transfers between devices  41.9 us (22%)
  matrix products  11.9 us (6%)
  other arithmetic  11.4 us (6%)
  local copies, waits for them, and re-layouts  7.82 us (4%)
  between operations  4.18 us (2%)
    ppermute x14, starting transfers between devices, swap(): return lax.ppermute(x, axis, [(i, i ^ bit) for i in range(n)])  57 us
    ppermute x9, starting transfers between devices, shift(): return lax.ppermute(x, axis, [(i, (i + by) % n) for i in range(n)])  32.9 us
    all_to_all x1, waiting for transfers between devices, local(): w = lax.all_to_all(w, ('zh', 'zl'), 0, 0, tiled=True).sum(axis=0)  14.3 us
    ppermute x9, waiting for transfers between devices, shift(): return lax.ppermute(x, axis, [(i, (i + by) % n) for i in range(n)])  12.4 us
    ppermute x14, waiting for transfers between devices, swap(): return lax.ppermute(x, axis, [(i, i ^ bit) for i in range(n)])  10.3 us
    dot_general x8, matrix products, dot(): return jnp.dot(a, b, precision=HIGH, preferred_element_type=jnp.float32)  9.62 us
    all_to_all x2, starting transfers between devices, spread(): return lax.all_to_all(copies, axes, 0, 0, tiled=True)  7.74 us
    all_to_all x1, starting transfers between devices, local(): w = lax.all_to_all(w, ('zh', 'zl'), 0, 0, tiled=True).sum(axis=0)  6.93 us
  transfers between devices with their start and end apart: 27, of which 9 were waited for; matrix products, arithmetic and copies ran while one was open for 15% of the time, Pallas kernels for 0%

profile of v5, /device:TPU:64, one launch (start us, length us, event | category | flops | bytes accessed | tf_op | source)
XLA Modules:
  0.0 186.6 jit_solution(12710578724935868431)
XLA Ops:
  0.6 14.1 %collective-permute-start.4 = (f32[32,1024]{1,0:T(8,128)}, f32[32,1024]{1,0:T(8,128)S(1)}, u32[]{:S(2)}, u32[]{:S(2)}) collective-permute-start(f32[32,1024]{1,0:T(8,128)} %param.6), channel_id=1, source_target_pairs={{0,256},{256,0},{1,257},{257,1},{2,258},{258,2},{3,259},{259,3},{4... | collective-permute-start | bytes 393224 | tf_op jit(solution)/shard_map/ppermute | solution.py:19
  14.7 4.3 %collective-permute-start.17 = (f32[1,32,1024]{2,1,0:T(8,128)}, f32[1,32,1024]{2,1,0:T(8,128)S(1)}, u32[]{:S(2)}, u32[]{:S(2)}) collective-permute-start(f32[1,32,1024]{2,1,0:T(8,128)} %bitcast.168), channel_id=1, source_target_pairs={{0,16},{4,20},{8,24},{12,28},{16,0},{20,4},{24,8},{28,12},{1,17},{... | collective-permute-start | bytes 393224 | tf_op jit(solution)/shard_map/ppermute | solution.py:19
  19.0 5.1 %collective-permute-start.1 = (f32[32,1024]{1,0:T(8,128)}, f32[32,1024]{1,0:T(8,128)}, u32[]{:S(2)}, u32[]{:S(2)}) collective-permute-start(f32[32,1024]{1,0:T(8,128)} %param.6), channel_id=1, source_target_pairs={{0,128},{64,192},{128,0},{192,64},{1,129},{65,193},{129,1},{193,65... | collective-permute-start | bytes 393224 | tf_op jit(solution)/shard_map/ppermute | solution.py:14
  24.1 2.6 %collective-permute-start.2 = (f32[32,1024]{1,0:T(8,128)}, f32[32,1024]{1,0:T(8,128)}, u32[]{:S(2)}, u32[]{:S(2)}) collective-permute-start(f32[32,1024]{1,0:T(8,128)} %param.6), channel_id=1, source_target_pairs={{0,64},{64,128},{128,192},{192,0},{1,65},{65,129},{129,193},{193,1... | collective-permute-start | bytes 393224 | tf_op jit(solution)/shard_map/ppermute | solution.py:14
  26.7 4.5 %collective-permute-start = (f32[32,1024]{1,0:T(8,128)}, f32[32,1024]{1,0:T(8,128)}, u32[]{:S(2)}, u32[]{:S(2)}) collective-permute-start(f32[32,1024]{1,0:T(8,128)} %param.6), channel_id=1, source_target_pairs={{0,192},{64,0},{128,64},{192,128},{1,193},{65,1},{129,65},{193,129... | collective-permute-start | bytes 393224 | tf_op jit(solution)/shard_map/ppermute | solution.py:14
  36.2 3.6 %all-to-all-start = ((f32[4,32,1024]{2,1,0:T(8,128)}), f32[4,32,1024]{2,1,0:T(8,128)S(1)}, u32[]{:S(2)}, u32[]{:S(2)}) async-start(f32[4,32,1024]{2,1,0:T(8,128)} %broadcast_in_dim.21), calls=%async_computation | async-start | bytes 1048576 | tf_op jit(solution)/shard_map/all_to_all | solution.py:24
  40.5 3.3 %collective-permute-start.18 = (f32[2,32,1024]{2,1,0:T(8,128)}, f32[2,32,1024]{2,1,0:T(8,128)}, u32[]{:S(2)}, u32[]{:S(2)}) collective-permute-start(f32[2,32,1024]{2,1,0:T(8,128)} %maximum_bitcast_fusion), channel_id=1, source_target_pairs={{0,8},{4,12},{8,0},{12,4},{16,24},{20,28},{24,16},{28,20},{1,9},{5... | collective-permute-start | bytes 786440 | tf_op jit(solution)/shard_map/ppermute | solution.py:19
  49.3 2.4 %collective-permute-start.5 = (f32[4,32,1024]{2,1,0:T(8,128)S(1)}, f32[4,32,1024]{2,1,0:T(8,128)S(1)}, u32[]{:S(2)}, u32[]{:S(2)}) collective-permute-start(f32[4,32,1024]{2,1,0:T(8,128)S(1)} %all-to-all-done), channel_id=1, source_target_pairs={{0,32},{32,0},{1,33},{33,1},{2,34},{34,2},{3,35},{35,3},{4,36},{36... | collective-permute-start | bytes 1572872 | tf_op jit(solution)/shard_map/ppermute | solution.py:19
  51.7 2.6 %collective-permute-done.18 = f32[2,32,1024]{2,1,0:T(8,128)} collective-permute-done((f32[2,32,1024]{2,1,0:T(8,128)}, f32[2,32,1024]{2,1,0:T(8,128)}, u32[]{:S(2)}, u32[]{:S(2)}) %collective-permute-start.18) | collective-permute-done | bytes 262176 | tf_op jit(solution)/shard_map/ppermute | solution.py:19
  55.4 4.5 %collective-permute-start.19 = (f32[4,32,1024]{2,1,0:T(8,128)S(1)}, f32[4,32,1024]{2,1,0:T(8,128)S(1)}, u32[]{:S(2)}, u32[]{:S(2)}) collective-permute-start(f32[4,32,1024]{2,1,0:T(8,128)S(1)} %bitcast.159), channel_id=1, source_target_pairs={{0,4},{4,0},{8,12},{12,8},{16,20},{20,16},{24,28},{28,24},{1,5},{5... | collective-permute-start | bytes 1572872 | tf_op jit(solution)/shard_map/ppermute | solution.py:19
  65.7 4.8 %collective-permute-start.12 = (f32[128,1024]{1,0:T(8,128)S(1)}, f32[128,1024]{1,0:T(8,128)S(1)}, u32[]{:S(2)}, u32[]{:S(2)}) collective-permute-start(f32[128,1024]{1,0:T(8,128)S(1)} %fusion.25), channel_id=1, source_target_pairs={{0,3},{1,0},{2,1},{3,2},{4,7},{5,4},{6,5},{7,6},{8,11},{9,8},{10,9... | collective-permute-start | bytes 1572872 | tf_op jit(solution)/shard_map/ppermute | solution.py:14
  75.5 2.6 %collective-permute-start.11 = (f32[128,1024]{1,0:T(8,128)}, f32[128,1024]{1,0:T(8,128)}, u32[]{:S(2)}, u32[]{:S(2)}) collective-permute-start(f32[128,1024]{1,0:T(8,128)} %fusion.24), channel_id=1, source_target_pairs={{0,1},{1,2},{2,3},{3,0},{4,5},{5,6},{6,7},{7,4},{8,9},{9,10},{10,1... | collective-permute-start | bytes 1572872 | tf_op jit(solution)/shard_map/ppermute | solution.py:14
  78.2 2.9 %collective-permute-done.12 = f32[128,1024]{1,0:T(8,128)S(1)} collective-permute-done((f32[128,1024]{1,0:T(8,128)S(1)}, f32[128,1024]{1,0:T(8,128)S(1)}, u32[]{:S(2)}, u32[]{:S(2)}) %collective-permute-start.12) | collective-permute-done | bytes 524320 | tf_op jit(solution)/shard_map/ppermute | solution.py:14
  82.0 5.6 %collective-permute-start.13 = (f32[128,1024]{1,0:T(8,128)}, f32[128,1024]{1,0:T(8,128)}, u32[]{:S(2)}, u32[]{:S(2)}) collective-permute-start(f32[128,1024]{1,0:T(8,128)} %add.186), channel_id=1, source_target_pairs={{0,3},{1,0},{2,1},{3,2},{4,7},{5,4},{6,5},{7,6},{8,11},{9,8},{10,9... | collective-permute-start | bytes 1572872 | tf_op jit(solution)/shard_map/ppermute | solution.py:14
  93.4 1.9 %collective-permute-start.6 = (f32[128,1024]{1,0:T(8,128)S(1)}, f32[128,1024]{1,0:T(8,128)S(1)}, u32[]{:S(2)}, u32[]{:S(2)}) collective-permute-start(f32[128,1024]{1,0:T(8,128)S(1)} %fusion.20), channel_id=1, source_target_pairs={{0,3},{1,0},{2,1},{3,2},{4,7},{5,4},{6,5},{7,6},{8,11},{9,8},{10,9... | collective-permute-start | bytes 1572872 | tf_op jit(solution)/shard_map/ppermute | solution.py:14
  96.4 3.9 %collective-permute-start.8 = (f32[128,1024]{1,0:T(8,128)S(1)}, f32[128,1024]{1,0:T(8,128)S(1)}, u32[]{:S(2)}, u32[]{:S(2)}) collective-permute-start(f32[128,1024]{1,0:T(8,128)S(1)} %add.175), channel_id=1, source_target_pairs={{0,1},{1,2},{2,3},{3,0},{4,5},{5,6},{6,7},{7,4},{8,9},{9,10},{10,1... | collective-permute-start | bytes 1572872 | tf_op jit(solution)/shard_map/ppermute | solution.py:14
  100.4 2.0 %fusion.1 = f32[128,1024]{1,0:T(8,128)S(1)} fusion(f32[128,1024]{1,0:T(8,128)} %collective-permute-done.13, f32[128,1024]{1,0:T(8,128)} %collective-permute-done.11, f32[128,512]{1,0:T(8,128)S(1)} %bitcast.167, f32[512,1024]{1,0:T(8,128)S(1)} %bitcast.146), kind=kOutput, calls=%fused_computation.5 | convolution fusion | flops 402915328 | bytes 3932160 | tf_op jit(solution)/shard_map/dot_general | solution.py:37
  102.5 1.9 %collective-permute-start.22 = (f32[2,128,256]{2,1,0:T(8,128)S(1)}, f32[2,128,256]{2,1,0:T(8,128)S(1)}, u32[]{:S(2)}, u32[]{:S(2)}) collective-permute-start(f32[2,128,256]{2,1,0:T(8,128)S(1)} %pad_maximum_fusion.7), channel_id=1, source_target_pairs={{0,32},{32,0},{1,33},{33,1},{2,34},{34,2},{3,35},{35,3},{4,36},{36... | collective-permute-start | bytes 786440 | tf_op jit(solution)/shard_map/ppermute | solution.py:19
  104.4 5.2 %collective-permute-done.6 = f32[128,1024]{1,0:T(8,128)S(1)} collective-permute-done((f32[128,1024]{1,0:T(8,128)S(1)}, f32[128,1024]{1,0:T(8,128)S(1)}, u32[]{:S(2)}, u32[]{:S(2)}) %collective-permute-start.6) | collective-permute-done | bytes 524320 | tf_op jit(solution)/shard_map/ppermute | solution.py:14
  109.6 4.3 %collective-permute-done.8 = f32[128,1024]{1,0:T(8,128)S(1)} collective-permute-done((f32[128,1024]{1,0:T(8,128)S(1)}, f32[128,1024]{1,0:T(8,128)S(1)}, u32[]{:S(2)}, u32[]{:S(2)}) %collective-permute-start.8) | collective-permute-done | bytes 524320 | tf_op jit(solution)/shard_map/ppermute | solution.py:14
  115.8 2.1 %collective-permute-start.21 = (f32[2,128,256]{2,1,0:T(8,128)S(1)}, f32[2,128,256]{2,1,0:T(8,128)S(1)}, u32[]{:S(2)}, u32[]{:S(2)}) collective-permute-start(f32[2,128,256]{2,1,0:T(8,128)S(1)} %pad_maximum_fusion.6), channel_id=1, source_target_pairs={{0,32},{32,0},{1,33},{33,1},{2,34},{34,2},{3,35},{35,3},{4,36},{36... | collective-permute-start | bytes 786440 | tf_op jit(solution)/shard_map/ppermute | solution.py:19
  120.9 4.9 %all-to-all-start.1 = ((f32[16,8,8,256]{3,2,1,0:T(8,128)}), f32[16,8,8,256]{3,2,1,0:T(8,128)S(1)}, u32[]{:S(2)}, u32[]{:S(2)}) async-start(f32[16,8,8,256]{3,2,1,0:T(8,128)} %bitcast.61), calls=%async_computation.1 | async-start | bytes 2097152 | tf_op jit(solution)/shard_map/all_to_all | solution.py:142
  125.8 2.2 %collective-permute-start.9 = (f32[2,32,1024]{2,1,0:T(8,128)S(1)}, f32[2,32,1024]{2,1,0:T(8,128)S(1)}, u32[]{:S(2)}, u32[]{:S(2)}) collective-permute-start(f32[2,32,1024]{2,1,0:T(8,128)S(1)} %dynamic-slice_bitcast_fusion.1), channel_id=1, source_target_pairs={{0,4},{4,0},{8,12},{12,8},{16,20},{20,16},{24,28},{28,24},{1,5},{5... | collective-permute-start | bytes 786440 | tf_op jit(solution)/shard_map/ppermute | solution.py:19
  128.1 3.6 %collective-permute-start.14 = (f32[2,32,1024]{2,1,0:T(8,128)S(1)}, f32[2,32,1024]{2,1,0:T(8,128)S(1)}, u32[]{:S(2)}, u32[]{:S(2)}) collective-permute-start(f32[2,32,1024]{2,1,0:T(8,128)S(1)} %dynamic-slice_bitcast_fusion), channel_id=1, source_target_pairs={{0,4},{4,0},{8,12},{12,8},{16,20},{20,16},{24,28},{28,24},{1,5},{5... | collective-permute-start | bytes 786440 | tf_op jit(solution)/shard_map/ppermute | solution.py:19
  131.8 5.1 %collective-permute-done.9 = f32[2,32,1024]{2,1,0:T(8,128)S(1)} collective-permute-done((f32[2,32,1024]{2,1,0:T(8,128)S(1)}, f32[2,32,1024]{2,1,0:T(8,128)S(1)}, u32[]{:S(2)}, u32[]{:S(2)}) %collective-permute-start.9) | collective-permute-done | bytes 262176 | tf_op jit(solution)/shard_map/ppermute | solution.py:19
  137.0 3.5 %collective-permute-start.10 = (f32[32,1024]{1,0:T(8,128)S(1)}, f32[32,1024]{1,0:T(8,128)S(1)}, u32[]{:S(2)}, u32[]{:S(2)}) collective-permute-start(f32[32,1024]{1,0:T(8,128)S(1)} %dynamic-slice_bitcast_fusion.11), channel_id=1, source_target_pairs={{0,8},{4,12},{8,0},{12,4},{16,24},{20,28},{24,16},{28,20},{1,9},{5... | collective-permute-start | bytes 393224 | tf_op jit(solution)/shard_map/ppermute | solution.py:19
  142.3 3.9 %collective-permute-start.15 = (f32[32,1024]{1,0:T(8,128)S(1)}, f32[32,1024]{1,0:T(8,128)S(1)}, u32[]{:S(2)}, u32[]{:S(2)}) collective-permute-start(f32[32,1024]{1,0:T(8,128)S(1)} %dynamic-slice_bitcast_fusion.10), channel_id=1, source_target_pairs={{0,8},{4,12},{8,0},{12,4},{16,24},{20,28},{24,16},{28,20},{1,9},{5... | collective-permute-start | bytes 393224 | tf_op jit(solution)/shard_map/ppermute | solution.py:19
  147.0 6.9 %all-to-all-start.2 = ((f32[16,8,256]{2,1,0:T(8,128)}), f32[16,8,256]{2,1,0:T(8,128)S(1)}, u32[]{:S(2)}, u32[]{:S(2)}) async-start(f32[16,8,256]{2,1,0:T(8,128)} %pad_maximum_fusion.8), calls=%async_computation.2 | async-start | bytes 262144 | tf_op jit(solution)/shard_map/all_to_all | solution.py:144
  154.0 7.3 %collective-permute-start.16 = (f32[32,1024]{1,0:T(8,128)S(1)}, f32[32,1024]{1,0:T(8,128)S(1)}, u32[]{:S(2)}, u32[]{:S(2)}) collective-permute-start(f32[32,1024]{1,0:T(8,128)S(1)} %broadcast_select_fusion), channel_id=1, source_target_pairs={{0,16},{4,20},{8,24},{12,28},{16,0},{20,4},{24,8},{28,12},{1,17},{... | collective-permute-start | bytes 393224 | tf_op jit(solution)/shard_map/ppermute | solution.py:19
  161.2 14.3 %all-to-all-done.2 = f32[16,8,256]{2,1,0:T(8,128)S(1)} async-done(((f32[16,8,256]{2,1,0:T(8,128)}), f32[16,8,256]{2,1,0:T(8,128)S(1)}, u32[]{:S(2)}, u32[]{:S(2)}) %all-to-all-start.2) | async-done | bytes 131104 | tf_op jit(solution)/shard_map/all_to_all | solution.py:144
  176.2 4.1 %all-to-all-start.3 = ((f32[8,8,256]{2,1,0:T(8,128)}), f32[8,8,256]{2,1,0:T(8,128)S(1)}, u32[]{:S(2)}, u32[]{:S(2)}) async-start(f32[8,8,256]{2,1,0:T(8,128)} %broadcast_in_dim.23), calls=%async_computation.3 | async-start | bytes 131072 | tf_op jit(solution)/shard_map/all_to_all | solution.py:24
  181.0 4.9 %all-to-all-done.3 = f32[8,8,256]{2,1,0:T(8,128)S(1)} async-done(((f32[8,8,256]{2,1,0:T(8,128)}), f32[8,8,256]{2,1,0:T(8,128)S(1)}, u32[]{:S(2)}, u32[]{:S(2)}) %all-to-all-start.3) | async-done | bytes 65568 | tf_op jit(solution)/shard_map/all_to_all | solution.py:24
  (96 shorter events, 37.4 us)
Async XLA Ops:
  0.6 39.1 %copy-start.10 = (f32[32,1024]{1,0:T(8,128)S(1)}, f32[32,1024]{1,0:T(8,128)}, u32[]{:S(2)}) copy-start(f32[32,1024]{1,0:T(8,128)} %param.6) | copy-start | bytes 393220
  0.6 34.6 %collective-permute-start.4 = (f32[32,1024]{1,0:T(8,128)}, f32[32,1024]{1,0:T(8,128)S(1)}, u32[]{:S(2)}, u32[]{:S(2)}) collective-permute-start(f32[32,1024]{1,0:T(8,128)} %param.6), channel_id=1, source_target_pairs={{0,256},{256,0},{1,257},{257,1},{2,258},{258,2},{3,259},{259,3},{4... | collective-permute-start | bytes 393224 | tf_op jit(solution)/shard_map/ppermute | solution.py:19
  14.7 25.1 %collective-permute-start.17 = (f32[1,32,1024]{2,1,0:T(8,128)}, f32[1,32,1024]{2,1,0:T(8,128)S(1)}, u32[]{:S(2)}, u32[]{:S(2)}) collective-permute-start(f32[1,32,1024]{2,1,0:T(8,128)} %bitcast.168), channel_id=1, source_target_pairs={{0,16},{4,20},{8,24},{12,28},{16,0},{20,4},{24,8},{28,12},{1,17},{... | collective-permute-start | bytes 393224 | tf_op jit(solution)/shard_map/ppermute | solution.py:19
  19.0 24.9 %collective-permute-start.1 = (f32[32,1024]{1,0:T(8,128)}, f32[32,1024]{1,0:T(8,128)}, u32[]{:S(2)}, u32[]{:S(2)}) collective-permute-start(f32[32,1024]{1,0:T(8,128)} %param.6), channel_id=1, source_target_pairs={{0,128},{64,192},{128,0},{192,64},{1,129},{65,193},{129,1},{193,65... | collective-permute-start | bytes 393224 | tf_op jit(solution)/shard_map/ppermute | solution.py:14
  24.1 19.8 %collective-permute-start.2 = (f32[32,1024]{1,0:T(8,128)}, f32[32,1024]{1,0:T(8,128)}, u32[]{:S(2)}, u32[]{:S(2)}) collective-permute-start(f32[32,1024]{1,0:T(8,128)} %param.6), channel_id=1, source_target_pairs={{0,64},{64,128},{128,192},{192,0},{1,65},{65,129},{129,193},{193,1... | collective-permute-start | bytes 393224 | tf_op jit(solution)/shard_map/ppermute | solution.py:14
  26.7 17.2 %collective-permute-start = (f32[32,1024]{1,0:T(8,128)}, f32[32,1024]{1,0:T(8,128)}, u32[]{:S(2)}, u32[]{:S(2)}) collective-permute-start(f32[32,1024]{1,0:T(8,128)} %param.6), channel_id=1, source_target_pairs={{0,192},{64,0},{128,64},{192,128},{1,193},{65,1},{129,65},{193,129... | collective-permute-start | bytes 393224 | tf_op jit(solution)/shard_map/ppermute | solution.py:14
  36.1 11.7 %copy-start = (f32[2,512,512]{2,1,0:T(8,128)S(1)}, f32[2,512,512]{2,1,0:T(8,128)}, u32[]{:S(2)}) copy-start(f32[2,512,512]{2,1,0:T(8,128)} %param.4) | copy-start | bytes 6291460
  36.2 13.2 %all-to-all-start = ((f32[4,32,1024]{2,1,0:T(8,128)}), f32[4,32,1024]{2,1,0:T(8,128)S(1)}, u32[]{:S(2)}, u32[]{:S(2)}) async-start(f32[4,32,1024]{2,1,0:T(8,128)} %broadcast_in_dim.21), calls=%async_computation | async-start | bytes 1048576 | tf_op jit(solution)/shard_map/all_to_all | solution.py:24
  40.5 13.8 %collective-permute-start.18 = (f32[2,32,1024]{2,1,0:T(8,128)}, f32[2,32,1024]{2,1,0:T(8,128)}, u32[]{:S(2)}, u32[]{:S(2)}) collective-permute-start(f32[2,32,1024]{2,1,0:T(8,128)} %maximum_bitcast_fusion), channel_id=1, source_target_pairs={{0,8},{4,12},{8,0},{12,4},{16,24},{20,28},{24,16},{28,20},{1,9},{5... | collective-permute-start | bytes 786440 | tf_op jit(solution)/shard_map/ppermute | solution.py:19
  45.9 14.0 %collective-permute-start.3 = (f32[4,32,1024]{2,1,0:T(8,128)}, f32[4,32,1024]{2,1,0:T(8,128)}, u32[]{:S(2)}, u32[]{:S(2)}) collective-permute-start(f32[4,32,1024]{2,1,0:T(8,128)} %pad_maximum_fusion.4), channel_id=1, source_target_pairs={{0,32},{32,0},{1,33},{33,1},{2,34},{34,2},{3,35},{35,3},{4,36},{36... | collective-permute-start | bytes 1572872 | tf_op jit(solution)/shard_map/ppermute | solution.py:19
  49.3 11.7 %collective-permute-start.5 = (f32[4,32,1024]{2,1,0:T(8,128)S(1)}, f32[4,32,1024]{2,1,0:T(8,128)S(1)}, u32[]{:S(2)}, u32[]{:S(2)}) collective-permute-start(f32[4,32,1024]{2,1,0:T(8,128)S(1)} %all-to-all-done), channel_id=1, source_target_pairs={{0,32},{32,0},{1,33},{33,1},{2,34},{34,2},{3,35},{35,3},{4,36},{36... | collective-permute-start | bytes 1572872 | tf_op jit(solution)/shard_map/ppermute | solution.py:19
  55.4 32.2 %collective-permute-start.19 = (f32[4,32,1024]{2,1,0:T(8,128)S(1)}, f32[4,32,1024]{2,1,0:T(8,128)S(1)}, u32[]{:S(2)}, u32[]{:S(2)}) collective-permute-start(f32[4,32,1024]{2,1,0:T(8,128)S(1)} %bitcast.159), channel_id=1, source_target_pairs={{0,4},{4,0},{8,12},{12,8},{16,20},{20,16},{24,28},{28,24},{1,5},{5... | collective-permute-start | bytes 1572872 | tf_op jit(solution)/shard_map/ppermute | solution.py:19
  65.7 8.3 %copy-start.3 = (f32[1,4,1,32,512]{4,3,2,1,0:T(8,128)S(1)}, f32[1,4,1,32,512]{4,3,2,1,0:T(8,128)}, u32[]{:S(2)}) copy-start(f32[1,4,1,32,512]{4,3,2,1,0:T(8,128)} %get-tuple-element.12) | copy-start | bytes 786436
  65.7 15.4 %collective-permute-start.12 = (f32[128,1024]{1,0:T(8,128)S(1)}, f32[128,1024]{1,0:T(8,128)S(1)}, u32[]{:S(2)}, u32[]{:S(2)}) collective-permute-start(f32[128,1024]{1,0:T(8,128)S(1)} %fusion.25), channel_id=1, source_target_pairs={{0,3},{1,0},{2,1},{3,2},{4,7},{5,4},{6,5},{7,6},{8,11},{9,8},{10,9... | collective-permute-start | bytes 1572872 | tf_op jit(solution)/shard_map/ppermute | solution.py:14
  72.1 23.2 %collective-permute-start.7 = (f32[128,1024]{1,0:T(8,128)}, f32[128,1024]{1,0:T(8,128)}, u32[]{:S(2)}, u32[]{:S(2)}) collective-permute-start(f32[128,1024]{1,0:T(8,128)} %fusion.23), channel_id=1, source_target_pairs={{0,1},{1,2},{2,3},{3,0},{4,5},{5,6},{6,7},{7,4},{8,9},{9,10},{10,1... | collective-permute-start | bytes 1572872 | tf_op jit(solution)/shard_map/ppermute | solution.py:14
  75.5 24.8 %collective-permute-start.11 = (f32[128,1024]{1,0:T(8,128)}, f32[128,1024]{1,0:T(8,128)}, u32[]{:S(2)}, u32[]{:S(2)}) collective-permute-start(f32[128,1024]{1,0:T(8,128)} %fusion.24), channel_id=1, source_target_pairs={{0,1},{1,2},{2,3},{3,0},{4,5},{5,6},{6,7},{7,4},{8,9},{9,10},{10,1... | collective-permute-start | bytes 1572872 | tf_op jit(solution)/shard_map/ppermute | solution.py:14
  82.0 18.4 %collective-permute-start.13 = (f32[128,1024]{1,0:T(8,128)}, f32[128,1024]{1,0:T(8,128)}, u32[]{:S(2)}, u32[]{:S(2)}) collective-permute-start(f32[128,1024]{1,0:T(8,128)} %add.186), channel_id=1, source_target_pairs={{0,3},{1,0},{2,1},{3,2},{4,7},{5,4},{6,5},{7,6},{8,11},{9,8},{10,9... | collective-permute-start | bytes 1572872 | tf_op jit(solution)/shard_map/ppermute | solution.py:14
  90.7 27.3 %collective-permute-start.20 = (f32[2,512,256]{2,1,0:T(8,128)S(1)}, f32[2,512,256]{2,1,0:T(8,128)S(1)}, u32[]{:S(2)}, u32[]{:S(2)}) collective-permute-start(f32[2,512,256]{2,1,0:T(8,128)S(1)} %bitcast.152), channel_id=1, source_target_pairs={{0,32},{32,0},{1,33},{33,1},{2,34},{34,2},{3,35},{35,3},{4,36},{36... | collective-permute-start | bytes 3145736 | tf_op jit(solution)/shard_map/ppermute | solution.py:19
  93.4 16.2 %collective-permute-start.6 = (f32[128,1024]{1,0:T(8,128)S(1)}, f32[128,1024]{1,0:T(8,128)S(1)}, u32[]{:S(2)}, u32[]{:S(2)}) collective-permute-start(f32[128,1024]{1,0:T(8,128)S(1)} %fusion.20), channel_id=1, source_target_pairs={{0,3},{1,0},{2,1},{3,2},{4,7},{5,4},{6,5},{7,6},{8,11},{9,8},{10,9... | collective-permute-start | bytes 1572872 | tf_op jit(solution)/shard_map/ppermute | solution.py:14
  96.4 17.4 %collective-permute-start.8 = (f32[128,1024]{1,0:T(8,128)S(1)}, f32[128,1024]{1,0:T(8,128)S(1)}, u32[]{:S(2)}, u32[]{:S(2)}) collective-permute-start(f32[128,1024]{1,0:T(8,128)S(1)} %add.175), channel_id=1, source_target_pairs={{0,1},{1,2},{2,3},{3,0},{4,5},{5,6},{6,7},{7,4},{8,9},{9,10},{10,1... | collective-permute-start | bytes 1572872 | tf_op jit(solution)/shard_map/ppermute | solution.py:14
  100.4 13.5 %copy-start.8 = (f32[1,4,1,32,512]{4,3,2,1,0:T(8,128)S(1)}, f32[1,4,1,32,512]{4,3,2,1,0:T(8,128)}, u32[]{:S(2)}) copy-start(f32[1,4,1,32,512]{4,3,2,1,0:T(8,128)} %get-tuple-element.10) | copy-start | bytes 786436
  102.5 15.5 %collective-permute-start.22 = (f32[2,128,256]{2,1,0:T(8,128)S(1)}, f32[2,128,256]{2,1,0:T(8,128)S(1)}, u32[]{:S(2)}, u32[]{:S(2)}) collective-permute-start(f32[2,128,256]{2,1,0:T(8,128)S(1)} %pad_maximum_fusion.7), channel_id=1, source_target_pairs={{0,32},{32,0},{1,33},{33,1},{2,34},{34,2},{3,35},{35,3},{4,36},{36... | collective-permute-start | bytes 786440 | tf_op jit(solution)/shard_map/ppermute | solution.py:19
  115.8 3.4 %collective-permute-start.21 = (f32[2,128,256]{2,1,0:T(8,128)S(1)}, f32[2,128,256]{2,1,0:T(8,128)S(1)}, u32[]{:S(2)}, u32[]{:S(2)}) collective-permute-start(f32[2,128,256]{2,1,0:T(8,128)S(1)} %pad_maximum_fusion.6), channel_id=1, source_target_pairs={{0,32},{32,0},{1,33},{33,1},{2,34},{34,2},{3,35},{35,3},{4,36},{36... | collective-permute-start | bytes 786440 | tf_op jit(solution)/shard_map/ppermute | solution.py:19
  120.9 25.3 %all-to-all-start.1 = ((f32[16,8,8,256]{3,2,1,0:T(8,128)}), f32[16,8,8,256]{3,2,1,0:T(8,128)S(1)}, u32[]{:S(2)}, u32[]{:S(2)}) async-start(f32[16,8,8,256]{3,2,1,0:T(8,128)} %bitcast.61), calls=%async_computation.1 | async-start | bytes 2097152 | tf_op jit(solution)/shard_map/all_to_all | solution.py:142
  125.8 11.1 %collective-permute-start.9 = (f32[2,32,1024]{2,1,0:T(8,128)S(1)}, f32[2,32,1024]{2,1,0:T(8,128)S(1)}, u32[]{:S(2)}, u32[]{:S(2)}) collective-permute-start(f32[2,32,1024]{2,1,0:T(8,128)S(1)} %dynamic-slice_bitcast_fusion.1), channel_id=1, source_target_pairs={{0,4},{4,0},{8,12},{12,8},{16,20},{20,16},{24,28},{28,24},{1,5},{5... | collective-permute-start | bytes 786440 | tf_op jit(solution)/shard_map/ppermute | solution.py:19
  128.1 14.1 %collective-permute-start.14 = (f32[2,32,1024]{2,1,0:T(8,128)S(1)}, f32[2,32,1024]{2,1,0:T(8,128)S(1)}, u32[]{:S(2)}, u32[]{:S(2)}) collective-permute-start(f32[2,32,1024]{2,1,0:T(8,128)S(1)} %dynamic-slice_bitcast_fusion), channel_id=1, source_target_pairs={{0,4},{4,0},{8,12},{12,8},{16,20},{20,16},{24,28},{28,24},{1,5},{5... | collective-permute-start | bytes 786440 | tf_op jit(solution)/shard_map/ppermute | solution.py:19
  137.0 49.0 %copy-start.11 = (f32[32,512]{1,0:T(8,128)S(1)}, f32[32,512]{1,0:T(8,128)}, u32[]{:S(2)}) copy-start(f32[32,512]{1,0:T(8,128)} %param.7) | copy-start | bytes 196612
  137.0 16.9 %collective-permute-start.10 = (f32[32,1024]{1,0:T(8,128)S(1)}, f32[32,1024]{1,0:T(8,128)S(1)}, u32[]{:S(2)}, u32[]{:S(2)}) collective-permute-start(f32[32,1024]{1,0:T(8,128)S(1)} %dynamic-slice_bitcast_fusion.11), channel_id=1, source_target_pairs={{0,8},{4,12},{8,0},{12,4},{16,24},{20,28},{24,16},{28,20},{1,9},{5... | collective-permute-start | bytes 393224 | tf_op jit(solution)/shard_map/ppermute | solution.py:19
  142.3 11.6 %collective-permute-start.15 = (f32[32,1024]{1,0:T(8,128)S(1)}, f32[32,1024]{1,0:T(8,128)S(1)}, u32[]{:S(2)}, u32[]{:S(2)}) collective-permute-start(f32[32,1024]{1,0:T(8,128)S(1)} %dynamic-slice_bitcast_fusion.10), channel_id=1, source_target_pairs={{0,8},{4,12},{8,0},{12,4},{16,24},{20,28},{24,16},{28,20},{1,9},{5... | collective-permute-start | bytes 393224 | tf_op jit(solution)/shard_map/ppermute | solution.py:19
  147.0 28.6 %all-to-all-start.2 = ((f32[16,8,256]{2,1,0:T(8,128)}), f32[16,8,256]{2,1,0:T(8,128)S(1)}, u32[]{:S(2)}, u32[]{:S(2)}) async-start(f32[16,8,256]{2,1,0:T(8,128)} %pad_maximum_fusion.8), calls=%async_computation.2 | async-start | bytes 262144 | tf_op jit(solution)/shard_map/all_to_all | solution.py:144
  154.0 26.4 %collective-permute-start.16 = (f32[32,1024]{1,0:T(8,128)S(1)}, f32[32,1024]{1,0:T(8,128)S(1)}, u32[]{:S(2)}, u32[]{:S(2)}) collective-permute-start(f32[32,1024]{1,0:T(8,128)S(1)} %broadcast_select_fusion), channel_id=1, source_target_pairs={{0,16},{4,20},{8,24},{12,28},{16,0},{20,4},{24,8},{28,12},{1,17},{... | collective-permute-start | bytes 393224 | tf_op jit(solution)/shard_map/ppermute | solution.py:19
  176.2 9.8 %all-to-all-start.3 = ((f32[8,8,256]{2,1,0:T(8,128)}), f32[8,8,256]{2,1,0:T(8,128)S(1)}, u32[]{:S(2)}, u32[]{:S(2)}) async-start(f32[8,8,256]{2,1,0:T(8,128)} %broadcast_in_dim.23), calls=%async_computation.3 | async-start | bytes 131072 | tf_op jit(solution)/shard_map/all_to_all | solution.py:24
  (7 other events, 28.5 us)

commit v6 on v3

--- a/solution.py
+++ b/solution.py
@@ -40,20 +40,12 @@
 def gathered_column(panel):
     c = lax.axis_index("c")
     zh = lax.axis_index("zh")
-    y = lax.axis_index("y")
     far = swap(panel, "zh", 1)
-    got = [panel]
-    for k in (1, 2, 3):
-        got.append(shift(panel, "y", -k))
-    near = []
-    for i in range(4):
-        away = (i - y) % 4
-        near.append(jnp.where(away < 2, jnp.where(away < 1, got[0], got[1]), jnp.where(away < 3, got[2], got[3])))
-    near = jnp.stack(near)
-    far = spread(far, "y")
-    near = ordered(near, swap(near, "c", 1), c, 1)
-    far = ordered(far, swap(far, "c", 1), c, 1)
-    return ordered(near, far, zh, 0)
+    both = jnp.concatenate([jnp.broadcast_to(r, (4, *r.shape)) for r in (panel, far)], axis=1)
+    both = lax.all_to_all(both, "y", 0, 0, tiled=True).reshape(4, 2, *panel.shape)
+    both = ordered(both, swap(both, "c", 1), c, 2)
+    low = zh == 0
+    return jnp.stack([jnp.where(low, both[:, 0], both[:, 1]), jnp.where(low, both[:, 1], both[:, 0])])
 
 
 def gathered_over_zl(rows):
@@ -79,21 +71,24 @@
     slots, block = inverse_tiles.shape[:2]
     tiles = inverse_tiles.reshape(slots, 4, 4, block // 16, block)
     column = column.reshape(block, -1)
+    left = {}
+    for d in range(4):
+        part = pick(tiles, (x + d) % 4, 2)
+        for i in range(2):
+            rows = jnp.where(codes[0] == i, part[0], jnp.where(codes[1] == i, part[1], 0.0))
+            left[d, i] = rows.reshape(block // 4, block)
 
     def product(d, i):
-        part = pick(tiles, (x + d) % 4, 2)
-        left = jnp.where(codes[0] == i, part[0], jnp.where(codes[1] == i, part[1], 0.0))
-        return dot(left.reshape(block // 4, block), column)
+        return dot(left[d, i], column)
 
     up_a = shift(product(2, 0), "x", 1)
     down_a = shift(product(2, 1), "x", -1)
     up_b = shift(product(1, 1), "x", 1)
     down_b = shift(product(3, 0), "x", -1)
-    rest = [product(*di) for di in ((1, 0), (3, 1), (0, 0), (0, 1))]
-    rest = lax.optimization_barrier(rest)
+    rest = lax.optimization_barrier([product(1, 0), product(3, 1)])
     up_c = shift(rest[0] + up_a, "x", 1)
     down_c = shift(rest[1] + down_a, "x", -1)
-    return rest[2] + down_b + up_c, rest[3] + up_b + down_c
+    return product(0, 0) + down_b + up_c, product(0, 1) + up_b + down_c
 
 
 def local(inverse_tiles, tile_rows, panel, pivot_base):
@@ -121,9 +116,9 @@
     w = [own[j] + dot(other_u[j], other_t[j]) for j in range(2)]
     w = jnp.concatenate([x.reshape(16, 4, 8, half) for x in w], axis=1)
     w = lax.all_to_all(w, ("y", "x"), 0, 0, tiled=True).sum(axis=0)
-    w = jnp.concatenate([w, w])
-    w = lax.all_to_all(w, ("zh", "zl"), 0, 0, tiled=True).sum(axis=0)
-    w = spread(w, ("y", "c"))
+    w = lax.all_to_all(w, "zl", 0, 0, tiled=True).sum(axis=0)
+    w = spread(w, PROW)
+    w = w[:8] + w[8:]
     w = w.reshape(4, 2, 8, half).transpose(0, 2, 1, 3).reshape(share, block)
     return (-trailing, pivot_base + w)
 

time: 186 us -> 207 us (1.11)
  waiting for transfers between devices: 37.7 us -> 55 us
  starting transfers between devices: 110 us -> 118 us
  other arithmetic: 14.8 us -> 12.2 us
    ppermute x11 -> x10, waiting for transfers between devices: 9.17 us -> 37.5 us  [swap(): return lax.ppermute(x, axis, [(i, i ^ bit) for i in range(n)])]
    ppermute x11 -> x10, starting transfers between devices: 51.7 us -> 69 us  [swap(): return lax.ppermute(x, axis, [(i, i ^ bit) for i in range(n)])]
    ppermute x9 -> x6, starting transfers between devices: 27.7 us -> 18 us  [shift(): return lax.ppermute(x, axis, [(i, (i + by) % n) for i in range(n)])]
    all_to_all x1, waiting for transfers between devices: 9.23 us -> 0.01 us  [local(): w = lax.all_to_all(w, ('y', 'x'), 0, 0, tiled=True).sum(axis=0)]
    all_to_all x1 -> x2, waiting for transfers between devices: 4.7 us -> 10 us  [the longest x1 9.85 us: local(): w = lax.all_to_all(w, 'zl', 0, 0, tiled=True).sum(axis=0)]
    all_to_all x2 -> x1, waiting for transfers between devices: 4.2 us -> 0.01 us  [spread(): return lax.all_to_all(copies, axes, 0, 0, tiled=True)]
    ppermute x9 -> x6, waiting for transfers between devices: 10.4 us -> 7.35 us  [shift(): return lax.ppermute(x, axis, [(i, (i + by) % n) for i in range(n)])]
    add x2 -> x1, other arithmetic: 2.58 us -> 0.01 us  [local(): w = w[:8] + w[8:]]
  transfers between devices with their start and end apart: 24 -> 20, of which waited for: 10 -> 9; matrix products, arithmetic and copies ran while one was open for 15% -> 12% of each run, Pallas kernels for 0% -> 0%
where the time goes in v6:
time: 207 us; the launch traced here: 206 us
  starting transfers between devices  118 us (57%)
  waiting for transfers between devices  55 us (27%)
  other arithmetic  12.2 us (6%)
  matrix products  11.5 us (6%)
  local copies, waits for them, and re-layouts  5.35 us (3%)
  between operations  3.92 us (2%)
    ppermute x10, starting transfers between devices, swap(): return lax.ppermute(x, axis, [(i, i ^ bit) for i in range(n)])  69 us
    ppermute x10, waiting for transfers between devices, swap(): return lax.ppermute(x, axis, [(i, i ^ bit) for i in range(n)])  37.5 us
    ppermute x6, starting transfers between devices, shift(): return lax.ppermute(x, axis, [(i, (i + by) % n) for i in range(n)])  18 us
    all_to_all x1, starting transfers between devices, spread(): return lax.all_to_all(copies, axes, 0, 0, tiled=True)  16.7 us
    dot_general x12, matrix products, dot(): return jnp.dot(a, b, precision=HIGH, preferred_element_type=jnp.float32)  11.5 us
    all_to_all x1, waiting for transfers between devices, local(): w = lax.all_to_all(w, 'zl', 0, 0, tiled=True).sum(axis=0)  9.85 us
    ppermute x6, waiting for transfers between devices, shift(): return lax.ppermute(x, axis, [(i, (i + by) % n) for i in range(n)])  7.35 us
    all_to_all x1, starting transfers between devices, local(): w = lax.all_to_all(w, 'zl', 0, 0, tiled=True).sum(axis=0)  5.06 us
  transfers between devices with their start and end apart: 20, of which 9 were waited for; matrix products, arithmetic and copies ran while one was open for 12% of the time, Pallas kernels for 0%

profile of v6, /device:TPU:1, one launch (start us, length us, event | category | flops | bytes accessed | tf_op | source)
XLA Modules:
  0.0 205.8 jit_solution(7775128087479641267)
XLA Ops:
  0.6 16.3 %collective-permute-start = (f32[32,1024]{1,0:T(8,128)}, f32[32,1024]{1,0:T(8,128)S(1)}, u32[]{:S(2)}, u32[]{:S(2)}) collective-permute-start(f32[32,1024]{1,0:T(8,128)} %param.6), channel_id=1, source_target_pairs={{0,256},{256,0},{1,257},{257,1},{2,258},{258,2},{3,259},{259,3},{4... | collective-permute-start | bytes 393224 | tf_op jit(solution)/shard_map/ppermute | solution.py:19
  16.9 2.9 %collective-permute-done = f32[32,1024]{1,0:T(8,128)S(1)} collective-permute-done((f32[32,1024]{1,0:T(8,128)}, f32[32,1024]{1,0:T(8,128)S(1)}, u32[]{:S(2)}, u32[]{:S(2)}) %collective-permute-start) | collective-permute-done | bytes 131104 | tf_op jit(solution)/shard_map/ppermute | solution.py:19
  21.8 4.9 %all-to-all-start = ((f32[4,64,1024]{2,1,0:T(8,128)}), f32[4,64,1024]{2,1,0:T(8,128)S(1)}, u32[]{:S(2)}, u32[]{:S(2)}) async-start(f32[4,64,1024]{2,1,0:T(8,128)} %pad_maximum_fusion.3), calls=%async_computation | async-start | bytes 2097152 | tf_op jit(solution)/shard_map/all_to_all | solution.py:45
  26.7 12.1 %collective-permute-start.11 = (f32[1,32,1024]{2,1,0:T(8,128)S(1)}, f32[1,32,1024]{2,1,0:T(8,128)}, u32[]{:S(2)}, u32[]{:S(2)}) collective-permute-start(f32[1,32,1024]{2,1,0:T(8,128)S(1)} %bitcast.157), channel_id=1, source_target_pairs={{0,16},{4,20},{8,24},{12,28},{16,0},{20,4},{24,8},{28,12},{1,17},{... | collective-permute-start | bytes 393224 | tf_op jit(solution)/shard_map/ppermute | solution.py:19
  39.0 5.6 %collective-permute-start.1 = (f32[4,2,32,1024]{3,2,1,0:T(8,128)S(1)}, f32[4,2,32,1024]{3,2,1,0:T(8,128)}, u32[]{:S(2)}, u32[]{:S(2)}) collective-permute-start(f32[4,2,32,1024]{3,2,1,0:T(8,128)S(1)} %bitcast.136), channel_id=1, source_target_pairs={{0,32},{32,0},{1,33},{33,1},{2,34},{34,2},{3,35},{35,3},{4,36},{36... | collective-permute-start | bytes 3145736 | tf_op jit(solution)/shard_map/ppermute | solution.py:19
  46.4 5.9 %collective-permute-start.12 = (f32[2,32,1024]{2,1,0:T(8,128)}, f32[2,32,1024]{2,1,0:T(8,128)}, u32[]{:S(2)}, u32[]{:S(2)}) collective-permute-start(f32[2,32,1024]{2,1,0:T(8,128)} %maximum_bitcast_fusion), channel_id=1, source_target_pairs={{0,8},{4,12},{8,0},{12,4},{16,24},{20,28},{24,16},{28,20},{1,9},{5... | collective-permute-start | bytes 786440 | tf_op jit(solution)/shard_map/ppermute | solution.py:19
  56.6 2.6 %collective-permute-done.12 = f32[2,32,1024]{2,1,0:T(8,128)} collective-permute-done((f32[2,32,1024]{2,1,0:T(8,128)}, f32[2,32,1024]{2,1,0:T(8,128)}, u32[]{:S(2)}, u32[]{:S(2)}) %collective-permute-start.12) | collective-permute-done | bytes 262176 | tf_op jit(solution)/shard_map/ppermute | solution.py:19
  60.3 9.1 %collective-permute-start.13 = (f32[4,32,1024]{2,1,0:T(8,128)S(1)}, f32[4,32,1024]{2,1,0:T(8,128)S(1)}, u32[]{:S(2)}, u32[]{:S(2)}) collective-permute-start(f32[4,32,1024]{2,1,0:T(8,128)S(1)} %bitcast.146), channel_id=1, source_target_pairs={{0,4},{4,0},{8,12},{12,8},{16,20},{20,16},{24,28},{28,24},{1,5},{5... | collective-permute-start | bytes 1572872 | tf_op jit(solution)/shard_map/ppermute | solution.py:19
  69.4 1.4 select_bitcast_fusion.2
  72.5 3.1 %collective-permute-start.3 = (f32[128,1024]{1,0:T(8,128)S(1)}, f32[128,1024]{1,0:T(8,128)S(1)}, u32[]{:S(2)}, u32[]{:S(2)}) collective-permute-start(f32[128,1024]{1,0:T(8,128)S(1)} %fusion.23), channel_id=1, source_target_pairs={{0,1},{1,2},{2,3},{3,0},{4,5},{5,6},{6,7},{7,4},{8,9},{9,10},{10,1... | collective-permute-start | bytes 1572872 | tf_op jit(solution)/shard_map/ppermute | solution.py:14
  77.9 3.4 %collective-permute-start.6 = (f32[128,1024]{1,0:T(8,128)S(1)}, f32[128,1024]{1,0:T(8,128)S(1)}, u32[]{:S(2)}, u32[]{:S(2)}) collective-permute-start(f32[128,1024]{1,0:T(8,128)S(1)} %fusion.25), channel_id=1, source_target_pairs={{0,3},{1,0},{2,1},{3,2},{4,7},{5,4},{6,5},{7,6},{8,11},{9,8},{10,9... | collective-permute-start | bytes 1572872 | tf_op jit(solution)/shard_map/ppermute | solution.py:14
  81.3 1.6 fusion.20
  82.8 3.2 %collective-permute-start.2 = (f32[128,1024]{1,0:T(8,128)}, f32[128,1024]{1,0:T(8,128)}, u32[]{:S(2)}, u32[]{:S(2)}) collective-permute-start(f32[128,1024]{1,0:T(8,128)} %fusion.20), channel_id=1, source_target_pairs={{0,3},{1,0},{2,1},{3,2},{4,7},{5,4},{6,5},{7,6},{8,11},{9,8},{10,9... | collective-permute-start | bytes 1572872 | tf_op jit(solution)/shard_map/ppermute | solution.py:14
  86.0 1.9 collective-permute-done.3
  88.8 1.9 collective-permute-start.4
  90.7 1.5 fusion.24
  92.3 3.1 %collective-permute-start.5 = (f32[128,1024]{1,0:T(8,128)}, f32[128,1024]{1,0:T(8,128)}, u32[]{:S(2)}, u32[]{:S(2)}) collective-permute-start(f32[128,1024]{1,0:T(8,128)} %fusion.24), channel_id=1, source_target_pairs={{0,1},{1,2},{2,3},{3,0},{4,5},{5,6},{6,7},{7,4},{8,9},{9,10},{10,1... | collective-permute-start | bytes 1572872 | tf_op jit(solution)/shard_map/ppermute | solution.py:14
  96.2 3.4 %collective-permute-start.7 = (f32[128,1024]{1,0:T(8,128)}, f32[128,1024]{1,0:T(8,128)}, u32[]{:S(2)}, u32[]{:S(2)}) collective-permute-start(f32[128,1024]{1,0:T(8,128)} %add.147), channel_id=1, source_target_pairs={{0,3},{1,0},{2,1},{3,2},{4,7},{5,4},{6,5},{7,6},{8,11},{9,8},{10,9... | collective-permute-start | bytes 1572872 | tf_op jit(solution)/shard_map/ppermute | solution.py:14
  102.6 4.9 %collective-permute-start.14 = (f32[2,512,256]{2,1,0:T(8,128)S(1)}, f32[2,512,256]{2,1,0:T(8,128)S(1)}, u32[]{:S(2)}, u32[]{:S(2)}) collective-permute-start(f32[2,512,256]{2,1,0:T(8,128)S(1)} %bitcast.138), channel_id=1, source_target_pairs={{0,32},{32,0},{1,33},{33,1},{2,34},{34,2},{3,35},{35,3},{4,36},{36... | collective-permute-start | bytes 3145736 | tf_op jit(solution)/shard_map/ppermute | solution.py:19
  107.6 1.9 fusion.1
  109.5 5.4 %collective-permute-done.5 = f32[128,1024]{1,0:T(8,128)} collective-permute-done((f32[128,1024]{1,0:T(8,128)}, f32[128,1024]{1,0:T(8,128)}, u32[]{:S(2)}, u32[]{:S(2)}) %collective-permute-start.5) | collective-permute-done | bytes 524320 | tf_op jit(solution)/shard_map/ppermute | solution.py:14
  114.9 1.9 fusion
  117.0 4.8 %collective-permute-start.15 = (f32[2,256,256]{2,1,0:T(8,128)S(1)}, f32[2,256,256]{2,1,0:T(8,128)S(1)}, u32[]{:S(2)}, u32[]{:S(2)}) collective-permute-start(f32[2,256,256]{2,1,0:T(8,128)S(1)} %pad_maximum_fusion.7), channel_id=1, source_target_pairs={{0,32},{32,0},{1,33},{33,1},{2,34},{34,2},{3,35},{35,3},{4,36},{36... | collective-permute-start | bytes 1572872 | tf_op jit(solution)/shard_map/ppermute | solution.py:19
  125.1 4.2 %all-to-all-start.1 = ((f32[16,8,8,256]{3,2,1,0:T(8,128)}), f32[16,8,8,256]{3,2,1,0:T(8,128)S(1)}, u32[]{:S(2)}, u32[]{:S(2)}) async-start(f32[16,8,8,256]{3,2,1,0:T(8,128)} %pad_maximum_fusion.5), calls=%async_computation.1 | async-start | bytes 2097152 | tf_op jit(solution)/shard_map/all_to_all | solution.py:118
  129.3 1.9 collective-permute-start.8
  131.3 12.7 %collective-permute-done.8 = f32[2,2,32,1024]{3,2,1,0:T(8,128)S(1)} collective-permute-done((f32[2,2,32,1024]{3,2,1,0:T(8,128)S(1)}, f32[2,2,32,1024]{3,2,1,0:T(8,128)S(1)}, u32[]{:S(2)}, u32[]{:S(2)}) %collective-permute-start.8) | collective-permute-done | bytes 524320 | tf_op jit(solution)/shard_map/ppermute | solution.py:19
  144.2 5.0 %collective-permute-start.9 = (f32[2,32,1024]{2,1,0:T(8,128)S(1)}, f32[2,32,1024]{2,1,0:T(8,128)S(1)}, u32[]{:S(2)}, u32[]{:S(2)}) collective-permute-start(f32[2,32,1024]{2,1,0:T(8,128)S(1)} %dynamic-slice_bitcast_fusion.1), channel_id=1, source_target_pairs={{0,8},{4,12},{8,0},{12,4},{16,24},{20,28},{24,16},{28,20},{1,9},{5... | collective-permute-start | bytes 786440 | tf_op jit(solution)/shard_map/ppermute | solution.py:19
  149.9 5.1 %all-to-all-start.2 = ((f32[8,8,256]{2,1,0:T(8,128)}), f32[8,8,256]{2,1,0:T(8,128)S(1)}, u32[]{:S(2)}, u32[]{:S(2)}) async-start(f32[8,8,256]{2,1,0:T(8,128)} %reduce_sum.18), calls=%async_computation.2 | async-start | bytes 131072 | tf_op jit(solution)/shard_map/all_to_all | solution.py:119
  155.0 9.9 %all-to-all-done.2 = f32[8,8,256]{2,1,0:T(8,128)S(1)} async-done(((f32[8,8,256]{2,1,0:T(8,128)}), f32[8,8,256]{2,1,0:T(8,128)S(1)}, u32[]{:S(2)}, u32[]{:S(2)}) %all-to-all-start.2) | async-done | bytes 65568 | tf_op jit(solution)/shard_map/all_to_all | solution.py:119
  165.5 16.7 %all-to-all-start.3 = ((f32[16,8,256]{2,1,0:T(8,128)}), f32[16,8,256]{2,1,0:T(8,128)S(1)}, u32[]{:S(2)}, u32[]{:S(2)}) async-start(f32[16,8,256]{2,1,0:T(8,128)} %broadcast_in_dim.27), calls=%async_computation.3 | async-start | bytes 262144 | tf_op jit(solution)/shard_map/all_to_all | solution.py:24
  182.3 3.4 %collective-permute-start.10 = (f32[32,1024]{1,0:T(8,128)S(1)}, f32[32,1024]{1,0:T(8,128)S(1)}, u32[]{:S(2)}, u32[]{:S(2)}) collective-permute-start(f32[32,1024]{1,0:T(8,128)S(1)} %dynamic-slice_bitcast_fusion.2), channel_id=1, source_target_pairs={{0,16},{4,20},{8,24},{12,28},{16,0},{20,4},{24,8},{28,12},{1,17},{... | collective-permute-start | bytes 393224 | tf_op jit(solution)/shard_map/ppermute | solution.py:19
  185.7 18.8 %collective-permute-done.10 = f32[32,1024]{1,0:T(8,128)S(1)} collective-permute-done((f32[32,1024]{1,0:T(8,128)S(1)}, f32[32,1024]{1,0:T(8,128)S(1)}, u32[]{:S(2)}, u32[]{:S(2)}) %collective-permute-start.10) | collective-permute-done | bytes 131104 | tf_op jit(solution)/shard_map/ppermute | solution.py:19
  (68 shorter events, 21.5 us)
Async XLA Ops:
  0.6 19.1 %collective-permute-start = (f32[32,1024]{1,0:T(8,128)}, f32[32,1024]{1,0:T(8,128)S(1)}, u32[]{:S(2)}, u32[]{:S(2)}) collective-permute-start(f32[32,1024]{1,0:T(8,128)} %param.6), channel_id=1, source_target_pairs={{0,256},{256,0},{1,257},{257,1},{2,258},{258,2},{3,259},{259,3},{4... | collective-permute-start | bytes 393224 | tf_op jit(solution)/shard_map/ppermute | solution.py:19
  20.8 5.9 %copy-start.3 = (f32[32,1024]{1,0:T(8,128)S(1)}, f32[32,1024]{1,0:T(8,128)}, u32[]{:S(2)}) copy-start(f32[32,1024]{1,0:T(8,128)} %param.6) | copy-start | bytes 393220
  21.8 30.4 %copy-start.5 = (s32[2,1]{0,1:T(1,128)S(1)}, s32[2,1]{0,1:T(1,128)}, u32[]{:S(2)}) copy-start(s32[2,1]{0,1:T(1,128)} %param.5) | copy-start | bytes 28
  21.8 33.7 %copy-start = (f32[2,512,512]{2,1,0:T(8,128)S(1)}, f32[2,512,512]{2,1,0:T(8,128)}, u32[]{:S(2)}) copy-start(f32[2,512,512]{2,1,0:T(8,128)} %param.4) | copy-start | bytes 6291460
  21.8 17.2 %all-to-all-start = ((f32[4,64,1024]{2,1,0:T(8,128)}), f32[4,64,1024]{2,1,0:T(8,128)S(1)}, u32[]{:S(2)}, u32[]{:S(2)}) async-start(f32[4,64,1024]{2,1,0:T(8,128)} %pad_maximum_fusion.3), calls=%async_computation | async-start | bytes 2097152 | tf_op jit(solution)/shard_map/all_to_all | solution.py:45
  26.7 18.0 %collective-permute-start.11 = (f32[1,32,1024]{2,1,0:T(8,128)S(1)}, f32[1,32,1024]{2,1,0:T(8,128)}, u32[]{:S(2)}, u32[]{:S(2)}) collective-permute-start(f32[1,32,1024]{2,1,0:T(8,128)S(1)} %bitcast.157), channel_id=1, source_target_pairs={{0,16},{4,20},{8,24},{12,28},{16,0},{20,4},{24,8},{28,12},{1,17},{... | collective-permute-start | bytes 393224 | tf_op jit(solution)/shard_map/ppermute | solution.py:19
  39.0 30.4 %collective-permute-start.1 = (f32[4,2,32,1024]{3,2,1,0:T(8,128)S(1)}, f32[4,2,32,1024]{3,2,1,0:T(8,128)}, u32[]{:S(2)}, u32[]{:S(2)}) collective-permute-start(f32[4,2,32,1024]{3,2,1,0:T(8,128)S(1)} %bitcast.136), channel_id=1, source_target_pairs={{0,32},{32,0},{1,33},{33,1},{2,34},{34,2},{3,35},{35,3},{4,36},{36... | collective-permute-start | bytes 3145736 | tf_op jit(solution)/shard_map/ppermute | solution.py:19
  46.4 12.9 %collective-permute-start.12 = (f32[2,32,1024]{2,1,0:T(8,128)}, f32[2,32,1024]{2,1,0:T(8,128)}, u32[]{:S(2)}, u32[]{:S(2)}) collective-permute-start(f32[2,32,1024]{2,1,0:T(8,128)} %maximum_bitcast_fusion), channel_id=1, source_target_pairs={{0,8},{4,12},{8,0},{12,4},{16,24},{20,28},{24,16},{28,20},{1,9},{5... | collective-permute-start | bytes 786440 | tf_op jit(solution)/shard_map/ppermute | solution.py:19
  60.3 39.3 %collective-permute-start.13 = (f32[4,32,1024]{2,1,0:T(8,128)S(1)}, f32[4,32,1024]{2,1,0:T(8,128)S(1)}, u32[]{:S(2)}, u32[]{:S(2)}) collective-permute-start(f32[4,32,1024]{2,1,0:T(8,128)S(1)} %bitcast.146), channel_id=1, source_target_pairs={{0,4},{4,0},{8,12},{12,8},{16,20},{20,16},{24,28},{28,24},{1,5},{5... | collective-permute-start | bytes 1572872 | tf_op jit(solution)/shard_map/ppermute | solution.py:19
  72.5 15.4 %collective-permute-start.3 = (f32[128,1024]{1,0:T(8,128)S(1)}, f32[128,1024]{1,0:T(8,128)S(1)}, u32[]{:S(2)}, u32[]{:S(2)}) collective-permute-start(f32[128,1024]{1,0:T(8,128)S(1)} %fusion.23), channel_id=1, source_target_pairs={{0,1},{1,2},{2,3},{3,0},{4,5},{5,6},{6,7},{7,4},{8,9},{9,10},{10,1... | collective-permute-start | bytes 1572872 | tf_op jit(solution)/shard_map/ppermute | solution.py:14
  77.9 17.5 %collective-permute-start.6 = (f32[128,1024]{1,0:T(8,128)S(1)}, f32[128,1024]{1,0:T(8,128)S(1)}, u32[]{:S(2)}, u32[]{:S(2)}) collective-permute-start(f32[128,1024]{1,0:T(8,128)S(1)} %fusion.25), channel_id=1, source_target_pairs={{0,3},{1,0},{2,1},{3,2},{4,7},{5,4},{6,5},{7,6},{8,11},{9,8},{10,9... | collective-permute-start | bytes 1572872 | tf_op jit(solution)/shard_map/ppermute | solution.py:14
  82.8 24.7 %collective-permute-start.2 = (f32[128,1024]{1,0:T(8,128)}, f32[128,1024]{1,0:T(8,128)}, u32[]{:S(2)}, u32[]{:S(2)}) collective-permute-start(f32[128,1024]{1,0:T(8,128)} %fusion.20), channel_id=1, source_target_pairs={{0,3},{1,0},{2,1},{3,2},{4,7},{5,4},{6,5},{7,6},{8,11},{9,8},{10,9... | collective-permute-start | bytes 1572872 | tf_op jit(solution)/shard_map/ppermute | solution.py:14
  88.8 18.7 %collective-permute-start.4 = (f32[128,1024]{1,0:T(8,128)}, f32[128,1024]{1,0:T(8,128)}, u32[]{:S(2)}, u32[]{:S(2)}) collective-permute-start(f32[128,1024]{1,0:T(8,128)} %add.144), channel_id=1, source_target_pairs={{0,1},{1,2},{2,3},{3,0},{4,5},{5,6},{6,7},{7,4},{8,9},{9,10},{10,1... | collective-permute-start | bytes 1572872 | tf_op jit(solution)/shard_map/ppermute | solution.py:14
  92.3 22.7 %collective-permute-start.5 = (f32[128,1024]{1,0:T(8,128)}, f32[128,1024]{1,0:T(8,128)}, u32[]{:S(2)}, u32[]{:S(2)}) collective-permute-start(f32[128,1024]{1,0:T(8,128)} %fusion.24), channel_id=1, source_target_pairs={{0,1},{1,2},{2,3},{3,0},{4,5},{5,6},{6,7},{7,4},{8,9},{9,10},{10,1... | collective-permute-start | bytes 1572872 | tf_op jit(solution)/shard_map/ppermute | solution.py:14
  96.2 18.7 %collective-permute-start.7 = (f32[128,1024]{1,0:T(8,128)}, f32[128,1024]{1,0:T(8,128)}, u32[]{:S(2)}, u32[]{:S(2)}) collective-permute-start(f32[128,1024]{1,0:T(8,128)} %add.147), channel_id=1, source_target_pairs={{0,3},{1,0},{2,1},{3,2},{4,7},{5,4},{6,5},{7,6},{8,11},{9,8},{10,9... | collective-permute-start | bytes 1572872 | tf_op jit(solution)/shard_map/ppermute | solution.py:14
  99.9 7.6 %copy-start.2 = (f32[1,4,1,32,512]{4,3,2,1,0:T(8,128)S(1)}, f32[1,4,1,32,512]{4,3,2,1,0:T(8,128)}, u32[]{:S(2)}) copy-start(f32[1,4,1,32,512]{4,3,2,1,0:T(8,128)} %get-tuple-element.10) | copy-start | bytes 786436
  102.6 12.3 %copy-start.1 = (f32[1,4,1,32,512]{4,3,2,1,0:T(8,128)S(1)}, f32[1,4,1,32,512]{4,3,2,1,0:T(8,128)}, u32[]{:S(2)}) copy-start(f32[1,4,1,32,512]{4,3,2,1,0:T(8,128)} %get-tuple-element.14) | copy-start | bytes 786436
  102.6 20.0 %collective-permute-start.14 = (f32[2,512,256]{2,1,0:T(8,128)S(1)}, f32[2,512,256]{2,1,0:T(8,128)S(1)}, u32[]{:S(2)}, u32[]{:S(2)}) collective-permute-start(f32[2,512,256]{2,1,0:T(8,128)S(1)} %bitcast.138), channel_id=1, source_target_pairs={{0,32},{32,0},{1,33},{33,1},{2,34},{34,2},{3,35},{35,3},{4,36},{36... | collective-permute-start | bytes 3145736 | tf_op jit(solution)/shard_map/ppermute | solution.py:19
  117.0 6.3 %collective-permute-start.15 = (f32[2,256,256]{2,1,0:T(8,128)S(1)}, f32[2,256,256]{2,1,0:T(8,128)S(1)}, u32[]{:S(2)}, u32[]{:S(2)}) collective-permute-start(f32[2,256,256]{2,1,0:T(8,128)S(1)} %pad_maximum_fusion.7), channel_id=1, source_target_pairs={{0,32},{32,0},{1,33},{33,1},{2,34},{34,2},{3,35},{35,3},{4,36},{36... | collective-permute-start | bytes 1572872 | tf_op jit(solution)/shard_map/ppermute | solution.py:19
  125.1 24.1 %all-to-all-start.1 = ((f32[16,8,8,256]{3,2,1,0:T(8,128)}), f32[16,8,8,256]{3,2,1,0:T(8,128)S(1)}, u32[]{:S(2)}, u32[]{:S(2)}) async-start(f32[16,8,8,256]{3,2,1,0:T(8,128)} %pad_maximum_fusion.5), calls=%async_computation.1 | async-start | bytes 2097152 | tf_op jit(solution)/shard_map/all_to_all | solution.py:118
  129.3 14.7 %collective-permute-start.8 = (f32[2,2,32,1024]{3,2,1,0:T(8,128)S(1)}, f32[2,2,32,1024]{3,2,1,0:T(8,128)S(1)}, u32[]{:S(2)}, u32[]{:S(2)}) collective-permute-start(f32[2,2,32,1024]{3,2,1,0:T(8,128)S(1)} %dynamic-slice_bitcast_fusion), channel_id=1, source_target_pairs={{0,4},{4,0},{8,12},{12,8},{16,20},{20,16},{24,28},{28,24},{1,5},{5... | collective-permute-start | bytes 1572872 | tf_op jit(solution)/shard_map/ppermute | solution.py:19
  144.1 61.0 %copy-start.4 = (f32[32,512]{1,0:T(8,128)S(1)}, f32[32,512]{1,0:T(8,128)}, u32[]{:S(2)}) copy-start(f32[32,512]{1,0:T(8,128)} %param.7) | copy-start | bytes 196612
  144.2 38.0 %collective-permute-start.9 = (f32[2,32,1024]{2,1,0:T(8,128)S(1)}, f32[2,32,1024]{2,1,0:T(8,128)S(1)}, u32[]{:S(2)}, u32[]{:S(2)}) collective-permute-start(f32[2,32,1024]{2,1,0:T(8,128)S(1)} %dynamic-slice_bitcast_fusion.1), channel_id=1, source_target_pairs={{0,8},{4,12},{8,0},{12,4},{16,24},{20,28},{24,16},{28,20},{1,9},{5... | collective-permute-start | bytes 786440 | tf_op jit(solution)/shard_map/ppermute | solution.py:19
  149.9 14.9 %all-to-all-start.2 = ((f32[8,8,256]{2,1,0:T(8,128)}), f32[8,8,256]{2,1,0:T(8,128)S(1)}, u32[]{:S(2)}, u32[]{:S(2)}) async-start(f32[8,8,256]{2,1,0:T(8,128)} %reduce_sum.18), calls=%async_computation.2 | async-start | bytes 131072 | tf_op jit(solution)/shard_map/all_to_all | solution.py:119
  165.5 39.6 %all-to-all-start.3 = ((f32[16,8,256]{2,1,0:T(8,128)}), f32[16,8,256]{2,1,0:T(8,128)S(1)}, u32[]{:S(2)}, u32[]{:S(2)}) async-start(f32[16,8,256]{2,1,0:T(8,128)} %broadcast_in_dim.27), calls=%async_computation.3 | async-start | bytes 262144 | tf_op jit(solution)/shard_map/all_to_all | solution.py:24
  182.3 22.1 %collective-permute-start.10 = (f32[32,1024]{1,0:T(8,128)S(1)}, f32[32,1024]{1,0:T(8,128)S(1)}, u32[]{:S(2)}, u32[]{:S(2)}) collective-permute-start(f32[32,1024]{1,0:T(8,128)S(1)} %dynamic-slice_bitcast_fusion.2), channel_id=1, source_target_pairs={{0,16},{4,20},{8,24},{12,28},{16,0},{20,4},{24,8},{28,12},{1,17},{... | collective-permute-start | bytes 393224 | tf_op jit(solution)/shard_map/ppermute | solution.py:19

commit v7 on v6

--- a/solution.py
+++ b/solution.py
@@ -60,10 +60,18 @@
 
 def reduced_over_zl(t):
     zl = lax.axis_index("zl")
-    for bit, axis in ((1, 2), (2, 1), (4, 0)):
-        mine = (zl // bit) % 2
-        t = pick(t, mine, axis) + swap(pick(t, 1 - mine, axis), "zl", bit)
-    return t
+    low, mid, high = zl % 2, (zl // 2) % 2, zl // 4
+    t = pick(t, low, 2) + swap(pick(t, 1 - low, 2), "zl", 1)
+
+    def part(flip_high, flip_mid):
+        first = (high ^ flip_high, mid ^ flip_mid, 0, 0)
+        return lax.dynamic_slice(t, first, (1, 1, *t.shape[2:]))[0, 0]
+
+    got = []
+    for flips in ((1, 1), (1, 0), (0, 1)):
+        bit = flips[0] * 4 + flips[1] * 2
+        got.append(swap(part(*flips), "zl", bit))
+    return part(0, 0) + got[0] + got[1] + got[2]
 
 
 def reduced_products(inverse_tiles, codes, column):
@@ -116,9 +124,9 @@
     w = [own[j] + dot(other_u[j], other_t[j]) for j in range(2)]
     w = jnp.concatenate([x.reshape(16, 4, 8, half) for x in w], axis=1)
     w = lax.all_to_all(w, ("y", "x"), 0, 0, tiled=True).sum(axis=0)
-    w = lax.all_to_all(w, "zl", 0, 0, tiled=True).sum(axis=0)
-    w = spread(w, PROW)
-    w = w[:8] + w[8:]
+    w = jnp.concatenate([w, w])
+    w = lax.all_to_all(w, ("zh", "zl"), 0, 0, tiled=True).sum(axis=0)
+    w = spread(w, ("y", "c"))
     w = w.reshape(4, 2, 8, half).transpose(0, 2, 1, 3).reshape(share, block)
     return (-trailing, pivot_base + w)
 

time: 207 us -> 199 us (0.961)
  waiting for transfers between devices: 55 us -> 37.6 us
  matrix products: 11.5 us -> 15.7 us
  starting transfers between devices: 118 us -> 122 us
    ppermute x10 -> x11, waiting for transfers between devices: 37.5 us -> 15.9 us  [swap(): return lax.ppermute(x, axis, [(i, i ^ bit) for i in range(n)])]
    all_to_all x1, waiting for transfers between devices: 0.01 us -> 15.1 us  [local(): w = lax.all_to_all(w, ('y', 'x'), 0, 0, tiled=True).sum(axis=0)]
    all_to_all x1, starting transfers between devices: 16.7 us -> 6.68 us  [spread(): return lax.all_to_all(copies, axes, 0, 0, tiled=True)]
    all_to_all x1, waiting for transfers between devices: 9.85 us -> 0.01 us  [local(): w = lax.all_to_all(w, ('zh', 'zl'), 0, 0, tiled=True).sum(axis=0)]
    all_to_all x1, starting transfers between devices: 5.06 us -> 14.3 us  [local(): w = lax.all_to_all(w, ('zh', 'zl'), 0, 0, tiled=True).sum(axis=0)]
    ppermute x10 -> x11, starting transfers between devices: 69 us -> 73.8 us  [swap(): return lax.ppermute(x, axis, [(i, i ^ bit) for i in range(n)])]
    dot_general x12, matrix products: 11.5 us -> 15.7 us  [dot(): return jnp.dot(a, b, precision=HIGH, preferred_element_type=jnp.float32)]
  transfers between devices with their start and end apart: 20 -> 21, of which waited for: 9 -> 8; matrix products, arithmetic and copies ran while one was open for 12% -> 14% of each run, Pallas kernels for 0% -> 0%
where the time goes in v7:
time: 199 us; the launch traced here: 197 us
  starting transfers between devices  122 us (61%)
  waiting for transfers between devices  37.6 us (19%)
  matrix products  15.7 us (8%)
  other arithmetic  12.2 us (6%)
  local copies, waits for them, and re-layouts  6.29 us (3%)
  between operations  3.93 us (2%)
    ppermute x11, starting transfers between devices, swap(): return lax.ppermute(x, axis, [(i, i ^ bit) for i in range(n)])  73.8 us
    ppermute x6, starting transfers between devices, shift(): return lax.ppermute(x, axis, [(i, (i + by) % n) for i in range(n)])  18 us
    ppermute x11, waiting for transfers between devices, swap(): return lax.ppermute(x, axis, [(i, i ^ bit) for i in range(n)])  15.9 us
    dot_general x12, matrix products, dot(): return jnp.dot(a, b, precision=HIGH, preferred_element_type=jnp.float32)  15.7 us
    all_to_all x1, waiting for transfers between devices, local(): w = lax.all_to_all(w, ('y', 'x'), 0, 0, tiled=True).sum(axis=0)  15.1 us
    all_to_all x1, starting transfers between devices, local(): w = lax.all_to_all(w, ('zh', 'zl'), 0, 0, tiled=True).sum(axis=0)  14.3 us
    all_to_all x1, starting transfers between devices, spread(): return lax.all_to_all(copies, axes, 0, 0, tiled=True)  6.68 us
    ppermute x6, waiting for transfers between devices, shift(): return lax.ppermute(x, axis, [(i, (i + by) % n) for i in range(n)])  6.38 us
  transfers between devices with their start and end apart: 21, of which 8 were waited for; matrix products, arithmetic and copies ran while one was open for 14% of the time, Pallas kernels for 0%

profile of v7, /device:TPU:1, one launch (start us, length us, event | category | flops | bytes accessed | tf_op | source)
XLA Modules:
  0.0 197.5 jit_solution(8144649025021123850)
XLA Ops:
  0.6 16.3 %collective-permute-start = (f32[32,1024]{1,0:T(8,128)}, f32[32,1024]{1,0:T(8,128)S(1)}, u32[]{:S(2)}, u32[]{:S(2)}) collective-permute-start(f32[32,1024]{1,0:T(8,128)} %param.6), channel_id=1, source_target_pairs={{0,256},{256,0},{1,257},{257,1},{2,258},{258,2},{3,259},{259,3},{4... | collective-permute-start | bytes 393224 | tf_op jit(solution)/shard_map/ppermute | solution.py:19
  16.9 2.9 %collective-permute-done = f32[32,1024]{1,0:T(8,128)S(1)} collective-permute-done((f32[32,1024]{1,0:T(8,128)}, f32[32,1024]{1,0:T(8,128)S(1)}, u32[]{:S(2)}, u32[]{:S(2)}) %collective-permute-start) | collective-permute-done | bytes 131104 | tf_op jit(solution)/shard_map/ppermute | solution.py:19
  21.8 4.9 %all-to-all-start = ((f32[4,64,1024]{2,1,0:T(8,128)}), f32[4,64,1024]{2,1,0:T(8,128)S(1)}, u32[]{:S(2)}, u32[]{:S(2)}) async-start(f32[4,64,1024]{2,1,0:T(8,128)} %pad_maximum_fusion.3), calls=%async_computation | async-start | bytes 2097152 | tf_op jit(solution)/shard_map/all_to_all | solution.py:45
  26.7 12.1 %collective-permute-start.12 = (f32[1,32,1024]{2,1,0:T(8,128)S(1)}, f32[1,32,1024]{2,1,0:T(8,128)}, u32[]{:S(2)}, u32[]{:S(2)}) collective-permute-start(f32[1,32,1024]{2,1,0:T(8,128)S(1)} %bitcast.158), channel_id=1, source_target_pairs={{0,16},{4,20},{8,24},{12,28},{16,0},{20,4},{24,8},{28,12},{1,17},{... | collective-permute-start | bytes 393224 | tf_op jit(solution)/shard_map/ppermute | solution.py:19
  39.0 5.6 %collective-permute-start.1 = (f32[4,2,32,1024]{3,2,1,0:T(8,128)S(1)}, f32[4,2,32,1024]{3,2,1,0:T(8,128)}, u32[]{:S(2)}, u32[]{:S(2)}) collective-permute-start(f32[4,2,32,1024]{3,2,1,0:T(8,128)S(1)} %bitcast.140), channel_id=1, source_target_pairs={{0,32},{32,0},{1,33},{33,1},{2,34},{34,2},{3,35},{35,3},{4,36},{36... | collective-permute-start | bytes 3145736 | tf_op jit(solution)/shard_map/ppermute | solution.py:19
  46.4 5.9 %collective-permute-start.13 = (f32[2,32,1024]{2,1,0:T(8,128)}, f32[2,32,1024]{2,1,0:T(8,128)}, u32[]{:S(2)}, u32[]{:S(2)}) collective-permute-start(f32[2,32,1024]{2,1,0:T(8,128)} %maximum_bitcast_fusion), channel_id=1, source_target_pairs={{0,8},{4,12},{8,0},{12,4},{16,24},{20,28},{24,16},{28,20},{1,9},{5... | collective-permute-start | bytes 786440 | tf_op jit(solution)/shard_map/ppermute | solution.py:19
  56.6 2.6 %collective-permute-done.13 = f32[2,32,1024]{2,1,0:T(8,128)} collective-permute-done((f32[2,32,1024]{2,1,0:T(8,128)}, f32[2,32,1024]{2,1,0:T(8,128)}, u32[]{:S(2)}, u32[]{:S(2)}) %collective-permute-start.13) | collective-permute-done | bytes 262176 | tf_op jit(solution)/shard_map/ppermute | solution.py:19
  60.3 9.1 %collective-permute-start.14 = (f32[4,32,1024]{2,1,0:T(8,128)S(1)}, f32[4,32,1024]{2,1,0:T(8,128)S(1)}, u32[]{:S(2)}, u32[]{:S(2)}) collective-permute-start(f32[4,32,1024]{2,1,0:T(8,128)S(1)} %bitcast.147), channel_id=1, source_target_pairs={{0,4},{4,0},{8,12},{12,8},{16,20},{20,16},{24,28},{28,24},{1,5},{5... | collective-permute-start | bytes 1572872 | tf_op jit(solution)/shard_map/ppermute | solution.py:19
  72.5 3.1 %collective-permute-start.3 = (f32[128,1024]{1,0:T(8,128)S(1)}, f32[128,1024]{1,0:T(8,128)S(1)}, u32[]{:S(2)}, u32[]{:S(2)}) collective-permute-start(f32[128,1024]{1,0:T(8,128)S(1)} %fusion.25), channel_id=1, source_target_pairs={{0,1},{1,2},{2,3},{3,0},{4,5},{5,6},{6,7},{7,4},{8,9},{9,10},{10,1... | collective-permute-start | bytes 1572872 | tf_op jit(solution)/shard_map/ppermute | solution.py:14
  77.9 3.4 %collective-permute-start.6 = (f32[128,1024]{1,0:T(8,128)S(1)}, f32[128,1024]{1,0:T(8,128)S(1)}, u32[]{:S(2)}, u32[]{:S(2)}) collective-permute-start(f32[128,1024]{1,0:T(8,128)S(1)} %fusion.27), channel_id=1, source_target_pairs={{0,3},{1,0},{2,1},{3,2},{4,7},{5,4},{6,5},{7,6},{8,11},{9,8},{10,9... | collective-permute-start | bytes 1572872 | tf_op jit(solution)/shard_map/ppermute | solution.py:14
  81.3 1.5 fusion.22
  82.8 3.2 %collective-permute-start.2 = (f32[128,1024]{1,0:T(8,128)}, f32[128,1024]{1,0:T(8,128)}, u32[]{:S(2)}, u32[]{:S(2)}) collective-permute-start(f32[128,1024]{1,0:T(8,128)} %fusion.22), channel_id=1, source_target_pairs={{0,3},{1,0},{2,1},{3,2},{4,7},{5,4},{6,5},{7,6},{8,11},{9,8},{10,9... | collective-permute-start | bytes 1572872 | tf_op jit(solution)/shard_map/ppermute | solution.py:14
  86.0 1.9 collective-permute-done.3
  88.8 1.9 collective-permute-start.4
  92.2 3.1 %collective-permute-start.5 = (f32[128,1024]{1,0:T(8,128)}, f32[128,1024]{1,0:T(8,128)}, u32[]{:S(2)}, u32[]{:S(2)}) collective-permute-start(f32[128,1024]{1,0:T(8,128)} %fusion.26), channel_id=1, source_target_pairs={{0,1},{1,2},{2,3},{3,0},{4,5},{5,6},{6,7},{7,4},{8,9},{9,10},{10,1... | collective-permute-start | bytes 1572872 | tf_op jit(solution)/shard_map/ppermute | solution.py:14
  96.2 3.4 %collective-permute-start.7 = (f32[128,1024]{1,0:T(8,128)}, f32[128,1024]{1,0:T(8,128)}, u32[]{:S(2)}, u32[]{:S(2)}) collective-permute-start(f32[128,1024]{1,0:T(8,128)} %add.143), channel_id=1, source_target_pairs={{0,3},{1,0},{2,1},{3,2},{4,7},{5,4},{6,5},{7,6},{8,11},{9,8},{10,9... | collective-permute-start | bytes 1572872 | tf_op jit(solution)/shard_map/ppermute | solution.py:14
  101.3 2.3 %copy.38 = f32[2,4,4,4,8,256]{5,4,3,2,1,0:T(8,128)} copy(f32[2,4,4,4,8,256]{5,4,1,2,3,0:T(8,128)} %bitcast.145) | data formatting | bytes 2097152 | tf_op jit(solution)/shard_map/transpose | solution.py:110
  103.6 4.9 %collective-permute-start.15 = (f32[2,512,256]{2,1,0:T(8,128)}, f32[2,512,256]{2,1,0:T(8,128)}, u32[]{:S(2)}, u32[]{:S(2)}) collective-permute-start(f32[2,512,256]{2,1,0:T(8,128)} %bitcast.44), channel_id=1, source_target_pairs={{0,32},{32,0},{1,33},{33,1},{2,34},{34,2},{3,35},{35,3},{4,36},{36... | collective-permute-start | bytes 3145736 | tf_op jit(solution)/shard_map/ppermute | solution.py:19
  108.5 1.9 fusion.1
  110.4 4.4 %collective-permute-done.5 = f32[128,1024]{1,0:T(8,128)} collective-permute-done((f32[128,1024]{1,0:T(8,128)}, f32[128,1024]{1,0:T(8,128)}, u32[]{:S(2)}, u32[]{:S(2)}) %collective-permute-start.5) | collective-permute-done | bytes 524320 | tf_op jit(solution)/shard_map/ppermute | solution.py:14
  114.9 1.9 fusion
  116.9 4.8 %collective-permute-start.16 = (f32[2,256,256]{2,1,0:T(8,128)S(1)}, f32[2,256,256]{2,1,0:T(8,128)S(1)}, u32[]{:S(2)}, u32[]{:S(2)}) collective-permute-start(f32[2,256,256]{2,1,0:T(8,128)S(1)} %pad_maximum_fusion.7), channel_id=1, source_target_pairs={{0,32},{32,0},{1,33},{33,1},{2,34},{34,2},{3,35},{35,3},{4,36},{36... | collective-permute-start | bytes 1572872 | tf_op jit(solution)/shard_map/ppermute | solution.py:19
  128.6 4.2 %all-to-all-start.1 = ((f32[16,8,8,256]{3,2,1,0:T(8,128)}), f32[16,8,8,256]{3,2,1,0:T(8,128)S(1)}, u32[]{:S(2)}, u32[]{:S(2)}) async-start(f32[16,8,8,256]{3,2,1,0:T(8,128)} %pad_maximum_fusion.5), calls=%async_computation.1 | async-start | bytes 2097152 | tf_op jit(solution)/shard_map/all_to_all | solution.py:126
  132.9 1.9 collective-permute-start.8
  134.9 15.1 %all-to-all-done.1 = f32[16,8,8,256]{3,2,1,0:T(8,128)S(1)} async-done(((f32[16,8,8,256]{3,2,1,0:T(8,128)}), f32[16,8,8,256]{3,2,1,0:T(8,128)S(1)}, u32[]{:S(2)}, u32[]{:S(2)}) %all-to-all-start.1) | async-done | bytes 1048608 | tf_op jit(solution)/shard_map/all_to_all | solution.py:126
  150.8 14.3 %all-to-all-start.2 = ((f32[16,8,256]{2,1,0:T(8,128)}), f32[16,8,256]{2,1,0:T(8,128)S(1)}, u32[]{:S(2)}, u32[]{:S(2)}) async-start(f32[16,8,256]{2,1,0:T(8,128)} %pad_maximum_fusion.8), calls=%async_computation.2 | async-start | bytes 262144 | tf_op jit(solution)/shard_map/all_to_all | solution.py:128
  165.2 7.2 %collective-permute-start.10 = (f32[32,1024]{1,0:T(8,128)S(1)}, f32[32,1024]{1,0:T(8,128)S(1)}, u32[]{:S(2)}, u32[]{:S(2)}) collective-permute-start(f32[32,1024]{1,0:T(8,128)S(1)} %get-tuple-element.28), channel_id=1, source_target_pairs={{0,16},{4,20},{8,24},{12,28},{16,0},{20,4},{24,8},{28,12},{1,17},{... | collective-permute-start | bytes 393224 | tf_op jit(solution)/shard_map/ppermute | solution.py:19
  172.4 4.0 %collective-permute-start.11 = (f32[32,1024]{1,0:T(8,128)S(1)}, f32[32,1024]{1,0:T(8,128)S(1)}, u32[]{:S(2)}, u32[]{:S(2)}) collective-permute-start(f32[32,1024]{1,0:T(8,128)S(1)} %get-tuple-element.27), channel_id=1, source_target_pairs={{0,8},{4,12},{8,0},{12,4},{16,24},{20,28},{24,16},{28,20},{1,9},{5... | collective-permute-start | bytes 393224 | tf_op jit(solution)/shard_map/ppermute | solution.py:19
  176.4 2.0 %collective-permute-start.9 = (f32[32,1024]{1,0:T(8,128)S(1)}, f32[32,1024]{1,0:T(8,128)S(1)}, u32[]{:S(2)}, u32[]{:S(2)}) collective-permute-start(f32[32,1024]{1,0:T(8,128)S(1)} %get-tuple-element.26), channel_id=1, source_target_pairs={{0,24},{4,28},{8,16},{12,20},{16,8},{20,12},{24,0},{28,4},{1,25},{... | collective-permute-start | bytes 393224 | tf_op jit(solution)/shard_map/ppermute | solution.py:19
  179.1 6.7 %all-to-all-start.3 = ((f32[8,8,256]{2,1,0:T(8,128)}), f32[8,8,256]{2,1,0:T(8,128)S(1)}, u32[]{:S(2)}, u32[]{:S(2)}) async-start(f32[8,8,256]{2,1,0:T(8,128)} %broadcast_in_dim.27), calls=%async_computation.3 | async-start | bytes 131072 | tf_op jit(solution)/shard_map/all_to_all | solution.py:24
  185.8 6.7 %collective-permute-done.10 = f32[32,1024]{1,0:T(8,128)S(1)} collective-permute-done((f32[32,1024]{1,0:T(8,128)S(1)}, f32[32,1024]{1,0:T(8,128)S(1)}, u32[]{:S(2)}, u32[]{:S(2)}) %collective-permute-start.10) | collective-permute-done | bytes 131104 | tf_op jit(solution)/shard_map/ppermute | solution.py:19
  192.5 3.6 %collective-permute-done.9 = f32[32,1024]{1,0:T(8,128)S(1)} collective-permute-done((f32[32,1024]{1,0:T(8,128)S(1)}, f32[32,1024]{1,0:T(8,128)S(1)}, u32[]{:S(2)}, u32[]{:S(2)}) %collective-permute-start.9) | collective-permute-done | bytes 131104 | tf_op jit(solution)/shard_map/ppermute | solution.py:19
  (68 shorter events, 26.6 us)
Async XLA Ops:
  0.6 19.1 %collective-permute-start = (f32[32,1024]{1,0:T(8,128)}, f32[32,1024]{1,0:T(8,128)S(1)}, u32[]{:S(2)}, u32[]{:S(2)}) collective-permute-start(f32[32,1024]{1,0:T(8,128)} %param.6), channel_id=1, source_target_pairs={{0,256},{256,0},{1,257},{257,1},{2,258},{258,2},{3,259},{259,3},{4... | collective-permute-start | bytes 393224 | tf_op jit(solution)/shard_map/ppermute | solution.py:19
  20.8 5.9 %copy-start.3 = (f32[32,1024]{1,0:T(8,128)S(1)}, f32[32,1024]{1,0:T(8,128)}, u32[]{:S(2)}) copy-start(f32[32,1024]{1,0:T(8,128)} %param.6) | copy-start | bytes 393220
  21.8 30.4 %copy-start.5 = (s32[2,1]{0,1:T(1,128)S(1)}, s32[2,1]{0,1:T(1,128)}, u32[]{:S(2)}) copy-start(s32[2,1]{0,1:T(1,128)} %param.5) | copy-start | bytes 28
  21.8 33.7 %copy-start = (f32[2,512,512]{2,1,0:T(8,128)S(1)}, f32[2,512,512]{2,1,0:T(8,128)}, u32[]{:S(2)}) copy-start(f32[2,512,512]{2,1,0:T(8,128)} %param.4) | copy-start | bytes 6291460
  21.8 17.2 %all-to-all-start = ((f32[4,64,1024]{2,1,0:T(8,128)}), f32[4,64,1024]{2,1,0:T(8,128)S(1)}, u32[]{:S(2)}, u32[]{:S(2)}) async-start(f32[4,64,1024]{2,1,0:T(8,128)} %pad_maximum_fusion.3), calls=%async_computation | async-start | bytes 2097152 | tf_op jit(solution)/shard_map/all_to_all | solution.py:45
  26.7 18.0 %collective-permute-start.12 = (f32[1,32,1024]{2,1,0:T(8,128)S(1)}, f32[1,32,1024]{2,1,0:T(8,128)}, u32[]{:S(2)}, u32[]{:S(2)}) collective-permute-start(f32[1,32,1024]{2,1,0:T(8,128)S(1)} %bitcast.158), channel_id=1, source_target_pairs={{0,16},{4,20},{8,24},{12,28},{16,0},{20,4},{24,8},{28,12},{1,17},{... | collective-permute-start | bytes 393224 | tf_op jit(solution)/shard_map/ppermute | solution.py:19
  39.0 30.4 %collective-permute-start.1 = (f32[4,2,32,1024]{3,2,1,0:T(8,128)S(1)}, f32[4,2,32,1024]{3,2,1,0:T(8,128)}, u32[]{:S(2)}, u32[]{:S(2)}) collective-permute-start(f32[4,2,32,1024]{3,2,1,0:T(8,128)S(1)} %bitcast.140), channel_id=1, source_target_pairs={{0,32},{32,0},{1,33},{33,1},{2,34},{34,2},{3,35},{35,3},{4,36},{36... | collective-permute-start | bytes 3145736 | tf_op jit(solution)/shard_map/ppermute | solution.py:19
  46.4 12.9 %collective-permute-start.13 = (f32[2,32,1024]{2,1,0:T(8,128)}, f32[2,32,1024]{2,1,0:T(8,128)}, u32[]{:S(2)}, u32[]{:S(2)}) collective-permute-start(f32[2,32,1024]{2,1,0:T(8,128)} %maximum_bitcast_fusion), channel_id=1, source_target_pairs={{0,8},{4,12},{8,0},{12,4},{16,24},{20,28},{24,16},{28,20},{1,9},{5... | collective-permute-start | bytes 786440 | tf_op jit(solution)/shard_map/ppermute | solution.py:19
  60.3 39.3 %collective-permute-start.14 = (f32[4,32,1024]{2,1,0:T(8,128)S(1)}, f32[4,32,1024]{2,1,0:T(8,128)S(1)}, u32[]{:S(2)}, u32[]{:S(2)}) collective-permute-start(f32[4,32,1024]{2,1,0:T(8,128)S(1)} %bitcast.147), channel_id=1, source_target_pairs={{0,4},{4,0},{8,12},{12,8},{16,20},{20,16},{24,28},{28,24},{1,5},{5... | collective-permute-start | bytes 1572872 | tf_op jit(solution)/shard_map/ppermute | solution.py:19
  72.5 15.4 %collective-permute-start.3 = (f32[128,1024]{1,0:T(8,128)S(1)}, f32[128,1024]{1,0:T(8,128)S(1)}, u32[]{:S(2)}, u32[]{:S(2)}) collective-permute-start(f32[128,1024]{1,0:T(8,128)S(1)} %fusion.25), channel_id=1, source_target_pairs={{0,1},{1,2},{2,3},{3,0},{4,5},{5,6},{6,7},{7,4},{8,9},{9,10},{10,1... | collective-permute-start | bytes 1572872 | tf_op jit(solution)/shard_map/ppermute | solution.py:14
  77.9 17.5 %collective-permute-start.6 = (f32[128,1024]{1,0:T(8,128)S(1)}, f32[128,1024]{1,0:T(8,128)S(1)}, u32[]{:S(2)}, u32[]{:S(2)}) collective-permute-start(f32[128,1024]{1,0:T(8,128)S(1)} %fusion.27), channel_id=1, source_target_pairs={{0,3},{1,0},{2,1},{3,2},{4,7},{5,4},{6,5},{7,6},{8,11},{9,8},{10,9... | collective-permute-start | bytes 1572872 | tf_op jit(solution)/shard_map/ppermute | solution.py:14
  82.8 25.7 %collective-permute-start.2 = (f32[128,1024]{1,0:T(8,128)}, f32[128,1024]{1,0:T(8,128)}, u32[]{:S(2)}, u32[]{:S(2)}) collective-permute-start(f32[128,1024]{1,0:T(8,128)} %fusion.22), channel_id=1, source_target_pairs={{0,3},{1,0},{2,1},{3,2},{4,7},{5,4},{6,5},{7,6},{8,11},{9,8},{10,9... | collective-permute-start | bytes 1572872 | tf_op jit(solution)/shard_map/ppermute | solution.py:14
  88.8 19.7 %collective-permute-start.4 = (f32[128,1024]{1,0:T(8,128)}, f32[128,1024]{1,0:T(8,128)}, u32[]{:S(2)}, u32[]{:S(2)}) collective-permute-start(f32[128,1024]{1,0:T(8,128)} %add.140), channel_id=1, source_target_pairs={{0,1},{1,2},{2,3},{3,0},{4,5},{5,6},{6,7},{7,4},{8,9},{9,10},{10,1... | collective-permute-start | bytes 1572872 | tf_op jit(solution)/shard_map/ppermute | solution.py:14
  92.2 22.7 %collective-permute-start.5 = (f32[128,1024]{1,0:T(8,128)}, f32[128,1024]{1,0:T(8,128)}, u32[]{:S(2)}, u32[]{:S(2)}) collective-permute-start(f32[128,1024]{1,0:T(8,128)} %fusion.26), channel_id=1, source_target_pairs={{0,1},{1,2},{2,3},{3,0},{4,5},{5,6},{6,7},{7,4},{8,9},{9,10},{10,1... | collective-permute-start | bytes 1572872 | tf_op jit(solution)/shard_map/ppermute | solution.py:14
  96.2 18.7 %collective-permute-start.7 = (f32[128,1024]{1,0:T(8,128)}, f32[128,1024]{1,0:T(8,128)}, u32[]{:S(2)}, u32[]{:S(2)}) collective-permute-start(f32[128,1024]{1,0:T(8,128)} %add.143), channel_id=1, source_target_pairs={{0,3},{1,0},{2,1},{3,2},{4,7},{5,4},{6,5},{7,6},{8,11},{9,8},{10,9... | collective-permute-start | bytes 1572872 | tf_op jit(solution)/shard_map/ppermute | solution.py:14
  99.9 8.6 %copy-start.2 = (f32[1,4,1,32,512]{4,3,2,1,0:T(8,128)S(1)}, f32[1,4,1,32,512]{4,3,2,1,0:T(8,128)}, u32[]{:S(2)}) copy-start(f32[1,4,1,32,512]{4,3,2,1,0:T(8,128)} %get-tuple-element.10) | copy-start | bytes 786436
  103.6 11.3 %copy-start.1 = (f32[1,4,1,32,512]{4,3,2,1,0:T(8,128)S(1)}, f32[1,4,1,32,512]{4,3,2,1,0:T(8,128)}, u32[]{:S(2)}) copy-start(f32[1,4,1,32,512]{4,3,2,1,0:T(8,128)} %get-tuple-element.14) | copy-start | bytes 786436
  103.6 21.0 %collective-permute-start.15 = (f32[2,512,256]{2,1,0:T(8,128)}, f32[2,512,256]{2,1,0:T(8,128)}, u32[]{:S(2)}, u32[]{:S(2)}) collective-permute-start(f32[2,512,256]{2,1,0:T(8,128)} %bitcast.44), channel_id=1, source_target_pairs={{0,32},{32,0},{1,33},{33,1},{2,34},{34,2},{3,35},{35,3},{4,36},{36... | collective-permute-start | bytes 3145736 | tf_op jit(solution)/shard_map/ppermute | solution.py:19
  116.9 7.7 %collective-permute-start.16 = (f32[2,256,256]{2,1,0:T(8,128)S(1)}, f32[2,256,256]{2,1,0:T(8,128)S(1)}, u32[]{:S(2)}, u32[]{:S(2)}) collective-permute-start(f32[2,256,256]{2,1,0:T(8,128)S(1)} %pad_maximum_fusion.7), channel_id=1, source_target_pairs={{0,32},{32,0},{1,33},{33,1},{2,34},{34,2},{3,35},{35,3},{4,36},{36... | collective-permute-start | bytes 1572872 | tf_op jit(solution)/shard_map/ppermute | solution.py:19
  128.6 21.5 %all-to-all-start.1 = ((f32[16,8,8,256]{3,2,1,0:T(8,128)}), f32[16,8,8,256]{3,2,1,0:T(8,128)S(1)}, u32[]{:S(2)}, u32[]{:S(2)}) async-start(f32[16,8,8,256]{3,2,1,0:T(8,128)} %pad_maximum_fusion.5), calls=%async_computation.1 | async-start | bytes 2097152 | tf_op jit(solution)/shard_map/all_to_all | solution.py:126
  132.9 32.1 %collective-permute-start.8 = (f32[2,2,32,1024]{3,2,1,0:T(8,128)S(1)}, f32[2,2,32,1024]{3,2,1,0:T(8,128)S(1)}, u32[]{:S(2)}, u32[]{:S(2)}) collective-permute-start(f32[2,2,32,1024]{3,2,1,0:T(8,128)S(1)} %dynamic-slice_bitcast_fusion), channel_id=1, source_target_pairs={{0,4},{4,0},{8,12},{12,8},{16,20},{20,16},{24,28},{28,24},{1,5},{5... | collective-permute-start | bytes 1572872 | tf_op jit(solution)/shard_map/ppermute | solution.py:19
  150.1 46.7 %copy-start.4 = (f32[32,512]{1,0:T(8,128)S(1)}, f32[32,512]{1,0:T(8,128)}, u32[]{:S(2)}) copy-start(f32[32,512]{1,0:T(8,128)} %param.7) | copy-start | bytes 196612
  150.8 27.6 %all-to-all-start.2 = ((f32[16,8,256]{2,1,0:T(8,128)}), f32[16,8,256]{2,1,0:T(8,128)S(1)}, u32[]{:S(2)}, u32[]{:S(2)}) async-start(f32[16,8,256]{2,1,0:T(8,128)} %pad_maximum_fusion.8), calls=%async_computation.2 | async-start | bytes 262144 | tf_op jit(solution)/shard_map/all_to_all | solution.py:128
  165.2 27.3 %collective-permute-start.10 = (f32[32,1024]{1,0:T(8,128)S(1)}, f32[32,1024]{1,0:T(8,128)S(1)}, u32[]{:S(2)}, u32[]{:S(2)}) collective-permute-start(f32[32,1024]{1,0:T(8,128)S(1)} %get-tuple-element.28), channel_id=1, source_target_pairs={{0,16},{4,20},{8,24},{12,28},{16,0},{20,4},{24,8},{28,12},{1,17},{... | collective-permute-start | bytes 393224 | tf_op jit(solution)/shard_map/ppermute | solution.py:19
  172.4 20.1 %collective-permute-start.11 = (f32[32,1024]{1,0:T(8,128)S(1)}, f32[32,1024]{1,0:T(8,128)S(1)}, u32[]{:S(2)}, u32[]{:S(2)}) collective-permute-start(f32[32,1024]{1,0:T(8,128)S(1)} %get-tuple-element.27), channel_id=1, source_target_pairs={{0,8},{4,12},{8,0},{12,4},{16,24},{20,28},{24,16},{28,20},{1,9},{5... | collective-permute-start | bytes 393224 | tf_op jit(solution)/shard_map/ppermute | solution.py:19
  176.4 19.8 %collective-permute-start.9 = (f32[32,1024]{1,0:T(8,128)S(1)}, f32[32,1024]{1,0:T(8,128)S(1)}, u32[]{:S(2)}, u32[]{:S(2)}) collective-permute-start(f32[32,1024]{1,0:T(8,128)S(1)} %get-tuple-element.26), channel_id=1, source_target_pairs={{0,24},{4,28},{8,16},{12,20},{16,8},{20,12},{24,0},{28,4},{1,25},{... | collective-permute-start | bytes 393224 | tf_op jit(solution)/shard_map/ppermute | solution.py:19
  179.1 17.8 %all-to-all-start.3 = ((f32[8,8,256]{2,1,0:T(8,128)}), f32[8,8,256]{2,1,0:T(8,128)S(1)}, u32[]{:S(2)}, u32[]{:S(2)}) async-start(f32[8,8,256]{2,1,0:T(8,128)} %broadcast_in_dim.27), calls=%async_computation.3 | async-start | bytes 131072 | tf_op jit(solution)/shard_map/all_to_all | solution.py:24

commit v8 on v7

--- a/solution.py
+++ b/solution.py
@@ -40,10 +40,19 @@
 def gathered_column(panel):
     c = lax.axis_index("c")
     zh = lax.axis_index("zh")
-    far = swap(panel, "zh", 1)
-    both = jnp.concatenate([jnp.broadcast_to(r, (4, *r.shape)) for r in (panel, far)], axis=1)
-    both = lax.all_to_all(both, "y", 0, 0, tiled=True).reshape(4, 2, *panel.shape)
-    both = ordered(both, swap(both, "c", 1), c, 2)
+    share, width = panel.shape
+    part = width // 4
+
+    def columns(which):
+        first = which * part
+        cuts = [lax.dynamic_slice_in_dim(panel, first + j * 2 * part, part, 1) for j in range(2)]
+        return jnp.concatenate(cuts, axis=1)
+
+    near = ordered(columns(c), swap(columns(1 - c), "c", 1), c, 0)
+    near = near.reshape(2 * share, width // 2)
+    far = swap(near, "zh", 1)
+    both = jnp.concatenate([jnp.broadcast_to(r, (4, *r.shape)) for r in (near, far)], axis=1)
+    both = lax.all_to_all(both, "y", 0, 0, tiled=True).reshape(4, 2, *near.shape)
     low = zh == 0
     return jnp.stack([jnp.where(low, both[:, 0], both[:, 1]), jnp.where(low, both[:, 1], both[:, 0])])
 
@@ -58,17 +67,19 @@
     return rows
 
 
-def reduced_over_zl(t):
+def reduced_over_zl(halves):
     zl = lax.axis_index("zl")
     low, mid, high = zl % 2, (zl // 2) % 2, zl // 4
-    t = pick(t, low, 2) + swap(pick(t, 1 - low, 2), "zl", 1)
+    rows = []
+    for t in halves:
+        rows.append(pick(t, low, 2) + swap(pick(t, 1 - low, 2), "zl", 1))
 
     def part(flip_high, flip_mid):
         first = (high ^ flip_high, mid ^ flip_mid, 0, 0)
-        return lax.dynamic_slice(t, first, (1, 1, *t.shape[2:]))[0, 0]
+        return jnp.stack([lax.dynamic_slice(t, first, (1, 1, *t.shape[2:]))[0, 0] for t in rows])
 
     got = []
-    for flips in ((1, 1), (1, 0), (0, 1)):
+    for flips in ((0, 1), (1, 0), (1, 1)):
         bit = flips[0] * 4 + flips[1] * 2
         got.append(swap(part(*flips), "zl", bit))
     return part(0, 0) + got[0] + got[1] + got[2]
@@ -76,18 +87,23 @@
 
 def reduced_products(inverse_tiles, codes, column):
     x = lax.axis_index("x")
-    slots, block = inverse_tiles.shape[:2]
-    tiles = inverse_tiles.reshape(slots, 4, 4, block // 16, block)
+    block = inverse_tiles.shape[1]
     column = column.reshape(block, -1)
+    first, second = inverse_tiles
+    tiles = [
+        jnp.where(codes[0] == i, first, jnp.where(codes[1] == i, second, 0.0)) for i in range(2)
+    ]
+    tiles = lax.optimization_barrier(jnp.stack(tiles))
+    tiles = (tiles, swap(tiles, "c", 1))
     left = {}
-    for d in range(4):
-        part = pick(tiles, (x + d) % 4, 2)
-        for i in range(2):
-            rows = jnp.where(codes[0] == i, part[0], jnp.where(codes[1] == i, part[1], 0.0))
-            left[d, i] = rows.reshape(block // 4, block)
+    for r in range(2):
+        rows = tiles[r].reshape(2, 4, 4, block // 16, block)
+        rows = [pick(rows, (x + d) % 4, 2).reshape(block // 2, block) for d in range(4)]
+        for d, cut in enumerate(lax.optimization_barrier(rows)):
+            left[d, r] = cut
 
-    def product(d, i):
-        return dot(left[d, i], column)
+    def product(d, r):
+        return dot(left[d, r], column)
 
     up_a = shift(product(2, 0), "x", 1)
     down_a = shift(product(2, 1), "x", -1)
@@ -96,7 +112,8 @@
     rest = lax.optimization_barrier([product(1, 0), product(3, 1)])
     up_c = shift(rest[0] + up_a, "x", 1)
     down_c = shift(rest[1] + down_a, "x", -1)
-    return product(0, 0) + down_b + up_c, product(0, 1) + up_b + down_c
+    first = product(0, 0) + down_b + up_c
+    return first, product(0, 1) + up_b + down_c
 
 
 def local(inverse_tiles, tile_rows, panel, pivot_base):
@@ -110,18 +127,16 @@
     u = u.reshape(2, 4, 4, 4, 8, 8 * share).transpose(0, 3, 2, 1, 4, 5)
     u = lax.optimization_barrier(u.reshape(2, block, 8 * share))
     other_u = swap(u, "c", 1)
-    t = jnp.concatenate(reduced_products(inverse_tiles, codes, column))
-    trailing = reduced_over_zl(t.reshape(2, 2, 2, share, width))
+    t = reduced_products(inverse_tiles, codes, column)
+    trailing = reduced_over_zl([x.reshape(2, 2, 2, share, block) for x in t])
+    other = swap(trailing[1], "c", 1)
+    low, high = ordered(trailing[0], other, c, 0)
+    trailing = [x[:, j * half : (j + 1) * half] for j in range(2) for x in (low, high)]
+    trailing = jnp.concatenate(trailing, axis=1)
 
-    def side(which):
-        first = which * half
-        cut = [lax.dynamic_slice_in_dim(t, first + j * block, half, 1) for j in range(2)]
-        return jnp.stack(cut)
-
-    other_t = swap(side(1 - c), "c", 1)
-    mine = side(c)
-    own = lax.optimization_barrier([dot(u[j], mine[j]) for j in range(2)])
-    w = [own[j] + dot(other_u[j], other_t[j]) for j in range(2)]
+    parts = [[t[r][:, j * half : (j + 1) * half] for j in range(2)] for r in range(2)]
+    own = lax.optimization_barrier([dot(u[j], parts[0][j]) for j in range(2)])
+    w = [own[j] + dot(other_u[j], parts[1][j]) for j in range(2)]
     w = jnp.concatenate([x.reshape(16, 4, 8, half) for x in w], axis=1)
     w = lax.all_to_all(w, ("y", "x"), 0, 0, tiled=True).sum(axis=0)
     w = jnp.concatenate([w, w])

time: 199 us -> 211 us (1.060)
  waiting for transfers between devices: 37.6 us -> 56 us
  starting transfers between devices: 122 us -> 114 us
  local copies, waits for them, and re-layouts: 6.29 us -> 13 us
  matrix products: 15.7 us -> 11 us
    all_to_all x1, waiting for transfers between devices: 15.1 us -> 0.01 us  [local(): w = lax.all_to_all(w, ('y', 'x'), 0, 0, tiled=True).sum(axis=0)]
    ppermute x6, waiting for transfers between devices: 6.38 us -> 20.1 us  [shift(): return lax.ppermute(x, axis, [(i, (i + by) % n) for i in range(n)])]
    all_to_all x1, waiting for transfers between devices: 0.01 us -> 12.3 us  [local(): w = lax.all_to_all(w, ('zh', 'zl'), 0, 0, tiled=True).sum(axis=0)]
    ppermute x11 -> x13, starting transfers between devices: 73.8 us -> 64.6 us  [swap(): return lax.ppermute(x, axis, [(i, i ^ bit) for i in range(n)])]
    all_to_all x1, starting transfers between devices: 4.86 us -> 10.6 us  [gathered_column(): lax.all_to_all(both, 'y', 0, 0, tiled=True).reshape(4, 2, *near.shape)]
    dot_general x12, matrix products: 15.7 us -> 11 us  [dot(): return jnp.dot(a, b, precision=HIGH, preferred_element_type=jnp.float32)]
    all_to_all x1, starting transfers between devices: 14.3 us -> 10.1 us  [local(): w = lax.all_to_all(w, ('zh', 'zl'), 0, 0, tiled=True).sum(axis=0)]
    all_to_all x1, waiting for transfers between devices: 0.01 us -> 4.19 us  [spread(): return lax.all_to_all(copies, axes, 0, 0, tiled=True)]
  transfers between devices with their start and end apart: 21 -> 23, of which waited for: 8 -> 8; matrix products, arithmetic and copies ran while one was open for 14% -> 16% of each run, Pallas kernels for 0% -> 0%
where the time goes in v8:
time: 211 us; the launch traced here: 209 us
  starting transfers between devices  114 us (54%)
  waiting for transfers between devices  56 us (27%)
  local copies, waits for them, and re-layouts  13 us (6%)
  other arithmetic  11.3 us (5%)
  matrix products  11 us (5%)
  between operations  4.03 us (2%)
    ppermute x13, starting transfers between devices, swap(): return lax.ppermute(x, axis, [(i, i ^ bit) for i in range(n)])  64.6 us
    ppermute x6, waiting for transfers between devices, shift(): return lax.ppermute(x, axis, [(i, (i + by) % n) for i in range(n)])  20.1 us
    ppermute x13, waiting for transfers between devices, swap(): return lax.ppermute(x, axis, [(i, i ^ bit) for i in range(n)])  19.4 us
    ppermute x6, starting transfers between devices, shift(): return lax.ppermute(x, axis, [(i, (i + by) % n) for i in range(n)])  17 us
    all_to_all x1, waiting for transfers between devices, local(): w = lax.all_to_all(w, ('zh', 'zl'), 0, 0, tiled=True).sum(axis=0)  12.3 us
    dot_general x12, matrix products, dot(): return jnp.dot(a, b, precision=HIGH, preferred_element_type=jnp.float32)  11 us
    all_to_all x1, starting transfers between devices, gathered_column(): lax.all_to_all(both, 'y', 0, 0, tiled=True).reshape(4, 2, *near.shape)  10.6 us
    all_to_all x1, starting transfers between devices, local(): w = lax.all_to_all(w, ('zh', 'zl'), 0, 0, tiled=True).sum(axis=0)  10.1 us
  transfers between devices with their start and end apart: 23, of which 8 were waited for; matrix products, arithmetic and copies ran while one was open for 16% of the time, Pallas kernels for 0%

profile of v8, /device:TPU:1, one launch (start us, length us, event | category | flops | bytes accessed | tf_op | source)
XLA Modules:
  0.0 209.4 jit_solution(15346030431043668814)
XLA Ops:
  0.6 9.8 %collective-permute-start.15 = (f32[1,32,1024]{2,1,0:T(8,128)}, f32[1,32,1024]{2,1,0:T(8,128)S(1)}, u32[]{:S(2)}, u32[]{:S(2)}) collective-permute-start(f32[1,32,1024]{2,1,0:T(8,128)} %bitcast.166), channel_id=1, source_target_pairs={{0,16},{4,20},{8,24},{12,28},{16,0},{20,4},{24,8},{28,12},{1,17},{... | collective-permute-start | bytes 393224 | tf_op jit(solution)/shard_map/ppermute | solution.py:19
  11.3 2.9 %collective-permute-start = (f32[32,512]{1,0:T(8,128)S(1)}, f32[32,512]{1,0:T(8,128)S(1)}, u32[]{:S(2)}, u32[]{:S(2)}) collective-permute-start(f32[32,512]{1,0:T(8,128)S(1)} %pad_maximum_fusion.12), channel_id=1, source_target_pairs={{0,32},{32,0},{1,33},{33,1},{2,34},{34,2},{3,35},{35,3},{4,36},{36... | collective-permute-start | bytes 196616 | tf_op jit(solution)/shard_map/ppermute | solution.py:19
  19.0 5.5 %collective-permute-start.16 = (f32[2,32,1024]{2,1,0:T(8,128)S(1)}, f32[2,32,1024]{2,1,0:T(8,128)S(1)}, u32[]{:S(2)}, u32[]{:S(2)}) collective-permute-start(f32[2,32,1024]{2,1,0:T(8,128)S(1)} %maximum_bitcast_fusion), channel_id=1, source_target_pairs={{0,8},{4,12},{8,0},{12,4},{16,24},{20,28},{24,16},{28,20},{1,9},{5... | collective-permute-start | bytes 786440 | tf_op jit(solution)/shard_map/ppermute | solution.py:19
  24.6 14.8 %collective-permute-start.1 = (f32[64,512]{1,0:T(8,128)S(1)}, f32[64,512]{1,0:T(8,128)S(1)}, u32[]{:S(2)}, u32[]{:S(2)}) collective-permute-start(f32[64,512]{1,0:T(8,128)S(1)} %bitcast.167), channel_id=1, source_target_pairs={{0,256},{256,0},{1,257},{257,1},{2,258},{258,2},{3,259},{259,3},{4... | collective-permute-start | bytes 393224 | tf_op jit(solution)/shard_map/ppermute | solution.py:19
  40.3 1.9 collective-permute-start.17
  43.8 2.8 %collective-permute-done.1 = f32[64,512]{1,0:T(8,128)S(1)} collective-permute-done((f32[64,512]{1,0:T(8,128)S(1)}, f32[64,512]{1,0:T(8,128)S(1)}, u32[]{:S(2)}, u32[]{:S(2)}) %collective-permute-start.1) | collective-permute-done | bytes 131104 | tf_op jit(solution)/shard_map/ppermute | solution.py:19
  47.8 10.6 %all-to-all-start = ((f32[4,128,512]{2,1,0:T(8,128)}), f32[4,128,512]{2,1,0:T(8,128)S(1)}, u32[]{:S(2)}, u32[]{:S(2)}) async-start(f32[4,128,512]{2,1,0:T(8,128)} %pad_maximum_fusion.1), calls=%async_computation | async-start | bytes 2097152 | tf_op jit(solution)/shard_map/all_to_all | solution.py:55
  60.1 4.8 %collective-permute-start.3 = (f32[2,512,512]{2,1,0:T(8,128)S(1)}, f32[2,512,512]{2,1,0:T(8,128)}, u32[]{:S(2)}, u32[]{:S(2)}) collective-permute-start(f32[2,512,512]{2,1,0:T(8,128)S(1)} %pad_maximum_fusion), channel_id=1, source_target_pairs={{0,32},{32,0},{1,33},{33,1},{2,34},{34,2},{3,35},{35,3},{4,36},{36... | collective-permute-start | bytes 6291464 | tf_op jit(solution)/shard_map/ppermute | solution.py:19
  69.0 2.6 %copy.25 = f32[1024,256]{1,0:T(8,128)} copy(f32[1024,256]{0,1:T(8,128)} %bitcast.154) | data formatting | bytes 2097152 | tf_op jit(solution)/shard_map/transpose | solution.py:126
  71.6 2.4 %copy.26 = f32[2,4,4,4,8,256]{5,4,3,2,1,0:T(8,128)} copy(f32[2,4,4,4,8,256]{5,4,1,2,3,0:T(8,128)} %bitcast.155) | data formatting | bytes 2097152 | tf_op jit(solution)/shard_map/transpose | solution.py:127
  77.7 3.1 %collective-permute-start.4 = (f32[256,512]{1,0:T(8,128)S(1)}, f32[256,512]{1,0:T(8,128)S(1)}, u32[]{:S(2)}, u32[]{:S(2)}) collective-permute-start(f32[256,512]{1,0:T(8,128)S(1)} %fusion.19), channel_id=1, source_target_pairs={{0,1},{1,2},{2,3},{3,0},{4,5},{5,6},{6,7},{7,4},{8,9},{9,10},{10,1... | collective-permute-start | bytes 1572872 | tf_op jit(solution)/shard_map/ppermute | solution.py:14
  82.1 3.4 %collective-permute-start.2 = (f32[256,512]{1,0:T(8,128)S(1)}, f32[256,512]{1,0:T(8,128)S(1)}, u32[]{:S(2)}, u32[]{:S(2)}) collective-permute-start(f32[256,512]{1,0:T(8,128)S(1)} %fusion.16), channel_id=1, source_target_pairs={{0,3},{1,0},{2,1},{3,2},{4,7},{5,4},{6,5},{7,6},{8,11},{9,8},{10,9... | collective-permute-start | bytes 1572872 | tf_op jit(solution)/shard_map/ppermute | solution.py:14
  87.9 5.8 %collective-permute-done.4 = f32[256,512]{1,0:T(8,128)S(1)} collective-permute-done((f32[256,512]{1,0:T(8,128)S(1)}, f32[256,512]{1,0:T(8,128)S(1)}, u32[]{:S(2)}, u32[]{:S(2)}) %collective-permute-start.4) | collective-permute-done | bytes 524320 | tf_op jit(solution)/shard_map/ppermute | solution.py:14
  93.8 2.1 collective-permute-start.5
  96.6 4.6 %collective-permute-start.8 = (f32[256,512]{1,0:T(8,128)S(1)}, f32[256,512]{1,0:T(8,128)S(1)}, u32[]{:S(2)}, u32[]{:S(2)}) collective-permute-start(f32[256,512]{1,0:T(8,128)S(1)} %fusion.21), channel_id=1, source_target_pairs={{0,3},{1,0},{2,1},{3,2},{4,7},{5,4},{6,5},{7,6},{8,11},{9,8},{10,9... | collective-permute-start | bytes 1572872 | tf_op jit(solution)/shard_map/ppermute | solution.py:14
  101.8 1.9 collective-permute-start.7
  103.7 5.5 %collective-permute-done.5 = f32[256,512]{1,0:T(8,128)S(1)} collective-permute-done((f32[256,512]{1,0:T(8,128)S(1)}, f32[256,512]{1,0:T(8,128)S(1)}, u32[]{:S(2)}, u32[]{:S(2)}) %collective-permute-start.5) | collective-permute-done | bytes 524320 | tf_op jit(solution)/shard_map/ppermute | solution.py:14
  109.9 2.8 %collective-permute-start.6 = (f32[2,2,32,512]{3,2,1,0:T(8,128)S(1)}, f32[2,2,32,512]{3,2,1,0:T(8,128)S(1)}, u32[]{:S(2)}, u32[]{:S(2)}) collective-permute-start(f32[2,2,32,512]{3,2,1,0:T(8,128)S(1)} %dynamic-slice_bitcast_fusion.1), channel_id=1, source_target_pairs={{0,4},{4,0},{8,12},{12,8},{16,20},{20,16},{24,28},{28,24},{1,5},{5... | collective-permute-start | bytes 786440 | tf_op jit(solution)/shard_map/ppermute | solution.py:19
  114.3 1.9 collective-permute-start.9
  117.8 2.7 %collective-permute-done.7 = f32[256,512]{1,0:T(8,128)S(1)} collective-permute-done((f32[256,512]{1,0:T(8,128)S(1)}, f32[256,512]{1,0:T(8,128)S(1)}, u32[]{:S(2)}, u32[]{:S(2)}) %collective-permute-start.7) | collective-permute-done | bytes 524320 | tf_op jit(solution)/shard_map/ppermute | solution.py:14
  120.4 6.1 %collective-permute-done.9 = f32[256,512]{1,0:T(8,128)S(1)} collective-permute-done((f32[256,512]{1,0:T(8,128)S(1)}, f32[256,512]{1,0:T(8,128)S(1)}, u32[]{:S(2)}, u32[]{:S(2)}) %collective-permute-start.9) | collective-permute-done | bytes 524320 | tf_op jit(solution)/shard_map/ppermute | solution.py:14
  127.3 1.9 collective-permute-start.10
  133.2 5.4 %all-to-all-start.1 = ((f32[16,8,8,256]{3,2,1,0:T(8,128)}), f32[16,8,8,256]{3,2,1,0:T(8,128)S(1)}, u32[]{:S(2)}, u32[]{:S(2)}) async-start(f32[16,8,8,256]{3,2,1,0:T(8,128)} %pad_maximum_fusion.4), calls=%async_computation.1 | async-start | bytes 2097152 | tf_op jit(solution)/shard_map/all_to_all | solution.py:141
  138.7 11.0 %collective-permute-start.13 = (f32[2,32,512]{2,1,0:T(8,128)S(1)}, f32[2,32,512]{2,1,0:T(8,128)S(1)}, u32[]{:S(2)}, u32[]{:S(2)}) collective-permute-start(f32[2,32,512]{2,1,0:T(8,128)S(1)} %pad_maximum_fusion.9), channel_id=1, source_target_pairs={{0,24},{4,28},{8,16},{12,20},{16,8},{20,12},{24,0},{28,4},{1,25},{... | collective-permute-start | bytes 393224 | tf_op jit(solution)/shard_map/ppermute | solution.py:19
  149.8 1.9 collective-permute-start.12
  151.7 2.2 %collective-permute-start.11 = (f32[2,32,512]{2,1,0:T(8,128)S(1)}, f32[2,32,512]{2,1,0:T(8,128)S(1)}, u32[]{:S(2)}, u32[]{:S(2)}) collective-permute-start(f32[2,32,512]{2,1,0:T(8,128)S(1)} %pad_maximum_fusion.7), channel_id=1, source_target_pairs={{0,8},{4,12},{8,0},{12,4},{16,24},{20,28},{24,16},{28,20},{1,9},{5... | collective-permute-start | bytes 393224 | tf_op jit(solution)/shard_map/ppermute | solution.py:19
  154.0 16.5 %collective-permute-done.12 = f32[2,32,512]{2,1,0:T(8,128)S(1)} collective-permute-done((f32[2,32,512]{2,1,0:T(8,128)S(1)}, f32[2,32,512]{2,1,0:T(8,128)S(1)}, u32[]{:S(2)}, u32[]{:S(2)}) %collective-permute-start.12) | collective-permute-done | bytes 131104 | tf_op jit(solution)/shard_map/ppermute | solution.py:19
  170.5 3.2 %collective-permute-start.14 = (f32[32,512]{1,0:T(8,128)S(1)}, f32[32,512]{1,0:T(8,128)S(1)}, u32[]{:S(2)}, u32[]{:S(2)}) collective-permute-start(f32[32,512]{1,0:T(8,128)S(1)} %slice_bitcast_fusion.8), channel_id=1, source_target_pairs={{0,32},{32,0},{1,33},{33,1},{2,34},{34,2},{3,35},{35,3},{4,36},{36... | collective-permute-start | bytes 196616 | tf_op jit(solution)/shard_map/ppermute | solution.py:19
  174.4 10.1 %all-to-all-start.2 = ((f32[16,8,256]{2,1,0:T(8,128)}), f32[16,8,256]{2,1,0:T(8,128)S(1)}, u32[]{:S(2)}, u32[]{:S(2)}) async-start(f32[16,8,256]{2,1,0:T(8,128)} %pad_maximum_fusion.10), calls=%async_computation.2 | async-start | bytes 262144 | tf_op jit(solution)/shard_map/all_to_all | solution.py:143
  184.6 12.3 %all-to-all-done.2 = f32[16,8,256]{2,1,0:T(8,128)S(1)} async-done(((f32[16,8,256]{2,1,0:T(8,128)}), f32[16,8,256]{2,1,0:T(8,128)S(1)}, u32[]{:S(2)}, u32[]{:S(2)}) %all-to-all-start.2) | async-done | bytes 131104 | tf_op jit(solution)/shard_map/all_to_all | solution.py:143
  197.6 6.4 %all-to-all-start.3 = ((f32[8,8,256]{2,1,0:T(8,128)}), f32[8,8,256]{2,1,0:T(8,128)S(1)}, u32[]{:S(2)}, u32[]{:S(2)}) async-start(f32[8,8,256]{2,1,0:T(8,128)} %broadcast_in_dim.21), calls=%async_computation.3 | async-start | bytes 131072 | tf_op jit(solution)/shard_map/all_to_all | solution.py:24
  204.6 4.2 %all-to-all-done.3 = f32[8,8,256]{2,1,0:T(8,128)S(1)} async-done(((f32[8,8,256]{2,1,0:T(8,128)}), f32[8,8,256]{2,1,0:T(8,128)S(1)}, u32[]{:S(2)}, u32[]{:S(2)}) %all-to-all-start.3) | async-done | bytes 65568 | tf_op jit(solution)/shard_map/all_to_all | solution.py:24
  (84 shorter events, 32.4 us)
Async XLA Ops:
  0.6 41.6 %copy-start = (f32[2,512,512]{2,1,0:T(8,128)S(1)}, f32[2,512,512]{2,1,0:T(8,128)}, u32[]{:S(2)}) copy-start(f32[2,512,512]{2,1,0:T(8,128)} %param.4) | copy-start | bytes 6291460
  0.6 17.4 %collective-permute-start.15 = (f32[1,32,1024]{2,1,0:T(8,128)}, f32[1,32,1024]{2,1,0:T(8,128)S(1)}, u32[]{:S(2)}, u32[]{:S(2)}) collective-permute-start(f32[1,32,1024]{2,1,0:T(8,128)} %bitcast.166), channel_id=1, source_target_pairs={{0,16},{4,20},{8,24},{12,28},{16,0},{20,4},{24,8},{28,12},{1,17},{... | collective-permute-start | bytes 393224 | tf_op jit(solution)/shard_map/ppermute | solution.py:19
  11.3 13.3 %collective-permute-start = (f32[32,512]{1,0:T(8,128)S(1)}, f32[32,512]{1,0:T(8,128)S(1)}, u32[]{:S(2)}, u32[]{:S(2)}) collective-permute-start(f32[32,512]{1,0:T(8,128)S(1)} %pad_maximum_fusion.12), channel_id=1, source_target_pairs={{0,32},{32,0},{1,33},{33,1},{2,34},{34,2},{3,35},{35,3},{4,36},{36... | collective-permute-start | bytes 196616 | tf_op jit(solution)/shard_map/ppermute | solution.py:19
  19.0 20.3 %collective-permute-start.16 = (f32[2,32,1024]{2,1,0:T(8,128)S(1)}, f32[2,32,1024]{2,1,0:T(8,128)S(1)}, u32[]{:S(2)}, u32[]{:S(2)}) collective-permute-start(f32[2,32,1024]{2,1,0:T(8,128)S(1)} %maximum_bitcast_fusion), channel_id=1, source_target_pairs={{0,8},{4,12},{8,0},{12,4},{16,24},{20,28},{24,16},{28,20},{1,9},{5... | collective-permute-start | bytes 786440 | tf_op jit(solution)/shard_map/ppermute | solution.py:19
  24.6 22.0 %collective-permute-start.1 = (f32[64,512]{1,0:T(8,128)S(1)}, f32[64,512]{1,0:T(8,128)S(1)}, u32[]{:S(2)}, u32[]{:S(2)}) collective-permute-start(f32[64,512]{1,0:T(8,128)S(1)} %bitcast.167), channel_id=1, source_target_pairs={{0,256},{256,0},{1,257},{257,1},{2,258},{258,2},{3,259},{259,3},{4... | collective-permute-start | bytes 393224 | tf_op jit(solution)/shard_map/ppermute | solution.py:19
  40.3 26.2 %collective-permute-start.17 = (f32[4,32,1024]{2,1,0:T(8,128)}, f32[4,32,1024]{2,1,0:T(8,128)}, u32[]{:S(2)}, u32[]{:S(2)}) collective-permute-start(f32[4,32,1024]{2,1,0:T(8,128)} %bitcast.48), channel_id=1, source_target_pairs={{0,4},{4,0},{8,12},{12,8},{16,20},{20,16},{24,28},{28,24},{1,5},{5... | collective-permute-start | bytes 1572872 | tf_op jit(solution)/shard_map/ppermute | solution.py:19
  47.8 28.1 %all-to-all-start = ((f32[4,128,512]{2,1,0:T(8,128)}), f32[4,128,512]{2,1,0:T(8,128)S(1)}, u32[]{:S(2)}, u32[]{:S(2)}) async-start(f32[4,128,512]{2,1,0:T(8,128)} %pad_maximum_fusion.1), calls=%async_computation | async-start | bytes 2097152 | tf_op jit(solution)/shard_map/all_to_all | solution.py:55
  60.1 25.4 %collective-permute-start.3 = (f32[2,512,512]{2,1,0:T(8,128)S(1)}, f32[2,512,512]{2,1,0:T(8,128)}, u32[]{:S(2)}, u32[]{:S(2)}) collective-permute-start(f32[2,512,512]{2,1,0:T(8,128)S(1)} %pad_maximum_fusion), channel_id=1, source_target_pairs={{0,32},{32,0},{1,33},{33,1},{2,34},{34,2},{3,35},{35,3},{4,36},{36... | collective-permute-start | bytes 6291464 | tf_op jit(solution)/shard_map/ppermute | solution.py:19
  73.9 55.3 %collective-permute-start.18 = (f32[2,512,256]{2,1,0:T(8,128)}, f32[2,512,256]{2,1,0:T(8,128)}, u32[]{:S(2)}, u32[]{:S(2)}) collective-permute-start(f32[2,512,256]{2,1,0:T(8,128)} %bitcast.55), channel_id=1, source_target_pairs={{0,32},{32,0},{1,33},{33,1},{2,34},{34,2},{3,35},{35,3},{4,36},{36... | collective-permute-start | bytes 3145736 | tf_op jit(solution)/shard_map/ppermute | solution.py:19
  76.0 1.0 copy-start.4
  76.1 4.7 %copy-start.3 = (f32[2,4,1,32,512]{4,3,2,1,0:T(8,128)S(1)}, f32[2,4,1,32,512]{4,3,2,1,0:T(8,128)}, u32[]{:S(2)}) copy-start(f32[2,4,1,32,512]{4,3,2,1,0:T(8,128)} %get-tuple-element.32) | copy-start | bytes 1572868
  77.0 4.5 %copy-start.2 = (f32[2,4,1,32,512]{4,3,2,1,0:T(8,128)S(1)}, f32[2,4,1,32,512]{4,3,2,1,0:T(8,128)}, u32[]{:S(2)}) copy-start(f32[2,4,1,32,512]{4,3,2,1,0:T(8,128)} %get-tuple-element.30) | copy-start | bytes 1572868
  77.7 16.1 %collective-permute-start.4 = (f32[256,512]{1,0:T(8,128)S(1)}, f32[256,512]{1,0:T(8,128)S(1)}, u32[]{:S(2)}, u32[]{:S(2)}) collective-permute-start(f32[256,512]{1,0:T(8,128)S(1)} %fusion.19), channel_id=1, source_target_pairs={{0,1},{1,2},{2,3},{3,0},{4,5},{5,6},{6,7},{7,4},{8,9},{9,10},{10,1... | collective-permute-start | bytes 1572872 | tf_op jit(solution)/shard_map/ppermute | solution.py:14
  82.1 21.6 %collective-permute-start.2 = (f32[256,512]{1,0:T(8,128)S(1)}, f32[256,512]{1,0:T(8,128)S(1)}, u32[]{:S(2)}, u32[]{:S(2)}) collective-permute-start(f32[256,512]{1,0:T(8,128)S(1)} %fusion.16), channel_id=1, source_target_pairs={{0,3},{1,0},{2,1},{3,2},{4,7},{5,4},{6,5},{7,6},{8,11},{9,8},{10,9... | collective-permute-start | bytes 1572872 | tf_op jit(solution)/shard_map/ppermute | solution.py:14
  93.8 15.4 %copy-start.1 = (f32[2,4,1,32,512]{4,3,2,1,0:T(8,128)S(1)}, f32[2,4,1,32,512]{4,3,2,1,0:T(8,128)}, u32[]{:S(2)}) copy-start(f32[2,4,1,32,512]{4,3,2,1,0:T(8,128)} %get-tuple-element.33) | copy-start | bytes 1572868
  93.8 15.4 %collective-permute-start.5 = (f32[256,512]{1,0:T(8,128)S(1)}, f32[256,512]{1,0:T(8,128)S(1)}, u32[]{:S(2)}, u32[]{:S(2)}) collective-permute-start(f32[256,512]{1,0:T(8,128)S(1)} %add.170), channel_id=1, source_target_pairs={{0,1},{1,2},{2,3},{3,0},{4,5},{5,6},{6,7},{7,4},{8,9},{9,10},{10,1... | collective-permute-start | bytes 1572872 | tf_op jit(solution)/shard_map/ppermute | solution.py:14
  96.6 17.6 %collective-permute-start.8 = (f32[256,512]{1,0:T(8,128)S(1)}, f32[256,512]{1,0:T(8,128)S(1)}, u32[]{:S(2)}, u32[]{:S(2)}) collective-permute-start(f32[256,512]{1,0:T(8,128)S(1)} %fusion.21), channel_id=1, source_target_pairs={{0,3},{1,0},{2,1},{3,2},{4,7},{5,4},{6,5},{7,6},{8,11},{9,8},{10,9... | collective-permute-start | bytes 1572872 | tf_op jit(solution)/shard_map/ppermute | solution.py:14
  101.8 18.6 %collective-permute-start.7 = (f32[256,512]{1,0:T(8,128)S(1)}, f32[256,512]{1,0:T(8,128)S(1)}, u32[]{:S(2)}, u32[]{:S(2)}) collective-permute-start(f32[256,512]{1,0:T(8,128)S(1)} %fusion.20), channel_id=1, source_target_pairs={{0,1},{1,2},{2,3},{3,0},{4,5},{5,6},{6,7},{7,4},{8,9},{9,10},{10,1... | collective-permute-start | bytes 1572872 | tf_op jit(solution)/shard_map/ppermute | solution.py:14
  109.9 7.7 %collective-permute-start.6 = (f32[2,2,32,512]{3,2,1,0:T(8,128)S(1)}, f32[2,2,32,512]{3,2,1,0:T(8,128)S(1)}, u32[]{:S(2)}, u32[]{:S(2)}) collective-permute-start(f32[2,2,32,512]{3,2,1,0:T(8,128)S(1)} %dynamic-slice_bitcast_fusion.1), channel_id=1, source_target_pairs={{0,4},{4,0},{8,12},{12,8},{16,20},{20,16},{24,28},{28,24},{1,5},{5... | collective-permute-start | bytes 786440 | tf_op jit(solution)/shard_map/ppermute | solution.py:19
  114.3 12.3 %collective-permute-start.9 = (f32[256,512]{1,0:T(8,128)S(1)}, f32[256,512]{1,0:T(8,128)S(1)}, u32[]{:S(2)}, u32[]{:S(2)}) collective-permute-start(f32[256,512]{1,0:T(8,128)S(1)} %add.180), channel_id=1, source_target_pairs={{0,3},{1,0},{2,1},{3,2},{4,7},{5,4},{6,5},{7,6},{8,11},{9,8},{10,9... | collective-permute-start | bytes 1572872 | tf_op jit(solution)/shard_map/ppermute | solution.py:14
  127.3 11.3 %collective-permute-start.10 = (f32[2,2,32,512]{3,2,1,0:T(8,128)S(1)}, f32[2,2,32,512]{3,2,1,0:T(8,128)S(1)}, u32[]{:S(2)}, u32[]{:S(2)}) collective-permute-start(f32[2,2,32,512]{3,2,1,0:T(8,128)S(1)} %dynamic-slice_bitcast_fusion), channel_id=1, source_target_pairs={{0,4},{4,0},{8,12},{12,8},{16,20},{20,16},{24,28},{28,24},{1,5},{5... | collective-permute-start | bytes 786440 | tf_op jit(solution)/shard_map/ppermute | solution.py:19
  133.2 40.5 %all-to-all-start.1 = ((f32[16,8,8,256]{3,2,1,0:T(8,128)}), f32[16,8,8,256]{3,2,1,0:T(8,128)S(1)}, u32[]{:S(2)}, u32[]{:S(2)}) async-start(f32[16,8,8,256]{3,2,1,0:T(8,128)} %pad_maximum_fusion.4), calls=%async_computation.1 | async-start | bytes 2097152 | tf_op jit(solution)/shard_map/all_to_all | solution.py:141
  138.7 70.1 %copy-start.5 = (f32[32,512]{1,0:T(8,128)S(1)}, f32[32,512]{1,0:T(8,128)}, u32[]{:S(2)}) copy-start(f32[32,512]{1,0:T(8,128)} %param.7) | copy-start | bytes 196612
  138.7 15.2 %collective-permute-start.13 = (f32[2,32,512]{2,1,0:T(8,128)S(1)}, f32[2,32,512]{2,1,0:T(8,128)S(1)}, u32[]{:S(2)}, u32[]{:S(2)}) collective-permute-start(f32[2,32,512]{2,1,0:T(8,128)S(1)} %pad_maximum_fusion.9), channel_id=1, source_target_pairs={{0,24},{4,28},{8,16},{12,20},{16,8},{20,12},{24,0},{28,4},{1,25},{... | collective-permute-start | bytes 393224 | tf_op jit(solution)/shard_map/ppermute | solution.py:19
  149.8 20.7 %collective-permute-start.12 = (f32[2,32,512]{2,1,0:T(8,128)S(1)}, f32[2,32,512]{2,1,0:T(8,128)S(1)}, u32[]{:S(2)}, u32[]{:S(2)}) collective-permute-start(f32[2,32,512]{2,1,0:T(8,128)S(1)} %pad_maximum_fusion.8), channel_id=1, source_target_pairs={{0,16},{4,20},{8,24},{12,28},{16,0},{20,4},{24,8},{28,12},{1,17},{... | collective-permute-start | bytes 393224 | tf_op jit(solution)/shard_map/ppermute | solution.py:19
  151.7 18.7 %collective-permute-start.11 = (f32[2,32,512]{2,1,0:T(8,128)S(1)}, f32[2,32,512]{2,1,0:T(8,128)S(1)}, u32[]{:S(2)}, u32[]{:S(2)}) collective-permute-start(f32[2,32,512]{2,1,0:T(8,128)S(1)} %pad_maximum_fusion.7), channel_id=1, source_target_pairs={{0,8},{4,12},{8,0},{12,4},{16,24},{20,28},{24,16},{28,20},{1,9},{5... | collective-permute-start | bytes 393224 | tf_op jit(solution)/shard_map/ppermute | solution.py:19
  170.5 14.0 %collective-permute-start.14 = (f32[32,512]{1,0:T(8,128)S(1)}, f32[32,512]{1,0:T(8,128)S(1)}, u32[]{:S(2)}, u32[]{:S(2)}) collective-permute-start(f32[32,512]{1,0:T(8,128)S(1)} %slice_bitcast_fusion.8), channel_id=1, source_target_pairs={{0,32},{32,0},{1,33},{33,1},{2,34},{34,2},{3,35},{35,3},{4,36},{36... | collective-permute-start | bytes 196616 | tf_op jit(solution)/shard_map/ppermute | solution.py:19
  174.4 22.5 %all-to-all-start.2 = ((f32[16,8,256]{2,1,0:T(8,128)}), f32[16,8,256]{2,1,0:T(8,128)S(1)}, u32[]{:S(2)}, u32[]{:S(2)}) async-start(f32[16,8,256]{2,1,0:T(8,128)} %pad_maximum_fusion.10), calls=%async_computation.2 | async-start | bytes 262144 | tf_op jit(solution)/shard_map/all_to_all | solution.py:143
  197.6 11.2 %all-to-all-start.3 = ((f32[8,8,256]{2,1,0:T(8,128)}), f32[8,8,256]{2,1,0:T(8,128)S(1)}, u32[]{:S(2)}, u32[]{:S(2)}) async-start(f32[8,8,256]{2,1,0:T(8,128)} %broadcast_in_dim.21), calls=%async_computation.3 | async-start | bytes 131072 | tf_op jit(solution)/shard_map/all_to_all | solution.py:24

commit v9 on v8

--- a/solution.py
+++ b/solution.py
@@ -67,16 +67,14 @@
     return rows
 
 
-def reduced_over_zl(halves):
+def reduced_over_zl(t):
     zl = lax.axis_index("zl")
     low, mid, high = zl % 2, (zl // 2) % 2, zl // 4
-    rows = []
-    for t in halves:
-        rows.append(pick(t, low, 2) + swap(pick(t, 1 - low, 2), "zl", 1))
+    t = pick(t, low, 3) + swap(pick(t, 1 - low, 3), "zl", 1)
 
     def part(flip_high, flip_mid):
-        first = (high ^ flip_high, mid ^ flip_mid, 0, 0)
-        return jnp.stack([lax.dynamic_slice(t, first, (1, 1, *t.shape[2:]))[0, 0] for t in rows])
+        first = (0, high ^ flip_high, mid ^ flip_mid, 0, 0)
+        return lax.dynamic_slice(t, first, (2, 1, 1, *t.shape[3:]))[:, 0, 0]
 
     got = []
     for flips in ((0, 1), (1, 0), (1, 1)):
@@ -112,8 +110,7 @@
     rest = lax.optimization_barrier([product(1, 0), product(3, 1)])
     up_c = shift(rest[0] + up_a, "x", 1)
     down_c = shift(rest[1] + down_a, "x", -1)
-    first = product(0, 0) + down_b + up_c
-    return first, product(0, 1) + up_b + down_c
+    return product(0, 0) + down_b + up_c, product(0, 1) + up_b + down_c
 
 
 def local(inverse_tiles, tile_rows, panel, pivot_base):
@@ -128,7 +125,7 @@
     u = lax.optimization_barrier(u.reshape(2, block, 8 * share))
     other_u = swap(u, "c", 1)
     t = reduced_products(inverse_tiles, codes, column)
-    trailing = reduced_over_zl([x.reshape(2, 2, 2, share, block) for x in t])
+    trailing = reduced_over_zl(jnp.stack(t).reshape(2, 2, 2, 2, share, block))
     other = swap(trailing[1], "c", 1)
     low, high = ordered(trailing[0], other, c, 0)
     trailing = [x[:, j * half : (j + 1) * half] for j in range(2) for x in (low, high)]

time: 211 us -> 197 us (0.934)
  starting transfers between devices: 114 us -> 105 us
  local copies, waits for them, and re-layouts: 13 us -> 8.42 us
  other arithmetic: 11.3 us -> 15.6 us
  waiting for transfers between devices: 56 us -> 52.5 us
    ppermute x6, waiting for transfers between devices: 20.1 us -> 11.7 us  [shift(): return lax.ppermute(x, axis, [(i, (i + by) % n) for i in range(n)])]
    all_to_all x1, starting transfers between devices: 10.6 us -> 4.18 us  [gathered_column(): lax.all_to_all(both, 'y', 0, 0, tiled=True).reshape(4, 2, *near.shape)]
    ppermute x13 -> x12, waiting for transfers between devices: 19.4 us -> 24.3 us  [swap(): return lax.ppermute(x, axis, [(i, i ^ bit) for i in range(n)])]
    ppermute x13 -> x12, starting transfers between devices: 64.6 us -> 60 us  [swap(): return lax.ppermute(x, axis, [(i, i ^ bit) for i in range(n)])]
    all_to_all x1, starting transfers between devices: 10.1 us -> 6.33 us  [local(): w = lax.all_to_all(w, ('zh', 'zl'), 0, 0, tiled=True).sum(axis=0)]
    ppermute x6, starting transfers between devices: 17 us -> 20.2 us  [shift(): return lax.ppermute(x, axis, [(i, (i + by) % n) for i in range(n)])]
    transpose x1, local copies, waits for them, and re-layouts: 2.37 us -> 0.13 us  [local(): u = u.reshape(2, 4, 4, 4, 8, 8 * share).transpose(0, 3, 2, 1, 4, 5)]
    transpose x1, local copies, waits for them, and re-layouts: 2.57 us -> 0.33 us  [local(): u = gathered_over_zl(panel).reshape(8 * share, width).T]
  transfers between devices with their start and end apart: 23 -> 22, of which waited for: 8 -> 11; matrix products, arithmetic and copies ran while one was open for 16% -> 16% of each run, Pallas kernels for 0% -> 0%
where the time goes in v9:
time: 197 us; the launch traced here: 195 us
  starting transfers between devices  105 us (53%)
  waiting for transfers between devices  52.5 us (27%)
  other arithmetic  15.6 us (8%)
  matrix products  10 us (5%)
  local copies, waits for them, and re-layouts  8.42 us (4%)
  between operations  3.97 us (2%)
    ppermute x12, starting transfers between devices, swap(): return lax.ppermute(x, axis, [(i, i ^ bit) for i in range(n)])  60 us
    ppermute x12, waiting for transfers between devices, swap(): return lax.ppermute(x, axis, [(i, i ^ bit) for i in range(n)])  24.3 us
    ppermute x6, starting transfers between devices, shift(): return lax.ppermute(x, axis, [(i, (i + by) % n) for i in range(n)])  20.2 us
    all_to_all x1, waiting for transfers between devices, local(): w = lax.all_to_all(w, ('zh', 'zl'), 0, 0, tiled=True).sum(axis=0)  12.3 us
    ppermute x6, waiting for transfers between devices, shift(): return lax.ppermute(x, axis, [(i, (i + by) % n) for i in range(n)])  11.7 us
    dot_general x12, matrix products, dot(): return jnp.dot(a, b, precision=HIGH, preferred_element_type=jnp.float32)  10 us
    all_to_all x1, starting transfers between devices, spread(): return lax.all_to_all(copies, axes, 0, 0, tiled=True)  7.36 us
    all_to_all x1, starting transfers between devices, local(): w = lax.all_to_all(w, ('y', 'x'), 0, 0, tiled=True).sum(axis=0)  6.71 us
  transfers between devices with their start and end apart: 22, of which 11 were waited for; matrix products, arithmetic and copies ran while one was open for 16% of the time, Pallas kernels for 0%

profile of v9, /device:TPU:1, one launch (start us, length us, event | category | flops | bytes accessed | tf_op | source)
XLA Modules:
  0.0 195.3 jit_solution(12498958861273519505)
XLA Ops:
  1.5 8.7 %collective-permute-start = (f32[32,512]{1,0:T(8,128)S(1)}, f32[32,512]{1,0:T(8,128)S(1)}, u32[]{:S(2)}, u32[]{:S(2)}) collective-permute-start(f32[32,512]{1,0:T(8,128)S(1)} %pad_maximum_fusion.9), channel_id=1, source_target_pairs={{0,32},{32,0},{1,33},{33,1},{2,34},{34,2},{3,35},{35,3},{4,36},{36... | collective-permute-start | bytes 196616 | tf_op jit(solution)/shard_map/ppermute | solution.py:19
  10.2 3.5 %collective-permute-start.14 = (f32[1,32,1024]{2,1,0:T(8,128)}, f32[1,32,1024]{2,1,0:T(8,128)S(1)}, u32[]{:S(2)}, u32[]{:S(2)}) collective-permute-start(f32[1,32,1024]{2,1,0:T(8,128)} %bitcast.167), channel_id=1, source_target_pairs={{0,16},{4,20},{8,24},{12,28},{16,0},{20,4},{24,8},{28,12},{1,17},{... | collective-permute-start | bytes 393224 | tf_op jit(solution)/shard_map/ppermute | solution.py:19
  17.6 3.2 %select_select_fusion.1 = (f32[1,512,512]{2,1,0:T(8,128)}, f32[1,512,512]{2,1,0:T(8,128)}) fusion(f32[2,512,512]{2,1,0:T(8,128)} %param.4, pred[]{:T(512)} %bitcast.1, pred[]{:T(512)} %bitcast, pred[]{:T(512)} %bitcast.3, pred[]{:T(512)} %bitcast.2), kind=kLoop, calls=%fused_computation.16 | loop fusion | flops 1048576 | bytes 4194308 | tf_op jit(solution)/shard_map/jit(_where)/select_n | solution.py:92
  20.9 10.6 %collective-permute-start.1 = (f32[64,512]{1,0:T(8,128)S(1)}, f32[64,512]{1,0:T(8,128)S(1)}, u32[]{:S(2)}, u32[]{:S(2)}) collective-permute-start(f32[64,512]{1,0:T(8,128)S(1)} %bitcast.168), channel_id=1, source_target_pairs={{0,256},{256,0},{1,257},{257,1},{2,258},{258,2},{3,259},{259,3},{4... | collective-permute-start | bytes 393224 | tf_op jit(solution)/shard_map/ppermute | solution.py:19
  32.3 3.1 %collective-permute-start.15 = (f32[2,32,1024]{2,1,0:T(8,128)}, f32[2,32,1024]{2,1,0:T(8,128)}, u32[]{:S(2)}, u32[]{:S(2)}) collective-permute-start(f32[2,32,1024]{2,1,0:T(8,128)} %maximum_bitcast_fusion), channel_id=1, source_target_pairs={{0,8},{4,12},{8,0},{12,4},{16,24},{20,28},{24,16},{28,20},{1,9},{5... | collective-permute-start | bytes 786440 | tf_op jit(solution)/shard_map/ppermute | solution.py:19
  37.4 4.2 %all-to-all-start = ((f32[4,128,512]{2,1,0:T(8,128)}), f32[4,128,512]{2,1,0:T(8,128)S(1)}, u32[]{:S(2)}, u32[]{:S(2)}) async-start(f32[4,128,512]{2,1,0:T(8,128)} %pad_maximum_fusion.1), calls=%async_computation | async-start | bytes 2097152 | tf_op jit(solution)/shard_map/all_to_all | solution.py:55
  43.3 3.5 %collective-permute-start.3 = (f32[2,512,512]{2,1,0:T(8,128)S(1)}, f32[2,512,512]{2,1,0:T(8,128)}, u32[]{:S(2)}, u32[]{:S(2)}) collective-permute-start(f32[2,512,512]{2,1,0:T(8,128)S(1)} %pad_maximum_fusion), channel_id=1, source_target_pairs={{0,32},{32,0},{1,33},{33,1},{2,34},{34,2},{3,35},{35,3},{4,36},{36... | collective-permute-start | bytes 6291464 | tf_op jit(solution)/shard_map/ppermute | solution.py:19
  48.3 8.6 %collective-permute-done.15 = f32[2,32,1024]{2,1,0:T(8,128)} collective-permute-done((f32[2,32,1024]{2,1,0:T(8,128)}, f32[2,32,1024]{2,1,0:T(8,128)}, u32[]{:S(2)}, u32[]{:S(2)}) %collective-permute-start.15) | collective-permute-done | bytes 262176 | tf_op jit(solution)/shard_map/ppermute | solution.py:19
  58.7 5.7 %collective-permute-start.16 = (f32[4,32,1024]{2,1,0:T(8,128)}, f32[4,32,1024]{2,1,0:T(8,128)}, u32[]{:S(2)}, u32[]{:S(2)}) collective-permute-start(f32[4,32,1024]{2,1,0:T(8,128)} %bitcast.42), channel_id=1, source_target_pairs={{0,4},{4,0},{8,12},{12,8},{16,20},{20,16},{24,28},{28,24},{1,5},{5... | collective-permute-start | bytes 1572872 | tf_op jit(solution)/shard_map/ppermute | solution.py:19
  66.2 3.1 %collective-permute-start.4 = (f32[256,512]{1,0:T(8,128)S(1)}, f32[256,512]{1,0:T(8,128)S(1)}, u32[]{:S(2)}, u32[]{:S(2)}) collective-permute-start(f32[256,512]{1,0:T(8,128)S(1)} %fusion.24), channel_id=1, source_target_pairs={{0,1},{1,2},{2,3},{3,0},{4,5},{5,6},{6,7},{7,4},{8,9},{9,10},{10,1... | collective-permute-start | bytes 1572872 | tf_op jit(solution)/shard_map/ppermute | solution.py:14
  71.4 3.4 %collective-permute-start.2 = (f32[256,512]{1,0:T(8,128)}, f32[256,512]{1,0:T(8,128)}, u32[]{:S(2)}, u32[]{:S(2)}) collective-permute-start(f32[256,512]{1,0:T(8,128)} %fusion.21), channel_id=1, source_target_pairs={{0,3},{1,0},{2,1},{3,2},{4,7},{5,4},{6,5},{7,6},{8,11},{9,8},{10,9... | collective-permute-start | bytes 1572872 | tf_op jit(solution)/shard_map/ppermute | solution.py:14
  74.8 2.7 %constant_dynamic-slice_fusion = (f32[2,4,1,32,512]{4,3,2,1,0:T(8,128)S(1)}, f32[2,4,1,32,512]{4,3,2,1,0:T(8,128)S(1)}, f32[2,4,1,32,512]{4,3,2,1,0:T(8,128)}, f32[2,4,1,32,512]{4,3,2,1,0:T(8,128)}) fusion(f32[2,4,4,32,512]{4,3,2,1,0:T(8,128)} %bitcast.19, s32[]{:T(128)S(6)} %select_n.230, s32[]{:T(128)S(6)} %select_n.228, s32[]{:T(128)S(6)} %select_n.226, ...), kind=kLoop, calls=%fused_computation.60 | loop fusion | bytes 4194320 | tf_op jit(solution)/shard_map/jit(dynamic_index_in_dim)/dynamic_slice | solution.py:33
  79.0 3.6 %collective-permute-done.4 = f32[256,512]{1,0:T(8,128)S(1)} collective-permute-done((f32[256,512]{1,0:T(8,128)S(1)}, f32[256,512]{1,0:T(8,128)S(1)}, u32[]{:S(2)}, u32[]{:S(2)}) %collective-permute-start.4) | collective-permute-done | bytes 524320 | tf_op jit(solution)/shard_map/ppermute | solution.py:14
  83.4 2.0 %collective-permute-start.5 = (f32[256,512]{1,0:T(8,128)}, f32[256,512]{1,0:T(8,128)}, u32[]{:S(2)}, u32[]{:S(2)}) collective-permute-start(f32[256,512]{1,0:T(8,128)} %add.157), channel_id=1, source_target_pairs={{0,1},{1,2},{2,3},{3,0},{4,5},{5,6},{6,7},{7,4},{8,9},{9,10},{10,1... | collective-permute-start | bytes 1572872 | tf_op jit(solution)/shard_map/ppermute | solution.py:14
  86.9 4.5 %collective-permute-start.7 = (f32[256,512]{1,0:T(8,128)}, f32[256,512]{1,0:T(8,128)}, u32[]{:S(2)}, u32[]{:S(2)}) collective-permute-start(f32[256,512]{1,0:T(8,128)} %fusion.26), channel_id=1, source_target_pairs={{0,3},{1,0},{2,1},{3,2},{4,7},{5,4},{6,5},{7,6},{8,11},{9,8},{10,9... | collective-permute-start | bytes 1572872 | tf_op jit(solution)/shard_map/ppermute | solution.py:14
  93.4 3.8 %collective-permute-start.17 = (f32[2,512,256]{2,1,0:T(8,128)S(1)}, f32[2,512,256]{2,1,0:T(8,128)S(1)}, u32[]{:S(2)}, u32[]{:S(2)}) collective-permute-start(f32[2,512,256]{2,1,0:T(8,128)S(1)} %bitcast.152), channel_id=1, source_target_pairs={{0,32},{32,0},{1,33},{33,1},{2,34},{34,2},{3,35},{35,3},{4,36},{36... | collective-permute-start | bytes 3145736 | tf_op jit(solution)/shard_map/ppermute | solution.py:19
  97.8 1.9 collective-permute-start.6
  102.6 5.3 %collective-permute-start.8 = (f32[256,512]{1,0:T(8,128)S(1)}, f32[256,512]{1,0:T(8,128)S(1)}, u32[]{:S(2)}, u32[]{:S(2)}) collective-permute-start(f32[256,512]{1,0:T(8,128)S(1)} %add.160), channel_id=1, source_target_pairs={{0,3},{1,0},{2,1},{3,2},{4,7},{5,4},{6,5},{7,6},{8,11},{9,8},{10,9... | collective-permute-start | bytes 1572872 | tf_op jit(solution)/shard_map/ppermute | solution.py:14
  108.0 1.8 fusion
  110.6 3.8 %collective-permute-done.6 = f32[256,512]{1,0:T(8,128)S(1)} collective-permute-done((f32[256,512]{1,0:T(8,128)S(1)}, f32[256,512]{1,0:T(8,128)S(1)}, u32[]{:S(2)}, u32[]{:S(2)}) %collective-permute-start.6) | collective-permute-done | bytes 524320 | tf_op jit(solution)/shard_map/ppermute | solution.py:14
  114.4 2.6 %collective-permute-done.8 = f32[256,512]{1,0:T(8,128)S(1)} collective-permute-done((f32[256,512]{1,0:T(8,128)S(1)}, f32[256,512]{1,0:T(8,128)S(1)}, u32[]{:S(2)}, u32[]{:S(2)}) %collective-permute-start.8) | collective-permute-done | bytes 524320 | tf_op jit(solution)/shard_map/ppermute | solution.py:14
  117.6 3.0 %collective-permute-start.9 = (f32[2,2,2,32,512]{4,3,2,1,0:T(8,128)S(1)}, f32[2,2,2,32,512]{4,3,2,1,0:T(8,128)S(1)}, u32[]{:S(2)}, u32[]{:S(2)}) collective-permute-start(f32[2,2,2,32,512]{4,3,2,1,0:T(8,128)S(1)} %fusion.3), channel_id=1, source_target_pairs={{0,4},{4,0},{8,12},{12,8},{16,20},{20,16},{24,28},{28,24},{1,5},{5... | collective-permute-start | bytes 1572872 | tf_op jit(solution)/shard_map/ppermute | solution.py:19
  122.5 6.7 %all-to-all-start.1 = ((f32[16,8,8,256]{3,2,1,0:T(8,128)}), f32[16,8,8,256]{3,2,1,0:T(8,128)S(1)}, u32[]{:S(2)}, u32[]{:S(2)}) async-start(f32[16,8,8,256]{3,2,1,0:T(8,128)} %pad_maximum_fusion.4), calls=%async_computation.1 | async-start | bytes 2097152 | tf_op jit(solution)/shard_map/all_to_all | solution.py:138
  130.0 1.9 collective-permute-start.12
  131.9 4.8 %collective-permute-start.11 = (f32[2,32,512]{2,1,0:T(8,128)S(1)}, f32[2,32,512]{2,1,0:T(8,128)S(1)}, u32[]{:S(2)}, u32[]{:S(2)}) collective-permute-start(f32[2,32,512]{2,1,0:T(8,128)S(1)} %get-tuple-element.42), channel_id=1, source_target_pairs={{0,16},{4,20},{8,24},{12,28},{16,0},{20,4},{24,8},{28,12},{1,17},{... | collective-permute-start | bytes 393224 | tf_op jit(solution)/shard_map/ppermute | solution.py:19
  136.8 6.4 %collective-permute-start.10 = (f32[2,32,512]{2,1,0:T(8,128)S(1)}, f32[2,32,512]{2,1,0:T(8,128)S(1)}, u32[]{:S(2)}, u32[]{:S(2)}) collective-permute-start(f32[2,32,512]{2,1,0:T(8,128)S(1)} %get-tuple-element.40), channel_id=1, source_target_pairs={{0,8},{4,12},{8,0},{12,4},{16,24},{20,28},{24,16},{28,20},{1,9},{5... | collective-permute-start | bytes 393224 | tf_op jit(solution)/shard_map/ppermute | solution.py:19
  144.5 12.9 %collective-permute-done.11 = f32[2,32,512]{2,1,0:T(8,128)S(1)} collective-permute-done((f32[2,32,512]{2,1,0:T(8,128)S(1)}, f32[2,32,512]{2,1,0:T(8,128)S(1)}, u32[]{:S(2)}, u32[]{:S(2)}) %collective-permute-start.11) | collective-permute-done | bytes 131104 | tf_op jit(solution)/shard_map/ppermute | solution.py:19
  157.5 4.8 %collective-permute-start.13 = (f32[32,512]{1,0:T(8,128)S(1)}, f32[32,512]{1,0:T(8,128)S(1)}, u32[]{:S(2)}, u32[]{:S(2)}) collective-permute-start(f32[32,512]{1,0:T(8,128)S(1)} %slice_bitcast_fusion.8), channel_id=1, source_target_pairs={{0,32},{32,0},{1,33},{33,1},{2,34},{34,2},{3,35},{35,3},{4,36},{36... | collective-permute-start | bytes 196616 | tf_op jit(solution)/shard_map/ppermute | solution.py:19
  163.1 6.3 %all-to-all-start.2 = ((f32[16,8,256]{2,1,0:T(8,128)}), f32[16,8,256]{2,1,0:T(8,128)S(1)}, u32[]{:S(2)}, u32[]{:S(2)}) async-start(f32[16,8,256]{2,1,0:T(8,128)} %pad_maximum_fusion.7), calls=%async_computation.2 | async-start | bytes 262144 | tf_op jit(solution)/shard_map/all_to_all | solution.py:140
  169.5 12.3 %all-to-all-done.2 = f32[16,8,256]{2,1,0:T(8,128)S(1)} async-done(((f32[16,8,256]{2,1,0:T(8,128)}), f32[16,8,256]{2,1,0:T(8,128)S(1)}, u32[]{:S(2)}, u32[]{:S(2)}) %all-to-all-start.2) | async-done | bytes 131104 | tf_op jit(solution)/shard_map/all_to_all | solution.py:140
  182.5 7.4 %all-to-all-start.3 = ((f32[8,8,256]{2,1,0:T(8,128)}), f32[8,8,256]{2,1,0:T(8,128)S(1)}, u32[]{:S(2)}, u32[]{:S(2)}) async-start(f32[8,8,256]{2,1,0:T(8,128)} %broadcast_in_dim.21), calls=%async_computation.3 | async-start | bytes 131072 | tf_op jit(solution)/shard_map/all_to_all | solution.py:24
  190.5 4.2 %all-to-all-done.3 = f32[8,8,256]{2,1,0:T(8,128)S(1)} async-done(((f32[8,8,256]{2,1,0:T(8,128)}), f32[8,8,256]{2,1,0:T(8,128)S(1)}, u32[]{:S(2)}, u32[]{:S(2)}) %all-to-all-start.3) | async-done | bytes 65568 | tf_op jit(solution)/shard_map/all_to_all | solution.py:24
  (82 shorter events, 30.9 us)
Async XLA Ops:
  1.5 19.4 %collective-permute-start = (f32[32,512]{1,0:T(8,128)S(1)}, f32[32,512]{1,0:T(8,128)S(1)}, u32[]{:S(2)}, u32[]{:S(2)}) collective-permute-start(f32[32,512]{1,0:T(8,128)S(1)} %pad_maximum_fusion.9), channel_id=1, source_target_pairs={{0,32},{32,0},{1,33},{33,1},{2,34},{34,2},{3,35},{35,3},{4,36},{36... | collective-permute-start | bytes 196616 | tf_op jit(solution)/shard_map/ppermute | solution.py:19
  10.2 21.3 %collective-permute-start.14 = (f32[1,32,1024]{2,1,0:T(8,128)}, f32[1,32,1024]{2,1,0:T(8,128)S(1)}, u32[]{:S(2)}, u32[]{:S(2)}) collective-permute-start(f32[1,32,1024]{2,1,0:T(8,128)} %bitcast.167), channel_id=1, source_target_pairs={{0,16},{4,20},{8,24},{12,28},{16,0},{20,4},{24,8},{28,12},{1,17},{... | collective-permute-start | bytes 393224 | tf_op jit(solution)/shard_map/ppermute | solution.py:19
  17.6 13.9 %copy-start.7 = (f32[32,1024]{1,0:T(8,128)S(1)}, f32[32,1024]{1,0:T(8,128)}, u32[]{:S(2)}) copy-start(f32[32,1024]{1,0:T(8,128)} %param.6) | copy-start | bytes 393220
  20.9 15.4 %collective-permute-start.1 = (f32[64,512]{1,0:T(8,128)S(1)}, f32[64,512]{1,0:T(8,128)S(1)}, u32[]{:S(2)}, u32[]{:S(2)}) collective-permute-start(f32[64,512]{1,0:T(8,128)S(1)} %bitcast.168), channel_id=1, source_target_pairs={{0,256},{256,0},{1,257},{257,1},{2,258},{258,2},{3,259},{259,3},{4... | collective-permute-start | bytes 393224 | tf_op jit(solution)/shard_map/ppermute | solution.py:19
  32.3 24.6 %collective-permute-start.15 = (f32[2,32,1024]{2,1,0:T(8,128)}, f32[2,32,1024]{2,1,0:T(8,128)}, u32[]{:S(2)}, u32[]{:S(2)}) collective-permute-start(f32[2,32,1024]{2,1,0:T(8,128)} %maximum_bitcast_fusion), channel_id=1, source_target_pairs={{0,8},{4,12},{8,0},{12,4},{16,24},{20,28},{24,16},{28,20},{1,9},{5... | collective-permute-start | bytes 786440 | tf_op jit(solution)/shard_map/ppermute | solution.py:19
  37.4 27.1 %all-to-all-start = ((f32[4,128,512]{2,1,0:T(8,128)}), f32[4,128,512]{2,1,0:T(8,128)S(1)}, u32[]{:S(2)}, u32[]{:S(2)}) async-start(f32[4,128,512]{2,1,0:T(8,128)} %pad_maximum_fusion.1), calls=%async_computation | async-start | bytes 2097152 | tf_op jit(solution)/shard_map/all_to_all | solution.py:55
  43.3 31.5 %collective-permute-start.3 = (f32[2,512,512]{2,1,0:T(8,128)S(1)}, f32[2,512,512]{2,1,0:T(8,128)}, u32[]{:S(2)}, u32[]{:S(2)}) collective-permute-start(f32[2,512,512]{2,1,0:T(8,128)S(1)} %pad_maximum_fusion), channel_id=1, source_target_pairs={{0,32},{32,0},{1,33},{33,1},{2,34},{34,2},{3,35},{35,3},{4,36},{36... | collective-permute-start | bytes 6291464 | tf_op jit(solution)/shard_map/ppermute | solution.py:19
  58.7 32.6 %collective-permute-start.16 = (f32[4,32,1024]{2,1,0:T(8,128)}, f32[4,32,1024]{2,1,0:T(8,128)}, u32[]{:S(2)}, u32[]{:S(2)}) collective-permute-start(f32[4,32,1024]{2,1,0:T(8,128)} %bitcast.42), channel_id=1, source_target_pairs={{0,4},{4,0},{8,12},{12,8},{16,20},{20,16},{24,28},{28,24},{1,5},{5... | collective-permute-start | bytes 1572872 | tf_op jit(solution)/shard_map/ppermute | solution.py:19
  64.6 1.0 copy-start.5
  64.7 4.7 %copy-start.4 = (f32[2,4,1,32,512]{4,3,2,1,0:T(8,128)S(1)}, f32[2,4,1,32,512]{4,3,2,1,0:T(8,128)}, u32[]{:S(2)}) copy-start(f32[2,4,1,32,512]{4,3,2,1,0:T(8,128)} %get-tuple-element.32) | copy-start | bytes 1572868
  65.6 4.4 %copy-start.3 = (f32[2,4,1,32,512]{4,3,2,1,0:T(8,128)S(1)}, f32[2,4,1,32,512]{4,3,2,1,0:T(8,128)}, u32[]{:S(2)}) copy-start(f32[2,4,1,32,512]{4,3,2,1,0:T(8,128)} %get-tuple-element.30) | copy-start | bytes 1572868
  66.2 16.3 %collective-permute-start.4 = (f32[256,512]{1,0:T(8,128)S(1)}, f32[256,512]{1,0:T(8,128)S(1)}, u32[]{:S(2)}, u32[]{:S(2)}) collective-permute-start(f32[256,512]{1,0:T(8,128)S(1)} %fusion.24), channel_id=1, source_target_pairs={{0,1},{1,2},{2,3},{3,0},{4,5},{5,6},{6,7},{7,4},{8,9},{9,10},{10,1... | collective-permute-start | bytes 1572872 | tf_op jit(solution)/shard_map/ppermute | solution.py:14
  71.4 36.5 %collective-permute-start.2 = (f32[256,512]{1,0:T(8,128)}, f32[256,512]{1,0:T(8,128)}, u32[]{:S(2)}, u32[]{:S(2)}) collective-permute-start(f32[256,512]{1,0:T(8,128)} %fusion.21), channel_id=1, source_target_pairs={{0,3},{1,0},{2,1},{3,2},{4,7},{5,4},{6,5},{7,6},{8,11},{9,8},{10,9... | collective-permute-start | bytes 1572872 | tf_op jit(solution)/shard_map/ppermute | solution.py:14
  83.4 24.5 %collective-permute-start.5 = (f32[256,512]{1,0:T(8,128)}, f32[256,512]{1,0:T(8,128)}, u32[]{:S(2)}, u32[]{:S(2)}) collective-permute-start(f32[256,512]{1,0:T(8,128)} %add.157), channel_id=1, source_target_pairs={{0,1},{1,2},{2,3},{3,0},{4,5},{5,6},{6,7},{7,4},{8,9},{9,10},{10,1... | collective-permute-start | bytes 1572872 | tf_op jit(solution)/shard_map/ppermute | solution.py:14
  86.9 14.6 %collective-permute-start.7 = (f32[256,512]{1,0:T(8,128)}, f32[256,512]{1,0:T(8,128)}, u32[]{:S(2)}, u32[]{:S(2)}) collective-permute-start(f32[256,512]{1,0:T(8,128)} %fusion.26), channel_id=1, source_target_pairs={{0,3},{1,0},{2,1},{3,2},{4,7},{5,4},{6,5},{7,6},{8,11},{9,8},{10,9... | collective-permute-start | bytes 1572872 | tf_op jit(solution)/shard_map/ppermute | solution.py:14
  93.2 3.9 %copy-start.6 = (f32[2,4,1,32,512]{4,3,2,1,0:T(8,128)S(1)}, f32[2,4,1,32,512]{4,3,2,1,0:T(8,128)}, u32[]{:S(2)}) copy-start(f32[2,4,1,32,512]{4,3,2,1,0:T(8,128)} %get-tuple-element.28) | copy-start | bytes 1572868
  93.2 8.3 %copy-start = (f32[256,512]{1,0:T(8,128)S(1)}, f32[256,512]{1,0:T(8,128)}, u32[]{:S(2)}) copy-start(f32[256,512]{1,0:T(8,128)} %fusion.23) | copy-start | bytes 1572868
  93.4 14.6 %copy-start.1 = (f32[2,4,1,32,512]{4,3,2,1,0:T(8,128)S(1)}, f32[2,4,1,32,512]{4,3,2,1,0:T(8,128)}, u32[]{:S(2)}) copy-start(f32[2,4,1,32,512]{4,3,2,1,0:T(8,128)} %get-tuple-element.33) | copy-start | bytes 1572868
  93.4 27.2 %collective-permute-start.17 = (f32[2,512,256]{2,1,0:T(8,128)S(1)}, f32[2,512,256]{2,1,0:T(8,128)S(1)}, u32[]{:S(2)}, u32[]{:S(2)}) collective-permute-start(f32[2,512,256]{2,1,0:T(8,128)S(1)} %bitcast.152), channel_id=1, source_target_pairs={{0,32},{32,0},{1,33},{33,1},{2,34},{34,2},{3,35},{35,3},{4,36},{36... | collective-permute-start | bytes 3145736 | tf_op jit(solution)/shard_map/ppermute | solution.py:19
  97.8 16.6 %collective-permute-start.6 = (f32[256,512]{1,0:T(8,128)S(1)}, f32[256,512]{1,0:T(8,128)S(1)}, u32[]{:S(2)}, u32[]{:S(2)}) collective-permute-start(f32[256,512]{1,0:T(8,128)S(1)} %fusion.25), channel_id=1, source_target_pairs={{0,1},{1,2},{2,3},{3,0},{4,5},{5,6},{6,7},{7,4},{8,9},{9,10},{10,1... | collective-permute-start | bytes 1572872 | tf_op jit(solution)/shard_map/ppermute | solution.py:14
  102.6 14.3 %collective-permute-start.8 = (f32[256,512]{1,0:T(8,128)S(1)}, f32[256,512]{1,0:T(8,128)S(1)}, u32[]{:S(2)}, u32[]{:S(2)}) collective-permute-start(f32[256,512]{1,0:T(8,128)S(1)} %add.160), channel_id=1, source_target_pairs={{0,3},{1,0},{2,1},{3,2},{4,7},{5,4},{6,5},{7,6},{8,11},{9,8},{10,9... | collective-permute-start | bytes 1572872 | tf_op jit(solution)/shard_map/ppermute | solution.py:14
  109.8 7.1 %copy-start.2 = (f32[2,4,1,32,512]{4,3,2,1,0:T(8,128)S(1)}, f32[2,4,1,32,512]{4,3,2,1,0:T(8,128)}, u32[]{:S(2)}) copy-start(f32[2,4,1,32,512]{4,3,2,1,0:T(8,128)} %get-tuple-element.29) | copy-start | bytes 1572868
  117.6 12.2 %collective-permute-start.9 = (f32[2,2,2,32,512]{4,3,2,1,0:T(8,128)S(1)}, f32[2,2,2,32,512]{4,3,2,1,0:T(8,128)S(1)}, u32[]{:S(2)}, u32[]{:S(2)}) collective-permute-start(f32[2,2,2,32,512]{4,3,2,1,0:T(8,128)S(1)} %fusion.3), channel_id=1, source_target_pairs={{0,4},{4,0},{8,12},{12,8},{16,20},{20,16},{24,28},{28,24},{1,5},{5... | collective-permute-start | bytes 1572872 | tf_op jit(solution)/shard_map/ppermute | solution.py:19
  122.5 39.9 %all-to-all-start.1 = ((f32[16,8,8,256]{3,2,1,0:T(8,128)}), f32[16,8,8,256]{3,2,1,0:T(8,128)S(1)}, u32[]{:S(2)}, u32[]{:S(2)}) async-start(f32[16,8,8,256]{3,2,1,0:T(8,128)} %pad_maximum_fusion.4), calls=%async_computation.1 | async-start | bytes 2097152 | tf_op jit(solution)/shard_map/all_to_all | solution.py:138
  129.9 64.7 %copy-start.8 = (f32[32,512]{1,0:T(8,128)S(1)}, f32[32,512]{1,0:T(8,128)}, u32[]{:S(2)}) copy-start(f32[32,512]{1,0:T(8,128)} %param.7) | copy-start | bytes 196612
  130.0 14.5 %collective-permute-start.12 = (f32[2,32,512]{2,1,0:T(8,128)S(1)}, f32[2,32,512]{2,1,0:T(8,128)S(1)}, u32[]{:S(2)}, u32[]{:S(2)}) collective-permute-start(f32[2,32,512]{2,1,0:T(8,128)S(1)} %get-tuple-element.41), channel_id=1, source_target_pairs={{0,24},{4,28},{8,16},{12,20},{16,8},{20,12},{24,0},{28,4},{1,25},{... | collective-permute-start | bytes 393224 | tf_op jit(solution)/shard_map/ppermute | solution.py:19
  131.9 25.5 %collective-permute-start.11 = (f32[2,32,512]{2,1,0:T(8,128)S(1)}, f32[2,32,512]{2,1,0:T(8,128)S(1)}, u32[]{:S(2)}, u32[]{:S(2)}) collective-permute-start(f32[2,32,512]{2,1,0:T(8,128)S(1)} %get-tuple-element.42), channel_id=1, source_target_pairs={{0,16},{4,20},{8,24},{12,28},{16,0},{20,4},{24,8},{28,12},{1,17},{... | collective-permute-start | bytes 393224 | tf_op jit(solution)/shard_map/ppermute | solution.py:19
  136.8 20.7 %collective-permute-start.10 = (f32[2,32,512]{2,1,0:T(8,128)S(1)}, f32[2,32,512]{2,1,0:T(8,128)S(1)}, u32[]{:S(2)}, u32[]{:S(2)}) collective-permute-start(f32[2,32,512]{2,1,0:T(8,128)S(1)} %get-tuple-element.40), channel_id=1, source_target_pairs={{0,8},{4,12},{8,0},{12,4},{16,24},{20,28},{24,16},{28,20},{1,9},{5... | collective-permute-start | bytes 393224 | tf_op jit(solution)/shard_map/ppermute | solution.py:19
  157.5 11.9 %collective-permute-start.13 = (f32[32,512]{1,0:T(8,128)S(1)}, f32[32,512]{1,0:T(8,128)S(1)}, u32[]{:S(2)}, u32[]{:S(2)}) collective-permute-start(f32[32,512]{1,0:T(8,128)S(1)} %slice_bitcast_fusion.8), channel_id=1, source_target_pairs={{0,32},{32,0},{1,33},{33,1},{2,34},{34,2},{3,35},{35,3},{4,36},{36... | collective-permute-start | bytes 196616 | tf_op jit(solution)/shard_map/ppermute | solution.py:19
  163.1 18.7 %all-to-all-start.2 = ((f32[16,8,256]{2,1,0:T(8,128)}), f32[16,8,256]{2,1,0:T(8,128)S(1)}, u32[]{:S(2)}, u32[]{:S(2)}) async-start(f32[16,8,256]{2,1,0:T(8,128)} %pad_maximum_fusion.7), calls=%async_computation.2 | async-start | bytes 262144 | tf_op jit(solution)/shard_map/all_to_all | solution.py:140
  182.5 12.2 %all-to-all-start.3 = ((f32[8,8,256]{2,1,0:T(8,128)}), f32[8,8,256]{2,1,0:T(8,128)S(1)}, u32[]{:S(2)}, u32[]{:S(2)}) async-start(f32[8,8,256]{2,1,0:T(8,128)} %broadcast_in_dim.21), calls=%async_computation.3 | async-start | bytes 131072 | tf_op jit(solution)/shard_map/all_to_all | solution.py:24
